TPU v7x, 32 devices: a whole 2x2x4 slice. The times are simulated.
32 devices in a mesh: dp: 2 (over x), sp: 16 (over z, y, core).
Axes of the slice: x: 2, y: 2, z: 4, core: 2. Of those that a mesh axis runs over, the one named last changes fastest.
Arguments:
- x_in: bfloat16 [4, 2048, 2048], P('dp', 'sp'), parts along dimension 0
- grad_y: bfloat16 [4, 2048, 2048], P('dp', 'sp'), parts along dimension 0
- positions: int32 [4, 2048], P('dp', 'sp'), parts along dimension 0
- g_norm: bfloat16 [2048], replicated
- w_query: bfloat16 [2048, 2048], replicated
- w_key: bfloat16 [2048, 2048], replicated
- w_value: bfloat16 [2048, 2048], replicated
- w_out: bfloat16 [2048, 2048], replicated
- g_query: bfloat16 [2048], replicated
- g_key: bfloat16 [2048], replicated
Outputs:
- output 1: bfloat16 [4, 2048, 2048], P('dp', 'sp'), parts along dimension 0
- output 2: bfloat16 [4, 2048, 2048], P('dp', 'sp'), parts along dimension 0
- output 3: float32 [4096], P(('dp', 'sp')), parts along dimension 0
- output 4: float32 [4096, 2048], P(('dp', 'sp')), parts along dimension 0
- output 5: float32 [4096, 2048], P(('dp', 'sp')), parts along dimension 0
- output 6: float32 [4096, 2048], P(('dp', 'sp')), parts along dimension 0
- output 7: float32 [4096, 2048], P(('dp', 'sp')), parts along dimension 0
- output 8: float32 [4096], P(('dp', 'sp')), parts along dimension 0
- output 9: float32 [4096], P(('dp', 'sp')), parts along dimension 0
There are 2 independent parts. A program takes and returns all parts, laid end to end along the dimension named above; an argument that names none is the same for every part.
All inputs are finite; a program needn't handle non-finite values.
Results may differ from a plain program's by a relative error of at most 0.01132.
Values are sent between devices in bfloat16 or wider.
A program may use at most 1 GiB of HBM per device.

v0:
```python
import functools
import jax
import jax.numpy as jnp
from jax import lax
from jax.sharding import PartitionSpec as P

HEAD_DIM = 128
QUERY_BLOCK = 128
NORM_EPS = 1e-5
ROPE_BASE = 10000.0
NEG_BIG = -1e30


def rope_tables(positions):
    half_dim = HEAD_DIM // 2
    inv_freq = ROPE_BASE ** (-jnp.arange(half_dim, dtype=jnp.float32) * (2.0 / HEAD_DIM))
    angles = positions.astype(jnp.float32)[..., None] * inv_freq
    return jnp.cos(angles)[:, :, None, :], jnp.sin(angles)[:, :, None, :]


def rope_apply(values, cos_t, sin_t):
    half_dim = values.shape[-1] // 2
    first_half = values[..., :half_dim]
    second_half = values[..., half_dim:]
    return jnp.concatenate([first_half * cos_t - second_half * sin_t, second_half * cos_t + first_half * sin_t], axis=-1)


def rope_revert(grads_in, cos_t, sin_t):
    half_dim = grads_in.shape[-1] // 2
    first_half = grads_in[..., :half_dim]
    second_half = grads_in[..., half_dim:]
    return jnp.concatenate([first_half * cos_t + second_half * sin_t, second_half * cos_t - first_half * sin_t], axis=-1)


def rms_forward(values, gain_vec):
    inv_rms = lax.rsqrt(jnp.mean(values * values, axis=-1, keepdims=True) + NORM_EPS)
    normed = values * inv_rms
    return normed * gain_vec.astype(jnp.float32), normed, inv_rms


def rms_backward(d_out, normed, inv_rms, gain_vec):
    d_normed = d_out * gain_vec.astype(jnp.float32)
    d_in = inv_rms * (d_normed - normed * jnp.mean(d_normed * normed, axis=-1, keepdims=True))
    return d_in, d_out * normed


def project(values, weight):
    return jnp.einsum('bsd,de->bse', values, weight, preferred_element_type=jnp.float32)


def project_back(grads_in, weight):
    return jnp.einsum('bse,de->bsd', grads_in, weight, preferred_element_type=jnp.float32)


def weight_grad(values, grads_in):
    return jnp.einsum('bsd,bse->de', values, grads_in, preferred_element_type=jnp.float32)


def block_front(x_in, positions, g_norm, w_query, w_key, w_value, g_query, g_key):
    n_batch, seq_len, d_model = x_in.shape
    head_shape = (n_batch, seq_len, d_model // HEAD_DIM, HEAD_DIM)
    cos_t, sin_t = rope_tables(positions)
    x_f = x_in.astype(jnp.float32)
    hid_f, x_hat, x_inv = rms_forward(x_f, g_norm)
    hidden = hid_f.astype(jnp.bfloat16)
    q_nrm, q_hat, q_inv = rms_forward(project(hidden, w_query), g_query)
    k_nrm, k_hat, k_inv = rms_forward(project(hidden, w_key), g_key)
    q_rot = rope_apply(q_nrm.reshape(head_shape), cos_t, sin_t).astype(jnp.bfloat16)
    k_rot = rope_apply(k_nrm.reshape(head_shape), cos_t, sin_t).astype(jnp.bfloat16)
    v_val = project(hidden, w_value).astype(jnp.bfloat16).reshape(head_shape)
    saved_fwd = (x_f, x_hat, x_inv, hidden, q_hat, q_inv, k_hat, k_inv, cos_t, sin_t)
    return q_rot, k_rot, v_val, saved_fwd


def block_back(saved_fwd, d_q, d_k, d_v, grad_y, g_norm, w_query, w_key, w_value, g_query, g_key):
    x_f, x_hat, x_inv, hidden, q_hat, q_inv, k_hat, k_inv, cos_t, sin_t = saved_fwd
    flat_shape = hidden.shape
    dq_rot = rope_revert(d_q.astype(jnp.float32), cos_t, sin_t).reshape(flat_shape)
    dk_rot = rope_revert(d_k.astype(jnp.float32), cos_t, sin_t).reshape(flat_shape)
    dq_raw, q_terms = rms_backward(dq_rot, q_hat, q_inv, g_query)
    dk_raw, k_terms = rms_backward(dk_rot, k_hat, k_inv, g_key)
    dq_bf = dq_raw.astype(jnp.bfloat16)
    dk_bf = dk_raw.astype(jnp.bfloat16)
    dv_bf = d_v.reshape(flat_shape)
    d_hidden = project_back(dq_bf, w_query) + project_back(dk_bf, w_key) + project_back(dv_bf, w_value)
    dx_norm, n_terms = rms_backward(d_hidden, x_hat, x_inv, g_norm)
    grad_x = (grad_y.astype(jnp.float32) + dx_norm).astype(jnp.bfloat16)
    return grad_x, (dq_bf, dk_bf, dv_bf), (n_terms, q_terms, k_terms)


def attend_forward(q_all, k_all, v_all, q_offset):
    q_len = q_all.shape[1]
    key_pos = jnp.arange(k_all.shape[1])
    blk_len = min(QUERY_BLOCK, q_len)
    qk_scale = q_all.shape[-1] ** -0.5

    def block_step(blk_idx, loop_state):
        out_buf, lse_buf = loop_state
        q_start = blk_idx * blk_len
        q_blk = lax.dynamic_slice_in_dim(q_all, q_start, blk_len, axis=1)
        scores = jnp.einsum('bqhd,bkhd->bhqk', q_blk, k_all, preferred_element_type=jnp.float32) * qk_scale
        q_pos = q_offset + q_start + jnp.arange(blk_len)
        scores = jnp.where(q_pos[:, None] >= key_pos[None, :], scores, NEG_BIG)
        row_max = jnp.max(scores, axis=-1, keepdims=True)
        exp_scores = jnp.exp(scores - row_max)
        row_sum = jnp.sum(exp_scores, axis=-1, keepdims=True)
        prob_bf = (exp_scores / row_sum).astype(jnp.bfloat16)
        out_blk = jnp.einsum('bhqk,bkhd->bqhd', prob_bf, v_all, preferred_element_type=jnp.float32)
        lse_blk = (row_max + jnp.log(row_sum))[..., 0]
        out_buf = lax.dynamic_update_slice_in_dim(out_buf, out_blk.astype(jnp.bfloat16), q_start, axis=1)
        lse_buf = lax.dynamic_update_slice_in_dim(lse_buf, lse_blk, q_start, axis=2)
        return out_buf, lse_buf

    init_state = (jnp.zeros(q_all.shape, jnp.bfloat16), jnp.zeros((q_all.shape[0], q_all.shape[2], q_len), jnp.float32))
    return lax.fori_loop(0, q_len // blk_len, block_step, init_state)


def attend_backward(q_all, k_all, v_all, lse_all, dout_all, q_offset):
    q_len = q_all.shape[1]
    key_pos = jnp.arange(k_all.shape[1])
    blk_len = min(QUERY_BLOCK, q_len)
    qk_scale = q_all.shape[-1] ** -0.5

    def block_step(blk_idx, loop_state):
        dq_buf, dk_acc, dv_acc = loop_state
        q_start = blk_idx * blk_len
        q_blk = lax.dynamic_slice_in_dim(q_all, q_start, blk_len, axis=1)
        do_blk = lax.dynamic_slice_in_dim(dout_all, q_start, blk_len, axis=1)
        lse_blk = lax.dynamic_slice_in_dim(lse_all, q_start, blk_len, axis=2)
        scores = jnp.einsum('bqhd,bkhd->bhqk', q_blk, k_all, preferred_element_type=jnp.float32) * qk_scale
        q_pos = q_offset + q_start + jnp.arange(blk_len)
        scores = jnp.where(q_pos[:, None] >= key_pos[None, :], scores, NEG_BIG)
        prob_f = jnp.exp(scores - lse_blk[..., None])
        d_prob = jnp.einsum('bqhd,bkhd->bhqk', do_blk, v_all, preferred_element_type=jnp.float32)
        row_dot = jnp.sum(prob_f * d_prob, axis=-1, keepdims=True)
        ds_bf = (prob_f * (d_prob - row_dot) * qk_scale).astype(jnp.bfloat16)
        prob_bf = prob_f.astype(jnp.bfloat16)
        dv_acc = dv_acc + jnp.einsum('bhqk,bqhd->bkhd', prob_bf, do_blk, preferred_element_type=jnp.float32)
        dk_acc = dk_acc + jnp.einsum('bhqk,bqhd->bkhd', ds_bf, q_blk, preferred_element_type=jnp.float32)
        dq_blk = jnp.einsum('bhqk,bkhd->bqhd', ds_bf, k_all, preferred_element_type=jnp.float32)
        dq_buf = lax.dynamic_update_slice_in_dim(dq_buf, dq_blk.astype(jnp.bfloat16), q_start, axis=1)
        return dq_buf, dk_acc, dv_acc

    init_state = (jnp.zeros(q_all.shape, jnp.bfloat16), jnp.zeros(k_all.shape, jnp.float32), jnp.zeros(v_all.shape, jnp.float32))
    return lax.fori_loop(0, q_len // blk_len, block_step, init_state)


def solution(mesh):
    to_heads = functools.partial(lax.all_to_all, axis_name='sp', split_axis=2, concat_axis=1, tiled=True)
    to_tokens = functools.partial(lax.all_to_all, axis_name='sp', split_axis=1, concat_axis=2, tiled=True)

    def sum_rows(partial_sum):
        return lax.psum_scatter(partial_sum, 'sp', scatter_dimension=0, tiled=True)

    def device_step(x_loc, grad_y, positions, g_norm, w_query, w_key, w_value, w_out, g_query, g_key):
        n_batch, loc_len, d_model = x_loc.shape
        q_loc, k_loc, v_loc, saved_fwd = block_front(x_loc, positions, g_norm, w_query, w_key, w_value, g_query, g_key)
        q_all = to_heads(q_loc)
        k_all = to_heads(k_loc)
        v_all = to_heads(v_loc)
        out_all, lse_all = attend_forward(q_all, k_all, v_all, 0)
        attended = to_tokens(out_all).reshape(n_batch, loc_len, d_model)
        y_out = (saved_fwd[0] + project(attended, w_out)).astype(jnp.bfloat16)
        grad_w_out = weight_grad(attended, grad_y)
        d_attn = project_back(grad_y, w_out).astype(jnp.bfloat16).reshape(q_loc.shape)
        dq_all, dk_acc, dv_acc = attend_backward(q_all, k_all, v_all, lse_all, to_heads(d_attn), 0)
        d_q = to_tokens(dq_all)
        d_k = to_tokens(dk_acc.astype(jnp.bfloat16))
        d_v = to_tokens(dv_acc.astype(jnp.bfloat16))
        grad_x, proj_grads, gain_terms = block_back(saved_fwd, d_q, d_k, d_v, grad_y, g_norm, w_query, w_key, w_value, g_query, g_key)
        hidden = saved_fwd[3]
        return (y_out, grad_x, sum_rows(jnp.sum(gain_terms[0], axis=(0, 1))), sum_rows(weight_grad(hidden, proj_grads[0])), sum_rows(weight_grad(hidden, proj_grads[1])), sum_rows(weight_grad(hidden, proj_grads[2])), sum_rows(grad_w_out), sum_rows(jnp.sum(gain_terms[1], axis=(0, 1))), sum_rows(jnp.sum(gain_terms[2], axis=(0, 1))))

    seq_spec = P('dp', 'sp', None)
    mat_rep = P(None, None)
    vec_rep = P(None)
    row_spec = P(('dp', 'sp'), None)
    vec_spec = P(('dp', 'sp'))
    return jax.shard_map(device_step, mesh=mesh, in_specs=(seq_spec, seq_spec, P('dp', 'sp'), vec_rep, mat_rep, mat_rep, mat_rep, mat_rep, vec_rep, vec_rep), out_specs=(seq_spec, seq_spec, vec_spec, row_spec, row_spec, row_spec, row_spec, vec_spec, vec_spec), check_vma=False)
```

profile of v0, /device:TPU:0, one launch (start us, length us, event | category | flops | bytes accessed | tf_op | source)
XLA Modules:
  0.0 1349.4 jit_solution(4513457329816623947)
XLA Ops:
  10.3 6.3 multiply_reduce_fusion.3
  30.2 7.7 all-to-all-start
  39.5 20.7 %all-to-all-done = bf16[2,128,16,128]{3,1,0,2:T(8,128)(2,1)} async-done(((bf16[2,128,16,128]{3,1,0,2:T(8,128)(2,1)}), bf16[2,128,16,128]{3,1,0,2:T(8,128)(2,1)}, u32[]{:S(2)}, u32[]{:S(2)}) %all-to-all-start) | async-done | bytes 1048608 | tf_op jit(solution)/shard_map/all_to_all | solution.py:158
  60.2 7.1 all-to-all-start.1
  67.3 5.8 fusion.107
  74.4 15.4 %all-to-all-done.1 = bf16[2,128,16,128]{3,1,0,2:T(8,128)(2,1)S(1)} async-done(((bf16[2,128,16,128]{3,1,0,2:T(8,128)(2,1)}), bf16[2,128,16,128]{3,1,0,2:T(8,128)(2,1)S(1)}, u32[]{:S(2)}, u32[]{:S(2)}) %all-to-all-start.1) | async-done | bytes 1048608 | tf_op jit(solution)/shard_map/all_to_all | solution.py:159
  89.8 7.1 all-to-all-start.2
  97.0 5.7 fusion.104
  107.3 12.0 all-to-all-done.2
  119.3 7.1 all-to-all-start.4
  129.1 62.5 %while.34 = (s32[]{:T(128)}, bf16[2,2048,1,128]{3,0,2,1:T(2,128)(2,1)}, f32[2,1,2048]{2,0,1:T(2,128)S(1)}, bf16[2,2048,1,128]{3,1,0,2:T(8,128)(2,1)}, bf16[2,204...) while((s32[]{:T(128)}, ...), condition=%wide.region_6.7_spmd.clone, body=%wide.region_3.6_spmd.clone.sunk | while | flops 272924544 | bytes 9184427 | solution.py:115
  195.3 318.8 %while.35 = (s32[]{:T(128)}, bf16[2,2048,1,128]{3,0,2,1:T(2,128)(2,1)}, f32[2,2048,1,128]{1,3,0,2:T(8,128)S(1)}, f32[2,2048,1,128]{1,3,0,2:T(8,128)}, bf16[2,204...) while((s32[]{:T(128)}, ...), condition=%wide.region_9.10_spmd.clone, body=%wide.region_7.9_spmd.clone.sunk | while | flops 680825472 | bytes 31396056 | solution.py:145
  201.5 4.5 fusion.164
  206.7 4.5 fusion.165
  220.8 4.5 fusion.164
  226.0 4.5 fusion.165
  240.7 4.5 fusion.164
  246.0 4.5 fusion.165
  250.4 4.1 fusion.166
  260.7 4.5 fusion.164
  265.9 4.5 fusion.165
  270.4 4.1 fusion.166
  280.7 4.5 fusion.164
  285.9 4.5 fusion.165
  300.6 4.5 fusion.164
  305.8 4.5 fusion.165
  320.6 4.5 fusion.164
  325.8 4.5 fusion.165
  340.5 4.5 fusion.164
  345.8 4.5 fusion.165
  360.5 4.5 fusion.164
  365.7 4.5 fusion.165
  380.5 4.5 fusion.164
  385.7 4.5 fusion.165
  400.5 4.5 fusion.164
  405.7 4.5 fusion.165
  420.4 4.5 fusion.164
  425.6 4.5 fusion.165
  440.4 4.5 fusion.164
  445.6 4.5 fusion.165
  460.4 4.5 fusion.164
  465.6 4.5 fusion.165
  480.3 4.5 fusion.164
  485.6 4.5 fusion.165
  500.3 4.5 fusion.164
  505.5 4.5 fusion.165
  514.1 6.0 all-to-all-start.5
  522.3 20.2 %all-to-all-done.5 = bf16[2,2048,1,128]{3,0,2,1:T(2,128)(2,1)S(1)} async-done(((bf16[2,2048,1,128]{3,0,2,1:T(2,128)(2,1)}), bf16[2,2048,1,128]{3,0,2,1:T(2,128)(2,1)S(1)}, u32[]{:S(2)}, u32[]{:S(2)}) %all-to-all-start.5) | async-done | bytes 1048608 | tf_op jit(solution)/shard_map/all_to_all | solution.py:167
  542.5 7.1 all-to-all-start.6
  550.1 22.0 %all-to-all-done.6 = bf16[2,2048,1,128]{3,0,2,1:T(2,128)(2,1)} async-done(((bf16[2,2048,1,128]{3,0,2,1:T(2,128)(2,1)}), bf16[2,2048,1,128]{3,0,2,1:T(2,128)(2,1)}, u32[]{:S(2)}, u32[]{:S(2)}) %all-to-all-start.6) | async-done | bytes 1048608 | tf_op jit(solution)/shard_map/all_to_all | solution.py:168
  579.9 8.2 convolution_bitcast_fusion.5
  595.1 8.2 convolution_bitcast_fusion.4
  607.2 43.4 %all_to_all.120 = bf16[2,2048,1,128]{3,0,2,1:T(2,128)(2,1)S(1)} all-to-all(bf16[2,2048,1,128]{3,0,2,1:T(2,128)(2,1)} %copy.75), channel_id=1, replica_groups=mesh['dp'=2,'sp'=16] {'sp'}, dimensions={1} | all-to-all | bytes 2097152 | tf_op jit(solution)/shard_map/all_to_all | solution.py:169
  651.7 8.2 convolution_bitcast_fusion.3
  661.2 57.0 %all_to_all.121 = bf16[2,2048,1,128]{3,0,2,1:T(2,128)(2,1)S(1)} all-to-all(bf16[2,2048,1,128]{3,0,2,1:T(2,128)(2,1)S(1)} %copy-done.21), channel_id=1, replica_groups=mesh['dp'=2,'sp'=16] {'sp'}, dimensions={1} | all-to-all | bytes 2097152 | tf_op jit(solution)/shard_map/all_to_all | solution.py:162
  721.4 8.1 convolution_bitcast_fusion.2
  731.5 5.9 fusion.61
  737.4 5.9 fusion.65
  743.3 4.4 fusion.100
  747.8 66.2 %all-reduce.3 = (f32[2048]{0:T(1024)S(1)}, f32[2048]{0:T(1024)S(1)}, f32[2048]{0:T(1024)S(1)}) all-reduce(f32[2048]{0:T(1024)S(1)} %get-tuple-element.360, f32[2048]{0:T(1024)S(1)} %get-tuple-element.358, f32[2048]{0:T(1024)S(1)} %get-tuple-element.356), channel_id=2, replica_groups=mesh['dp'=2,'sp'=16] {'sp'}, use_global_device_ids=true, to_apply=%region_14.15.clone | all-reduce | flops 6144 | bytes 49152
  819.0 6.7 fusion.85
  825.7 157.3 %reduce-scatter.7.cloned.1.call-done = f32[128,2048]{1,0:T(8,128)} async-done(((f32[2048,2048]{1,0:T(8,128)}), f32[128,2048]{1,0:T(8,128)}) %reduce-scatter.7.cloned.1.call-update) | async-done | bytes 1048592 | tf_op jit(solution)/shard_map/reduce_scatter | solution.py:153
  983.0 179.9 %reduce-scatter.9.cloned.1.call-done = f32[128,2048]{1,0:T(8,128)} async-done(((f32[2048,2048]{1,0:T(8,128)}), f32[128,2048]{1,0:T(8,128)}) %reduce-scatter.9.cloned.1.call-update) | async-done | bytes 1048592 | tf_op jit(solution)/shard_map/reduce_scatter | solution.py:153
  1162.9 179.7 %reduce-scatter.11.cloned.1.call-done = f32[128,2048]{1,0:T(8,128)} async-done(((f32[2048,2048]{1,0:T(8,128)}), f32[128,2048]{1,0:T(8,128)}) %reduce-scatter.11.cloned.1.call-update) | async-done | bytes 1048592 | tf_op jit(solution)/shard_map/reduce_scatter | solution.py:153
  (347 shorter events, 292.0 us)
Async XLA Ops:
  7.9 10.4 slice-start
  10.2 8.1 slice-start.1
  16.6 1.3 copy-start.3
  17.9 1.2 copy-start.1
  19.1 2.5 copy-start.22
  21.7 1.3 copy-start.5
  23.0 0.7 copy-start.23
  30.2 30.1 %all-to-all-start = ((bf16[2,128,16,128]{3,1,0,2:T(8,128)(2,1)}), bf16[2,128,16,128]{3,1,0,2:T(8,128)(2,1)}, u32[]{:S(2)}, u32[]{:S(2)}) async-start(bf16[2,128,16,128]{3,1,0,2:T(8,128)(2,1)} %copy.57), calls=%async_computation | async-start | bytes 2097152 | tf_op jit(solution)/shard_map/all_to_all | solution.py:158
  60.2 29.5 %all-to-all-start.1 = ((bf16[2,128,16,128]{3,1,0,2:T(8,128)(2,1)}), bf16[2,128,16,128]{3,1,0,2:T(8,128)(2,1)S(1)}, u32[]{:S(2)}, u32[]{:S(2)}) async-start(bf16[2,128,16,128]{3,1,0,2:T(8,128)(2,1)} %copy.61), calls=%async_computation.1 | async-start | bytes 2097152 | tf_op jit(solution)/shard_map/all_to_all | solution.py:159
  73.1 23.8 %copy-start.9 = (bf16[2,128,2048]{2,1,0:T(8,128)(2,1)S(1)}, bf16[2,128,2048]{2,1,0:T(8,128)(2,1)}, u32[]{:S(2)}) copy-start(bf16[2,128,2048]{2,1,0:T(8,128)(2,1)} %param.15) | copy-start | bytes 3145732
  89.8 7.1 copy-start.19
  89.8 29.5 %all-to-all-start.2 = ((bf16[2,128,16,128]{3,1,0,2:T(8,128)(2,1)}), bf16[2,128,16,128]{3,1,0,2:T(8,128)(2,1)}, u32[]{:S(2)}, u32[]{:S(2)}) async-start(bf16[2,128,16,128]{3,1,0,2:T(8,128)(2,1)} %bitcast.209), calls=%async_computation.2 | async-start | bytes 2097152 | tf_op jit(solution)/shard_map/all_to_all | solution.py:160
  102.7 3.6 copy-start.20
  119.3 72.3 %all-to-all-start.4 = ((bf16[2,128,16,128]{3,1,0,2:T(8,128)(2,1)}), bf16[2,128,16,128]{3,1,0,2:T(8,128)(2,1)}, u32[]{:S(2)}, u32[]{:S(2)}) async-start(bf16[2,128,16,128]{3,1,0,2:T(8,128)(2,1)} %bitcast.208), calls=%async_computation.4 | async-start | bytes 2097152 | tf_op jit(solution)/shard_map/all_to_all | solution.py:166
  514.1 28.4 %all-to-all-start.5 = ((bf16[2,2048,1,128]{3,0,2,1:T(2,128)(2,1)}), bf16[2,2048,1,128]{3,0,2,1:T(2,128)(2,1)S(1)}, u32[]{:S(2)}, u32[]{:S(2)}) async-start(bf16[2,2048,1,128]{3,0,2,1:T(2,128)(2,1)} %get-tuple-element.307), calls=%async_computation.5 | async-start | bytes 2097152 | tf_op jit(solution)/shard_map/all_to_all | solution.py:167
  542.5 29.5 %all-to-all-start.6 = ((bf16[2,2048,1,128]{3,0,2,1:T(2,128)(2,1)}), bf16[2,2048,1,128]{3,0,2,1:T(2,128)(2,1)}, u32[]{:S(2)}, u32[]{:S(2)}) async-start(bf16[2,2048,1,128]{3,0,2,1:T(2,128)(2,1)} %copy.72), calls=%async_computation.6 | async-start | bytes 2097152 | tf_op jit(solution)/shard_map/all_to_all | solution.py:168
  549.6 276.1 %reduce-scatter.5.cloned.1.call-start = ((), (), s32[]{:S(2)}) async-start(), calls=%async_computation.12 | async-start | bytes 17825792 | tf_op jit(solution)/shard_map/reduce_scatter | solution.py:153
  573.6 3.2 copy-start.6
  577.8 2.0 copy-start.2
  578.9 1.0 copy-start.11
  588.1 1.6 copy-start.4
  588.1 394.9 %reduce-scatter.7.cloned.1.call-start = ((), (), s32[]{:S(2)}) async-start(), calls=%async_computation.13 | async-start | bytes 17825792 | tf_op jit(solution)/shard_map/reduce_scatter | solution.py:153
  589.7 3.3 copy-start.7
  589.7 3.5 copy-start.8
  594.1 1.0 copy-start.13
  603.3 1.6 copy-start
  603.4 559.5 %reduce-scatter.9.cloned.1.call-start = ((), (), s32[]{:S(2)}) async-start(), calls=%async_computation.14 | async-start | bytes 17825792 | tf_op jit(solution)/shard_map/reduce_scatter | solution.py:153
  651.7 8.2 copy-start.17
  659.9 1.2 copy-start.21
  660.0 682.6 %reduce-scatter.11.cloned.1.call-start = ((), (), s32[]{:S(2)}) async-start(), calls=%async_computation.15 | async-start | bytes 17825792 | tf_op jit(solution)/shard_map/reduce_scatter | solution.py:153
  718.2 3.2 copy-start.10
  721.4 8.1 copy-start.15
  729.5 0.7 copy-start.24
  729.5 1.9 copy-start.18
  731.4 5.9 copy-start.14
  731.4 11.9 slice-start.2
  737.4 5.9 copy-start.12
  737.4 5.9 slice-start.3
  815.7 3.3 copy-start.16
Sparse Core Ops, SparseCore 0:
  588.3 214.9 reduce-scatter.4
  807.9 175.0 reduce-scatter.6
  987.7 175.1 reduce-scatter.8
  1167.4 175.1 reduce-scatter.10
where the time goes:
time: 1360 us; the launch traced here: 1350 us
  waiting for transfers between devices  607 us (45%)
  matrix products  420 us (31%)
  blocking collectives  167 us (12%)
  local copies, waits for them, and re-layouts  62 us (5%)
  starting transfers between devices  42.3 us (3%)
  other arithmetic  35.5 us (3%)
  between operations  15.2 us (1%)
    reduce_scatter x4, waiting for transfers between devices, sum_rows(): return lax.psum_scatter(partial_sum, 'sp', scatter_dimension=0, tiled=True)  517 us
    dot_general x32, matrix products, block_step(): jnp.einsum('bqhd,bkhd->bhqk', q_blk, k_all, preferred_element_type=jnp.fl...  83.6 us
    dot_general x16, matrix products, block_step(): jnp.einsum('bhqk,bkhd->bqhd', ds_bf, k_all, preferred_element_type=jnp.fl...  72.1 us
    dot_general x16, matrix products, block_step(): jnp.einsum('bhqk,bqhd->bkhd', ds_bf, q_blk, preferred_element_type=jnp.fl...  71.9 us
    unnamed x1, blocking collectives  66.2 us
    dot_general x16, matrix products, block_step(): jnp.einsum('bhqk,bqhd->bkhd', prob_bf, do_blk, preferred_element_type=jnp...  64.5 us
    all_to_all x1, blocking collectives, device_step(): attended = to_tokens(out_all).reshape(n_batch, loc_len, d_model)  57 us
    all_to_all x1, blocking collectives, device_step(): d_v = to_tokens(dv_acc.astype(jnp.bfloat16))  43.4 us
  transfers between devices with their start and end apart: 10, of which 8 were waited for; matrix products, arithmetic and copies ran while one was open for 11% of the time, Pallas kernels for 0%

commit v1 on v0

v1 whole, which is shorter than its diff:
```python
import functools
import jax
import jax.numpy as jnp
from jax import lax
from jax.experimental import pallas as pl
from jax.experimental.pallas import tpu as pltpu
from jax.sharding import PartitionSpec as P

HEAD_DIM = 128
NORM_EPS = 1e-5
ROPE_BASE = 10000.0
NEG_BIG = -1e30
LOG2E = 1.4426950408889634
FWD_BLOCK = 1024
BWD_BLOCK = 512
F32, BF = jnp.float32, jnp.bfloat16
NT = (((1,), (1,)), ((), ()))


def rope_tables(positions):
    half = HEAD_DIM // 2
    inv_freq = ROPE_BASE ** (-jnp.arange(half, dtype=F32) * (2.0 / HEAD_DIM))
    angles = positions.astype(F32)[:, None] * inv_freq
    cos_t, sin_t = jnp.cos(angles), jnp.sin(angles)
    return jnp.concatenate([cos_t, cos_t], 1), jnp.concatenate([-sin_t, sin_t], 1)


def column(row):
    return jnp.broadcast_to(row, (HEAD_DIM, row.shape[1])).T


def as_row(col):
    return jnp.broadcast_to(col, (col.shape[0], HEAD_DIM)).T[0:1, :]


def half_roll(u):
    return pltpu.roll(u, HEAD_DIM // 2, 1)


def proj_kernel(h_ref, w_ref, st_ref, c_ref, s_ref, g_ref, q_ref, k_ref, v_ref, qh_ref, kh_ref):
    h = h_ref[0]
    cols = q_ref.shape[1]
    for idx, (out, hat_out) in enumerate(((q_ref, qh_ref), (k_ref, kh_ref))):
        raw = mm32(h, w_ref[:, idx * cols:(idx + 1) * cols])
        inv = column(st_ref[0, idx:idx + 1, :])
        for lo in range(0, cols, HEAD_DIM):
            hs = slice(lo, lo + HEAD_DIM)
            hat = raw[:, hs] * inv
            hat_out[:, hs] = hat
            u = hat * g_ref[idx:idx + 1, hs]
            out[:, hs] = (u * c_ref[...] + half_roll(u) * s_ref[...]).astype(BF)
    v_ref[...] = mm32(h, w_ref[:, 2 * cols:]).astype(BF)


def tok_kernel(dq_ref, dk_ref, qr_ref, kr_ref, st_ref, c_ref, s_ref, g_ref, qo_ref, ko_ref, row_ref, nrm_ref):
    n_chip, rows, cols = dq_ref.shape
    dim = n_chip * cols
    for idx, (d_ref, raw_ref, out) in enumerate(((dq_ref, qr_ref, qo_ref), (dk_ref, kr_ref, ko_ref))):
        inv = column(st_ref[idx:idx + 1, :])
        acc = jnp.zeros((rows, HEAD_DIM), F32)
        for lo in range(0, dim, HEAD_DIM):
            hs = slice(lo, lo + HEAD_DIM)
            d = d_ref[lo // cols, :, lo % cols:lo % cols + HEAD_DIM].astype(F32)
            nrm = (d * c_ref[...] - half_roll(d) * s_ref[...]) * g_ref[idx:idx + 1, hs]
            nrm_ref[:, hs] = nrm
            acc += nrm * (raw_ref[:, hs] * inv)
        row = jnp.sum(acc, axis=1, keepdims=True) / dim
        row_ref[idx:idx + 1, :] = as_row(row)
        for lo in range(0, dim, HEAD_DIM):
            hs = slice(lo, lo + HEAD_DIM)
            out[:, hs] = (inv * (nrm_ref[:, hs] - raw_ref[:, hs] * inv * row)).astype(BF)


def dw_qk_kernel(d_ref, hat_ref, st_ref, row_ref, c_ref, s_ref, g_ref, h_ref, out_ref, dg_ref, dt_ref, *, idx):
    n_chip, rows = st_ref.shape[0], st_ref.shape[2]
    cols = d_ref.shape[1]

    @pl.when(pl.program_id(0) == 0)
    def _():
        dg_ref[...] = jnp.zeros_like(dg_ref)
        for p in range(n_chip):
            ts = slice(p * rows, (p + 1) * rows)
            inv = column(st_ref[p, idx:idx + 1, :])
            row = column(row_ref[p, idx:idx + 1, :])
            for lo in range(0, cols, HEAD_DIM):
                hs = slice(lo, lo + HEAD_DIM)
                d = d_ref[ts, hs].astype(F32)
                rot = d * c_ref[ts, :] - half_roll(d) * s_ref[ts, :]
                hat = hat_ref[ts, hs]
                raw = inv * (rot * g_ref[idx:idx + 1, hs] - hat * row)
                dt_ref[hs, ts] = raw.astype(BF).T
                dg_ref[0:1, hs] += jnp.sum(rot * hat, axis=0, keepdims=True)

    dw_block(dt_ref, h_ref, out_ref)


def dw_v_kernel(d_ref, h_ref, out_ref, dt_ref):
    @pl.when(pl.program_id(0) == 0)
    def _():
        dt_ref[...] = d_ref[...].T

    dw_block(dt_ref, h_ref, out_ref)


def dw_block(dt_ref, h_ref, out_ref):
    dw = mm32(dt_ref[...], h_ref[...]).T
    half = out_ref.shape[2]
    out_ref[0, 0] = dw[:half]
    out_ref[0, 1] = dw[half:]


def attn_fwd_kernel(q_ref,k_ref,v_ref,o_ref,ot_ref,lse_ref,vt_ref,*,blk,heads):
    n=q_ref.shape[0]; nb=n//blk
    c=HEAD_DIM**-0.5*LOG2E
    for h in range(heads):
        vt_ref[h*HEAD_DIM:(h+1)*HEAD_DIM,:]=v_ref[:,h*HEAD_DIM:(h+1)*HEAD_DIM].T
    causal=(lax.broadcasted_iota(jnp.int32,(blk,blk),0)<=lax.broadcasted_iota(jnp.int32,(blk,blk),1))
    def qstep(j,_):
        qs=pl.ds(pl.multiple_of(j*blk,blk),blk)
        qb=[q_ref[qs,h*HEAD_DIM:(h+1)*HEAD_DIM] for h in range(heads)]
        def tile(i,carry,diag):
            ks=pl.ds(pl.multiple_of(i*blk,blk),blk)
            out=[]
            for h in range(heads):
                m,l,acc=carry[h]
                s=mm32_nt(k_ref[ks,h*HEAD_DIM:(h+1)*HEAD_DIM],qb[h])
                if diag: s=jnp.where(causal,s,NEG_BIG)
                mn=jnp.maximum(m,jnp.max(s,axis=0,keepdims=True))
                al=jnp.exp2((m-mn)*c)
                p=jnp.exp2((s-mn)*c)
                l=al*l+jnp.sum(p,axis=0,keepdims=True)
                acc=al*acc+mm32(vt_ref[h*HEAD_DIM:(h+1)*HEAD_DIM,ks],p.astype(BF))
                out.append((mn,l,acc))
            return tuple(out)
        init=tuple((jnp.full((1,blk),NEG_BIG,F32),jnp.zeros((1,blk),F32),jnp.zeros((HEAD_DIM,blk),F32)) for _ in range(heads))
        st=lax.fori_loop(0,j,lambda i,cr:tile(i,cr,False),init)
        st=tile(j,st,True)
        for h in range(heads):
            m,l,acc=st[h]
            ot=acc/l
            ot_ref[h*HEAD_DIM:(h+1)*HEAD_DIM,qs]=ot
            o_ref[qs,h*HEAD_DIM:(h+1)*HEAD_DIM]=ot.T.astype(BF)
            lse_ref[h:h+1,qs]=m*c+jnp.log2(l)
        return 0
    lax.fori_loop(0,nb,qstep,0)

def attn_bwd_kernel(q_ref,k_ref,v_ref,do_ref,ot_ref,lse_ref,dq_ref,dk_ref,dv_ref,kt_ref,dka_ref,dva_ref,*,blk,heads):
    n=q_ref.shape[0]; nb=n//blk
    sc=HEAD_DIM**-0.5; c=sc*LOG2E
    for h in range(heads):
        kt_ref[h*HEAD_DIM:(h+1)*HEAD_DIM,:]=k_ref[:,h*HEAD_DIM:(h+1)*HEAD_DIM].T
    dka_ref[...]=jnp.zeros_like(dka_ref); dva_ref[...]=jnp.zeros_like(dva_ref)
    causal=(lax.broadcasted_iota(jnp.int32,(blk,blk),0)<=lax.broadcasted_iota(jnp.int32,(blk,blk),1))
    def qstep(j,_):
        qs=pl.ds(pl.multiple_of(j*blk,blk),blk)
        hs=[slice(h*HEAD_DIM,(h+1)*HEAD_DIM) for h in range(heads)]
        qb=[q_ref[qs,s] for s in hs]; dob=[do_ref[qs,s] for s in hs]
        lse=[lse_ref[h:h+1,qs] for h in range(heads)]
        dl=[jnp.sum(ot_ref[hs[h],qs]*dob[h].astype(F32).T,axis=0,keepdims=True) for h in range(heads)]
        def tile(i,carry,diag):
            ks=pl.ds(pl.multiple_of(i*blk,blk),blk)
            out=[]
            for h in range(heads):
                s=mm32_nt(k_ref[ks,hs[h]],qb[h])
                dp=mm32_nt(v_ref[ks,hs[h]],dob[h])
                p=jnp.exp2(s*c-lse[h])
                if diag: p=jnp.where(causal,p,0.0)
                ds=(p*(dp-dl[h])).astype(BF)
                dva_ref[ks,hs[h]]+=mm32(p.astype(BF),dob[h])
                dka_ref[ks,hs[h]]+=mm32(ds,qb[h])
                out.append(carry[h]+mm32(kt_ref[hs[h],ks],ds))
            return tuple(out)
        st=tuple(jnp.zeros((HEAD_DIM,blk),F32) for _ in range(heads))
        st=lax.fori_loop(0,j,lambda i,cr:tile(i,cr,False),st)
        st=tile(j,st,True)
        for h in range(heads):
            dq_ref[qs,hs[h]]=(st[h]*sc).T.astype(BF)
        return 0
    lax.fori_loop(0,nb,qstep,0)
    dk_ref[...]=(dka_ref[...]*sc).astype(BF)
    dv_ref[...]=dva_ref[...].astype(BF)


VM = pl.BlockSpec(memory_space=pltpu.VMEM)


def attn_fwd(q, k, v):
    n, d = q.shape
    heads = d // HEAD_DIM
    return pl.pallas_call(
        functools.partial(attn_fwd_kernel, blk=FWD_BLOCK, heads=heads),
        out_shape=(jax.ShapeDtypeStruct((n, d), BF), jax.ShapeDtypeStruct((d, n), F32), jax.ShapeDtypeStruct((heads, n), F32)),
        in_specs=[VM] * 3, out_specs=(VM,) * 3, scratch_shapes=[pltpu.VMEM((d, n), BF)], name='attn_fwd',
        cost_estimate=pl.CostEstimate(flops=8 * n * n * d, bytes_accessed=12 * n * d, transcendentals=n * n * heads // 2),
    )(q, k, v)


def attn_bwd(q, k, v, do, ot, lse):
    n, d = q.shape
    heads = d // HEAD_DIM
    return pl.pallas_call(
        functools.partial(attn_bwd_kernel, blk=BWD_BLOCK, heads=heads),
        out_shape=(jax.ShapeDtypeStruct((n, d), BF),) * 3,
        in_specs=[VM] * 6, out_specs=(VM,) * 3,
        scratch_shapes=[pltpu.VMEM((d, n), BF), pltpu.VMEM((n, d), F32), pltpu.VMEM((n, d), F32)], name='attn_bwd',
        cost_estimate=pl.CostEstimate(flops=12 * n * n * d, bytes_accessed=20 * n * d, transcendentals=n * n * heads // 2),
    )(q, k, v, do, ot, lse)


def mm32(a, b):
    return jnp.dot(a, b, preferred_element_type=F32)


def mm32_nt(a, b):
    return lax.dot_general(a, b, NT, preferred_element_type=F32)


def whole(shape):
    return pl.BlockSpec(shape, lambda p: (0,) * len(shape))


def project_heads(hid, w_cat, stats, cos_a, sin_a, gains):
    n_chip, rows, dim = hid.shape
    cols = w_cat.shape[1] // 3
    n = n_chip * rows
    block = pl.BlockSpec((rows, cols), lambda p: (p, 0))
    table = pl.BlockSpec((rows, HEAD_DIM), lambda p: (p, 0))
    return pl.pallas_call(
        proj_kernel, grid=(n_chip,), name='proj',
        out_shape=(jax.ShapeDtypeStruct((n, cols), BF),) * 3 + (jax.ShapeDtypeStruct((n, cols), F32),) * 2,
        in_specs=[pl.BlockSpec((1, rows, dim), lambda p: (p, 0, 0)), whole(w_cat.shape), pl.BlockSpec((1,) + stats.shape[1:], lambda p: (p, 0, 0)), table, table, whole(gains.shape)],
        out_specs=(block,) * 5,
        cost_estimate=pl.CostEstimate(flops=6 * n * dim * cols, bytes_accessed=2 * n * dim + 20 * n * cols, transcendentals=0),
    )(hid, w_cat, stats, cos_a, sin_a, gains)


def token_back(dq, dk, q_raw, k_raw, st, cos_t, sin_t, gains):
    rows, dim = q_raw.shape
    return pl.pallas_call(
        tok_kernel, name='tok_back', in_specs=[VM] * 8, out_specs=(VM,) * 3,
        out_shape=(jax.ShapeDtypeStruct((rows, dim), BF),) * 2 + (jax.ShapeDtypeStruct((2, rows), F32),),
        scratch_shapes=[pltpu.VMEM((rows, dim), F32)],
        cost_estimate=pl.CostEstimate(flops=200 * rows * dim, bytes_accessed=16 * rows * dim, transcendentals=0),
    )(dq, dk, q_raw, k_raw, st, cos_t, sin_t, gains)


def weight_back(d, hid, extra=None, idx=0):
    n, cols = d.shape
    dim = hid.shape[1]
    n_chip = dim // cols
    out_shape = jax.ShapeDtypeStruct((n_chip, 2, cols // 2, cols), F32)
    out_spec = pl.BlockSpec((1, 2, cols // 2, cols), lambda p: (p, 0, 0, 0))
    h_spec = pl.BlockSpec((n, cols), lambda p: (0, p))
    scratch = [pltpu.VMEM((cols, n), BF)]
    cost = pl.CostEstimate(flops=2 * n * cols * dim, bytes_accessed=2 * n * dim + 4 * cols * dim, transcendentals=0)
    if extra is None:
        return pl.pallas_call(dw_v_kernel, grid=(n_chip,), name='dw_v', out_shape=out_shape, in_specs=[whole(d.shape), h_spec], out_specs=out_spec, scratch_shapes=scratch, cost_estimate=cost)(d, hid)
    return pl.pallas_call(
        functools.partial(dw_qk_kernel, idx=idx), grid=(n_chip,), name='dw_qk',
        out_shape=(out_shape, jax.ShapeDtypeStruct((8, cols), F32)),
        in_specs=[whole(d.shape)] + [whole(e.shape) for e in extra] + [h_spec],
        out_specs=(out_spec, whole((8, cols))), scratch_shapes=scratch, cost_estimate=cost,
    )(d, *extra, hid)


def solution(mesh):
    n_sp = mesh.shape['sp']
    n_chip = n_sp // 2
    same_core = [[2 * p + c for p in range(n_chip)] for c in range(2)]
    pairs = [(i, i ^ 1) for i in range(n_sp)]

    def swap(t):
        return lax.ppermute(t, 'sp', pairs)

    def gather(t):
        return lax.all_gather(t, 'sp', axis=0, axis_index_groups=same_core)

    def exchange(t):
        return lax.all_to_all(t, 'sp', split_axis=0, concat_axis=0, axis_index_groups=same_core)

    def device_step(x_loc, gy_loc, positions, g_norm, w_query, w_key, w_value, w_out, g_query, g_key):
        me = lax.axis_index('sp')
        chip, core = me // 2, me % 2
        first = core == 0
        loc, dim = x_loc.shape[1], x_loc.shape[2]
        rows = 2 * loc
        cols = dim // n_chip

        def pick(t, idx):
            return lax.dynamic_index_in_dim(t, idx, 0, keepdims=False)

        def join(mine, other):
            return jnp.where(first, jnp.concatenate([mine, other], 0), jnp.concatenate([other, mine], 0))

        def to_core(t):
            return join(pick(t, core), swap(pick(t, 1 - core)))

        def from_core(t):
            halves = t.reshape(2, loc, dim)
            mine, other = pick(halves, core), swap(pick(halves, 1 - core))
            return jnp.where(first, jnp.stack([mine, other]), jnp.stack([other, mine]))

        def my_cols(w):
            return lax.dynamic_slice_in_dim(w, chip * cols, cols, axis=1)

        def inv_of(raw):
            return lax.rsqrt(jnp.mean(raw * raw, axis=-1, keepdims=True) + NORM_EPS)

        def spread(t):
            return exchange(jnp.broadcast_to(t[None], (n_chip,) + t.shape))

        x_f = to_core(x_loc).astype(F32)
        gy = to_core(gy_loc)
        pos = to_core(positions)
        x_inv = inv_of(x_f)
        x_hat = x_f * x_inv
        hidden = (x_hat * g_norm.astype(F32)).astype(BF)
        hid_all = gather(hidden)
        gy_tied, _ = lax.optimization_barrier((gy, hidden))
        gy_all = gather(gy_tied).reshape(n_chip * rows, dim)
        q_raw, k_raw = mm32(hidden, w_query), mm32(hidden, w_key)
        st = jnp.stack([inv_of(q_raw)[:, 0], inv_of(k_raw)[:, 0], pos.astype(F32)])
        cos_t, sin_t = rope_tables(pos)
        stats = spread(st)

        cos_a, sin_a = rope_tables(stats[:, 2].reshape(n_chip * rows))
        gains = jnp.stack([g_query, g_key]).astype(F32)
        gains_h = lax.dynamic_slice_in_dim(gains, chip * cols, cols, axis=1)
        w_cat = jnp.concatenate([my_cols(w_query), my_cols(w_key), my_cols(w_value)], 1)
        q, k, v, qh_hat, kh_hat = project_heads(hid_all, w_cat, stats, cos_a, sin_a, gains_h)
        hid_all = hid_all.reshape(n_chip * rows, dim)
        att, att_t, lse = attn_fwd(q, k, v)

        def to_tokens(t):
            return exchange(t.reshape(n_chip, rows, cols))

        def flat(t):
            return jnp.moveaxis(t, 0, 1).reshape(rows, dim)

        att_tok = to_tokens(att)
        att_tok, gy_all = lax.optimization_barrier((att_tok, gy_all))
        y = (x_f + mm32(flat(att_tok), w_out)).astype(BF)
        w_rows = lax.dynamic_slice_in_dim(w_out, chip * cols, cols, axis=0)
        d_att = mm32_nt(gy_all, w_rows).astype(BF)
        dq, dk, dv = attn_bwd(q, k, v, d_att, att_t, lse)
        dq_tok, dk_tok, dv_tok = to_tokens(dq), to_tokens(dk), to_tokens(dv)

        dwo = mm32(att_t.astype(BF), gy_all).reshape(2, loc, dim)
        dwo = pick(dwo, core) + swap(pick(dwo, 1 - core))

        def finish_cols(part):
            mine = lax.dynamic_index_in_dim(part, core, 1, keepdims=False)
            other = lax.dynamic_index_in_dim(part, 1 - core, 1, keepdims=False)
            return jnp.moveaxis(exchange(mine + swap(other)), 0, 1).reshape(loc, dim)

        dwv = finish_cols(weight_back(dv, hid_all))
        dq_raw, dk_raw, rowst = token_back(dq_tok, dk_tok, q_raw, k_raw, st, cos_t, sin_t, gains)
        row_all = spread(rowst)
        dwq, dgq = weight_back(dq, hid_all, (qh_hat, stats, row_all, cos_a, sin_a, gains_h), 0)
        dwk, dgk = weight_back(dk, hid_all, (kh_hat, stats, row_all, cos_a, sin_a, gains_h), 1)
        dwq, dwk = finish_cols(dwq), finish_cols(dwk)
        dg = jnp.stack([dgq[0], dgk[0]]).reshape(2, 2, loc)
        dg = jnp.moveaxis(dg, 1, 0)
        dg = pick(dg, core) + swap(pick(dg, 1 - core))

        d_hid = mm32_nt(flat(dv_tok), w_value) + mm32_nt(dq_raw, w_query) + mm32_nt(dk_raw, w_key)
        d_nrm = d_hid * g_norm.astype(F32)
        dxn = x_inv * (d_nrm - x_hat * jnp.mean(d_nrm * x_hat, axis=-1, keepdims=True))
        grad_x = (gy.astype(F32) + dxn).astype(BF)
        dgn = jnp.sum(d_hid * x_hat, axis=0).reshape(n_sp, loc)
        dgn = jnp.sum(lax.all_to_all(dgn, 'sp', split_axis=0, concat_axis=0), axis=0)
        return from_core(y), from_core(grad_x), dgn, dwq, dwk, dwv, dwo, dg[0], dg[1]

    seq_spec = P('dp', 'sp', None)
    mat_rep = P(None, None)
    vec_rep = P(None)
    row_spec = P(('dp', 'sp'), None)
    vec_spec = P(('dp', 'sp'))
    return jax.shard_map(device_step, mesh=mesh, in_specs=(seq_spec, seq_spec, P('dp', 'sp'), vec_rep, mat_rep, mat_rep, mat_rep, mat_rep, vec_rep, vec_rep), out_specs=(seq_spec, seq_spec, vec_spec, row_spec, row_spec, row_spec, row_spec, vec_spec, vec_spec), check_vma=False)
```

time: 1360 us -> 561 us (0.41)
  matrix products: 420 us -> 51.5 us
  waiting for transfers between devices: 607 us -> 264 us
  blocking collectives: 167 us -> 39.4 us
  Pallas kernels: 0 us -> 88.3 us
  local copies, waits for them, and re-layouts: 62 us -> 29.8 us
    reduce_scatter x4 -> x0, waiting for transfers between devices: 517 us -> none  [sum_rows(): return lax.psum_scatter(partial_sum, 'sp', scatter_dimension=0, tiled=True)]
    dot_general x124 -> x8, matrix products: 420 us -> 51.5 us  [the longest x4 29 us: mm32_nt(): return lax.dot_general(a, b, NT, preferred_element_type=F32)]
    all_gather x0 -> x2, waiting for transfers between devices: none -> 195 us  [gather(): return lax.all_gather(t, 'sp', axis=0, axis_index_groups=same_core)]
    pallas_call x0 -> x7, Pallas kernels: none -> 88.3 us  [the longest x2 25.7 us: weight_back(): pl.pallas_call(functools.partial(dw_qk_kernel, idx=idx), grid=(n_chip,),...]
    unnamed x1 -> x0, blocking collectives: 66.2 us -> none
    all_to_all x2, blocking collectives: 100 us -> 39.4 us  [the longest x1 29.1 us: exchange(): lax.all_to_all(t, 'sp', split_axis=0, concat_axis=0, axis_index_groups=sa...]
    all_to_all x6 -> x8, waiting for transfers between devices: 90.3 us -> 65.1 us  [exchange(): lax.all_to_all(t, 'sp', split_axis=0, concat_axis=0, axis_index_groups=sa...]
    dynamic_update_slice x32 -> x0, local copies, waits for them, and re-layouts: 22.5 us -> none  [the longest x16 11.3 us: block_step(): lax.dynamic_update_slice_in_dim(out_buf, out_blk.astype(jnp.bfloat16), q_...]
  transfers between devices with their start and end apart: 10 -> 20, of which waited for: 8 -> 10; matrix products, arithmetic and copies ran while one was open for 11% -> 17% of each run, Pallas kernels for 0% -> 12%
where the time goes in v1:
time: 561 us; the launch traced here: 554 us
  waiting for transfers between devices  264 us (47%)
  Pallas kernels  88.3 us (16%)
  matrix products  51.5 us (9%)
  starting transfers between devices  39.5 us (7%)
  blocking collectives  39.4 us (7%)
  local copies, waits for them, and re-layouts  29.8 us (5%)
  other arithmetic  26.5 us (5%)
  between operations  15 us (3%)
    all_gather x2, waiting for transfers between devices, gather(): return lax.all_gather(t, 'sp', axis=0, axis_index_groups=same_core)  195 us
    all_to_all x8, waiting for transfers between devices, exchange(): lax.all_to_all(t, 'sp', split_axis=0, concat_axis=0, axis_index_groups=sa...  65.1 us
    all_to_all x8, starting transfers between devices, exchange(): lax.all_to_all(t, 'sp', split_axis=0, concat_axis=0, axis_index_groups=sa...  36.7 us
    all_to_all x1, blocking collectives, exchange(): lax.all_to_all(t, 'sp', split_axis=0, concat_axis=0, axis_index_groups=sa...  29.1 us
    dot_general x4, matrix products, mm32_nt(): return lax.dot_general(a, b, NT, preferred_element_type=F32)  29 us
    pallas_call x2, Pallas kernels, weight_back(): pl.pallas_call(functools.partial(dw_qk_kernel, idx=idx), grid=(n_chip,),...  25.7 us
    dot_general x4, matrix products, mm32(): return jnp.dot(a, b, preferred_element_type=F32)  22.6 us
    pallas_call x1, Pallas kernels, attn_bwd(): pl.pallas_call(functools.partial(attn_bwd_kernel, blk=BWD_BLOCK, heads=he...  20.9 us
  transfers between devices with their start and end apart: 20, of which 10 were waited for; matrix products, arithmetic and copies ran while one was open for 17% of the time, Pallas kernels for 12%

profile of v1, /device:TPU:0, one launch (start us, length us, event | category | flops | bytes accessed | tf_op | source)
XLA Modules:
  0.0 553.8 jit_solution(14657201355069634215)
XLA Ops:
  7.3 1.3 constant_dynamic-slice_fusion.10
  9.1 1.5 collective-permute-done
  11.0 1.5 multiply_convert_fusion
  13.2 1.5 collective-permute-done.2
  14.7 1.3 maximum_select_fusion.2
  17.1 1.3 constant_dynamic-slice_fusion.9
  18.4 1.7 constant_dynamic-slice_fusion.7
  20.1 1.7 pad_maximum_fusion.w_ref
  22.5 7.2 %multiply_reduce_fusion.1 = (f32[256]{0:T(256)S(1)}, f32[256,2048]{1,0:T(8,128)}) fusion(bf16[256,2048]{1,0:T(8,128)(2,1)S(1)} %fusion.5, bf16[2048,2048]{1,0:T(8,128)(2,1)} %param.14), kind=kOutput, calls=%fused_computation.21 | convolution fusion | flops 2148531968 | bytes 11535360 | tf_op jit(solution)/shard_map/dot_general | solution.py:211
  29.7 3.9 multiply_reduce_fusion
  34.2 7.5 %all-to-all-start = ((f32[8,3,256]{2,1,0:T(4,128)}), f32[8,3,256]{2,1,0:T(4,128)S(1)}, u32[]{:S(2)}, u32[]{:S(2)}) async-start(f32[8,3,256]{2,1,0:T(4,128)} %broadcast_in_dim.4), calls=%async_computation | async-start | bytes 65536 | tf_op jit(solution)/shard_map/all_to_all | solution.py:279
  41.7 6.9 %all-to-all-done.st_ref = f32[8,3,256]{2,1,0:T(4,128)S(1)} async-done(((f32[8,3,256]{2,1,0:T(4,128)}), f32[8,3,256]{2,1,0:T(4,128)S(1)}, u32[]{:S(2)}, u32[]{:S(2)}) %all-to-all-start) | async-done | bytes 24608 | tf_op jit(solution)/shard_map/all_to_all | solution.py:279
  48.6 3.7 fusion.16
  52.3 1.9 pad_maximum_fusion.1
  54.2 85.4 %all-gather.4.cloned.1.call-done.h_ref = bf16[8,256,2048]{2,1,0:T(8,128)(2,1)} async-done(((bf16[1,256,2048]{2,1,0:T(8,128)(2,1)}), bf16[8,256,2048]{2,1,0:T(8,128)(2,1)}) %all-gather.4.cloned.1.call-update) | async-done | bytes 8388624 | tf_op jit(solution)/shard_map/all_gather | solution.py:276
  139.7 13.0 %proj.1 = (bf16[2048,256]{1,0:T(8,128)(2,1)}, bf16[2048,256]{1,0:T(8,128)(2,1)}, bf16[2048,256]{1,0:T(8,128)(2,1)}, f32[2048,256]{1,0:T(8,128)}, f32[2048,256]{1,0:T(8,128)}) custom-call(bf16[8,256,2048]{2,1,0:T(8,128)(2,1)} %all-gather.4.cloned.1.call-done.h_ref, bf16[2048,768]{1,0:T(8,128)(2,1)} %pad_maximum_fusion.w_ref, f32[8,3,256]{2,1,0:T(4,128)} %copy-done.10, ...), custom_call_target="tpu_custom_call" | custom-call | flops 6442450944 | bytes 18874368 | tf_op jit(solution)/shard_map/proj/pallas_call | solution.py:228
  152.7 12.8 %attn_fwd.1 = (bf16[2048,256]{1,0:T(8,128)(2,1)}, f32[256,2048]{1,0:T(8,128)}, f32[2,2048]{1,0:T(2,128)}) custom-call(bf16[2048,256]{1,0:T(8,128)(2,1)} %get-tuple-element.30.q_ref, bf16[2048,256]{1,0:T(8,128)(2,1)} %get-tuple-element.31.k_ref, bf16[2048,256]{1,0:T(8,128)(2,1)} %get-tuple-element.32.v_ref), custom_call_target="tpu_custom_call" | custom-call | flops 8589934592 | bytes 6291456 | tf_op jit(solution)/shard_map/attn_fwd/pallas_call | solution.py:190
  165.5 2.3 copy.45
  167.8 3.7 all-to-all-start.1
  171.5 110.0 %all-gather.6.cloned.1.call-done = bf16[2048,2048]{1,0:T(8,128)(2,1)} async-done(((bf16[256,2048]{1,0:T(8,128)(2,1)}), bf16[2048,2048]{1,0:T(8,128)(2,1)}) %all-gather.6.cloned.1.call-update) | async-done | bytes 8388624 | tf_op jit(solution)/shard_map/all_gather | solution.py:276
  281.5 7.4 %convolution_convert_fusion.do_ref = bf16[2048,256]{1,0:T(8,128)(2,1)} fusion(bf16[2048,2048]{1,0:T(8,128)(2,1)} %all-gather.6.cloned.1.call-done, bf16[2048,2048]{1,0:T(8,128)(2,1)} %param.17, s32[]{:T(128)S(6)} %select_n.114), kind=kOutput, calls=%fused_computation.11 | convolution fusion | flops 2148007936 | bytes 10485764 | tf_op jit(solution)/shard_map/dot_general | solution.py:215
  288.9 20.9 %attn_bwd.1 = (bf16[2048,256]{1,0:T(8,128)(2,1)}, bf16[2048,256]{1,0:T(8,128)(2,1)}, bf16[2048,256]{1,0:T(8,128)(2,1)}) custom-call(bf16[2048,256]{1,0:T(8,128)(2,1)} %get-tuple-element.30.q_ref, bf16[2048,256]{1,0:T(8,128)(2,1)} %get-tuple-element.31.k_ref, bf16[2048,256]{1,0:T(8,128)(2,1)} %get-tuple-element.32.v_ref, ...), custom_call_target="tpu_custom_call" | custom-call | flops 12884901888 | bytes 10485760 | tf_op jit(solution)/shard_map/attn_bwd/pallas_call | solution.py:201
  309.9 3.6 all-to-all-start.4
  313.5 1.5 copy.46
  314.9 23.8 %all-to-all-done.4.dk_ref = bf16[8,256,256]{2,1,0:T(8,128)(2,1)S(1)} async-done(((bf16[8,256,256]{2,1,0:T(8,128)(2,1)}), bf16[8,256,256]{2,1,0:T(8,128)(2,1)S(1)}, u32[]{:S(2)}, u32[]{:S(2)}) %all-to-all-start.4) | async-done | bytes 1048608 | tf_op jit(solution)/shard_map/all_to_all | solution.py:279
  338.8 29.1 %all_to_all.54 = bf16[8,256,256]{1,2,0:T(8,128)(2,1)} all-to-all(bf16[8,256,256]{1,2,0:T(8,128)(2,1)S(1)} %copy.46), channel_id=1, replica_groups={{0,2,4,6,8,10,12,14},{1,3,5,7,9,11,13,15},{16,18,20,22,24,26,28,30},{17..., dimensions={0} | all-to-all | bytes 2097152 | tf_op jit(solution)/shard_map/all_to_all | solution.py:279
  367.9 4.3 all-to-all-start.3
  372.7 0.9 pad_maximum_fusion.3
  373.6 9.5 %dw_v.1 = f32[8,2,128,256]{3,2,1,0:T(8,128)} custom-call(bf16[2048,256]{1,0:T(8,128)(2,1)} %get-tuple-element.39.d_ref, bf16[2048,2048]{1,0:T(8,128)(2,1)} %bitcast.79), custom_call_target="tpu_custom_call" | custom-call | flops 2147483648 | bytes 10485760 | tf_op jit(solution)/shard_map/dw_v/pallas_call | solution.py:257
  383.1 2.4 dynamic-slice_bitcast_fusion.1
  385.5 7.1 %fusion.22 = f32[256,2048]{1,0:T(8,128)} fusion(bf16[256,2048]{0,1:T(8,128)(2,1)S(1)} %bitcast.98, bf16[2048,2048]{1,0:T(8,128)(2,1)} %param.16), kind=kOutput, calls=%fused_computation.81 | convolution fusion | flops 2147483648 | bytes 11534336 | tf_op jit(solution)/shard_map/dot_general | solution.py:215
  392.6 5.1 all-to-all-done.3.dq_ref
  397.7 1.0 copy-done.3
  398.7 6.3 %tok_back.1 = (bf16[256,2048]{1,0:T(8,128)(2,1)}, bf16[256,2048]{1,0:T(8,128)(2,1)}, f32[2,256]{1,0:T(2,128)}) custom-call(bf16[8,256,256]{2,1,0:T(8,128)(2,1)} %copy-done.3, bf16[8,256,256]{2,1,0:T(8,128)(2,1)} %copy-done.2, f32[256,2048]{1,0:T(8,128)} %get-tuple-element.112.qr_ref, f32[256,2048]{1,0:T(8,128)} %get-tuple-element.110.kr_ref, ...), custom_call_target="tpu_custom_call" | custom-call | flops 104857600 | bytes 8388608 | tf_op jit(solution)/shard_map/tok_back/pallas_call | solution.py:239
  405.0 6.7 %convolution_add_fusion.1 = f32[256,2048]{1,0:T(8,128)S(1)} fusion(f32[256,2048]{1,0:T(8,128)} %fusion.22, bf16[256,2048]{1,0:T(8,128)(2,1)} %get-tuple-element.42, bf16[2048,2048]{1,0:T(8,128)(2,1)} %param.14), kind=kOutput, calls=%fused_computation.9 | convolution fusion | flops 2148007936 | bytes 13631488 | tf_op jit(solution)/shard_map/dot_general | solution.py:215
  411.7 7.8 %fusion.11 = (f32[2048]{0:T(1024)S(1)}, f32[256]{0:T(256)S(1)}, f32[256,2048]{1,0:T(8,128)}) fusion(f32[256]{0:T(256)S(1)} %add_rsqrt_fusion.2, bf16[128,2048]{1,0:T(8,128)(2,1)S(1)} %bitcast.84, bf16[128,2048]{1,0:T(8,128)(2,1)S(1)} %collective-permute-done, pred[]{:T(512)S(6)} %eq.5, f32[2048]{0:T(1024)S(1)} %convert_element_type.65, ...), kind=kOutput, calls=%fused_computation.18 | convolution fusion | flops 2156394240 | bytes 14698497 | tf_op jit(solution)/shard_map/dot_general | solution.py:215
  419.5 10.4 %all_to_all.55 = f32[16,1,128]{2,1,0:T(1,128)S(1)} all-to-all(f32[16,1,128]{2,1,0:T(1,128)S(1)} %bitcast.107), channel_id=1, replica_groups=mesh['dp'=2,'sp'=16] {'sp'}, dimensions={0} | all-to-all | bytes 16384 | tf_op jit(solution)/shard_map/all_to_all | solution.py:371
  430.5 3.3 all-to-all-start.6
  433.8 2.3 bitcast_add_fusion.1
  436.2 3.9 all-to-all-done.6.row_ref
  440.1 3.8 all-to-all-start.9
  444.0 12.9 %dw_qk.2 = (f32[8,2,128,256]{3,2,1,0:T(8,128)}, f32[8,256]{1,0:T(8,128)}) custom-call(bf16[2048,256]{1,0:T(8,128)(2,1)} %get-tuple-element.40.d_ref, f32[2048,256]{1,0:T(8,128)} %get-tuple-element.44.hat_ref, f32[8,3,256]{2,1,0:T(4,128)} %copy-done.10, f32[8,2,256]{2,1,0:T(2,128)} %copy-done.11, f32[2048,128]{1,0:T(8,128)} %get-tuple-element.116.c_ref, ...), custom_call_target="tpu_custom_call" | custom-call | flops 2147483648 | bytes 10485760 | tf_op jit(solution)/shard_map/dw_qk/pallas_call | solution.py:258
  456.9 2.4 dynamic-slice_bitcast_fusion.3
  459.2 5.8 %fusion.4 = bf16[256,2048]{1,0:T(8,128)(2,1)S(1)} fusion(bf16[256,2048]{0,1:T(8,128)(2,1)S(1)} %bitcast.97, bf16[2048,2048]{1,0:T(8,128)(2,1)} %param.17, bf16[128,2048]{1,0:T(8,128)(2,1)S(1)} %bitcast.85, bf16[128,2048]{1,0:T(8,128)(2,1)S(1)} %collective-permute-done, pred[]{:T(512)S(6)} %eq.5), kind=kOutput, calls=%fused_computation.10 | convolution fusion | flops 2153775104 | bytes 11534337 | tf_op jit(solution)/shard_map/dot_general | solution.py:211
  465.0 0.9 constant_dynamic-slice_fusion.3
  466.4 12.8 %dw_qk.3 = (f32[8,2,128,256]{3,2,1,0:T(8,128)}, f32[8,256]{1,0:T(8,128)}) custom-call(bf16[2048,256]{1,0:T(8,128)(2,1)} %get-tuple-element.41.d_ref, f32[2048,256]{1,0:T(8,128)} %get-tuple-element.47.hat_ref, f32[8,3,256]{2,1,0:T(4,128)} %copy-done.10, f32[8,2,256]{2,1,0:T(2,128)} %copy-done.11, f32[2048,128]{1,0:T(8,128)} %get-tuple-element.116.c_ref, ...), custom_call_target="tpu_custom_call" | custom-call | flops 2147483648 | bytes 10485760 | tf_op jit(solution)/shard_map/dw_qk/pallas_call | solution.py:258
  479.2 2.6 bitcast_add_fusion.3
  481.9 6.0 %all-to-all-start.7 = ((f32[8,128,256]{2,1,0:T(8,128)}), f32[8,128,256]{2,1,0:T(8,128)}, u32[]{:S(2)}, u32[]{:S(2)}) async-start(f32[8,128,256]{2,1,0:T(8,128)} %bitcast_add_fusion.3), calls=%async_computation.7 | async-start | bytes 2097152 | tf_op jit(solution)/shard_map/all_to_all | solution.py:279
  487.9 1.5 dynamic-slice_bitcast_fusion.2
  489.8 5.8 %fusion.13 = f32[256,2048]{1,0:T(8,128)S(1)} fusion(bf16[2048,2048]{1,0:T(8,128)(2,1)} %all-gather.6.cloned.1.call-done, f32[256,2048]{1,0:T(8,128)S(1)} %copy-done.20), kind=kOutput, calls=%fused_computation.37 | convolution fusion | flops 2148007936 | bytes 12582912 | tf_op jit(solution)/shard_map/dot_general | solution.py:211
  495.6 1.1 dynamic-slice_bitcast_fusion
  496.8 1.1 maximum_select_fusion.3
  498.7 1.2 bitcast_add_fusion.2
  499.8 13.7 %all-to-all-done.7 = f32[8,128,256]{2,1,0:T(8,128)} async-done(((f32[8,128,256]{2,1,0:T(8,128)}), f32[8,128,256]{2,1,0:T(8,128)}, u32[]{:S(2)}, u32[]{:S(2)}) %all-to-all-start.7) | async-done | bytes 1048608 | tf_op jit(solution)/shard_map/all_to_all | solution.py:279
  513.5 4.5 all-to-all-start.8
  518.0 2.4 fusion.10
  522.6 2.6 bitcast_add_fusion
  526.3 1.1 maximum_select_fusion.4
  527.8 1.3 copy.53
  529.1 1.6 copy.48
  530.6 1.3 copy.51
  531.9 11.6 %all-to-all-done.8 = f32[8,128,256]{2,1,0:T(8,128)} async-done(((f32[8,128,256]{2,1,0:T(8,128)}), f32[8,128,256]{2,1,0:T(8,128)}, u32[]{:S(2)}, u32[]{:S(2)}) %all-to-all-start.8) | async-done | bytes 1048608 | tf_op jit(solution)/shard_map/all_to_all | solution.py:279
  543.5 1.6 copy.49
  545.1 1.3 copy.52
  (101 shorter events, 10.5 us)
Async XLA Ops:
  7.2 2.0 copy-start.14
  7.2 132.5 %all-gather.4.cloned.1.call-start = ((), (), s32[]{:S(2)}) async-start(), calls=%async_computation.10 | async-start | bytes 9437184 | tf_op jit(solution)/shard_map/all_gather | solution.py:276
  8.6 2.1 collective-permute-start
  10.7 1.9 copy-start.9
  12.6 269.0 %all-gather.6.cloned.1.call-start = ((), (), s32[]{:S(2)}) async-start(), calls=%async_computation.11 | async-start | bytes 9437184 | tf_op jit(solution)/shard_map/all_gather | solution.py:276
  12.7 2.0 collective-permute-start.2
  16.0 0.7 copy-start.18
  16.0 1.1 copy-start.15
  16.0 1.1 copy-start.16
  16.6 5.8 %collective-permute-start.1 = (s32[128]{0:T(128)S(1)}, s32[128]{0:T(128)S(1)}, u32[]{:S(2)}, u32[]{:S(2)}) collective-permute-start(s32[128]{0:T(128)S(1)} %get-tuple-element.108), channel_id=1, source_target_pairs={{0,1},{1,0},{2,3},{3,2},{4,5},{5,4},{6,7},{7,6},{8,9},{9,8},{10,11... | collective-permute-start | bytes 1544 | tf_op jit(solution)/shard_map/ppermute | solution.py:273
  17.1 4.8 copy-start.12
  20.1 9.6 %slice-start = ((s8[8388608]{0:T(1024)(128)(4,1)}), s8[4194304]{0:T(1024)(128)(4,1)S(1)}, s32[]{:S(2)}) async-start(s8[8388608]{0:T(1024)(128)(4,1)} %bitcast.103), calls=%async_computation.12 | async-start | bytes 8388608
  22.5 7.2 %slice-start.1 = ((s8[8388608]{0:T(1024)(128)(4,1)}), s8[4194304]{0:T(1024)(128)(4,1)S(1)}, s32[]{:S(2)}) async-start(s8[8388608]{0:T(1024)(128)(4,1)} %bitcast.103), calls=%async_computation.13 | async-start | bytes 8388608
  33.5 20.7 %copy-start.13 = (f32[3,256]{1,0:T(4,128)}, f32[3,256]{1,0:T(4,128)S(1)}, u32[]{:S(2)}) copy-start(f32[3,256]{1,0:T(4,128)S(1)} %pad_maximum_fusion.5.st_ref) | copy-start | bytes 9220
  34.2 14.4 %all-to-all-start = ((f32[8,3,256]{2,1,0:T(4,128)}), f32[8,3,256]{2,1,0:T(4,128)S(1)}, u32[]{:S(2)}, u32[]{:S(2)}) async-start(f32[8,3,256]{2,1,0:T(4,128)} %broadcast_in_dim.4), calls=%async_computation | async-start | bytes 65536 | tf_op jit(solution)/shard_map/all_to_all | solution.py:279
  48.6 5.7 %copy-start.10 = (f32[8,3,256]{2,1,0:T(4,128)}, f32[8,3,256]{2,1,0:T(4,128)S(1)}, u32[]{:S(2)}) copy-start(f32[8,3,256]{2,1,0:T(4,128)S(1)} %all-to-all-done.st_ref) | copy-start | bytes 73732
  167.8 113.7 %all-to-all-start.1 = ((bf16[8,256,256]{1,2,0:T(8,128)(2,1)}), bf16[8,256,256]{1,2,0:T(8,128)(2,1)S(1)}, u32[]{:S(2)}, u32[]{:S(2)}) async-start(bf16[8,256,256]{1,2,0:T(8,128)(2,1)} %copy.45), calls=%async_computation.1 | async-start | bytes 2097152 | tf_op jit(solution)/shard_map/all_to_all | solution.py:279
  281.5 7.4 %copy-start.6 = (bf16[8,256,256]{1,2,0:T(8,128)(2,1)}, bf16[8,256,256]{1,2,0:T(8,128)(2,1)S(1)}, u32[]{:S(2)}) copy-start(bf16[8,256,256]{1,2,0:T(8,128)(2,1)S(1)} %all-to-all-done.1) | copy-start | bytes 3145732
  309.9 28.9 %all-to-all-start.4 = ((bf16[8,256,256]{2,1,0:T(8,128)(2,1)}), bf16[8,256,256]{2,1,0:T(8,128)(2,1)S(1)}, u32[]{:S(2)}, u32[]{:S(2)}) async-start(bf16[8,256,256]{2,1,0:T(8,128)(2,1)} %bitcast.88), calls=%async_computation.4 | async-start | bytes 2097152 | tf_op jit(solution)/shard_map/all_to_all | solution.py:279
  338.8 29.1 %copy-start.2 = (bf16[8,256,256]{2,1,0:T(8,128)(2,1)}, bf16[8,256,256]{2,1,0:T(8,128)(2,1)S(1)}, u32[]{:S(2)}) copy-start(bf16[8,256,256]{2,1,0:T(8,128)(2,1)S(1)} %all-to-all-done.4.dk_ref) | copy-start | bytes 3145732
  367.9 29.8 %all-to-all-start.3 = ((bf16[8,256,256]{2,1,0:T(8,128)(2,1)}), bf16[8,256,256]{2,1,0:T(8,128)(2,1)S(1)}, u32[]{:S(2)}, u32[]{:S(2)}) async-start(bf16[8,256,256]{2,1,0:T(8,128)(2,1)} %bitcast.19), calls=%async_computation.3 | async-start | bytes 2097152 | tf_op jit(solution)/shard_map/all_to_all | solution.py:279
  383.1 2.4 copy-start.8
  385.5 48.4 %collective-permute-start.7 = (f32[8,128,256]{2,1,0:T(8,128)}, f32[8,128,256]{2,1,0:T(8,128)}, u32[]{:S(2)}, u32[]{:S(2)}) collective-permute-start(f32[8,128,256]{2,1,0:T(8,128)} %dynamic-slice_bitcast_fusion.1), channel_id=1, source_target_pairs={{0,1},{1,0},{2,3},{3,2},{4,5},{5,4},{6,7},{7,6},{8,9},{9,8},{10,11... | collective-permute-start | bytes 3145736 | tf_op jit(solution)/shard_map/ppermute | solution.py:273
  397.7 1.0 copy-start.3
  404.9 6.7 %copy-start.19 = (bf16[256,2048]{1,0:T(8,128)(2,1)S(1)}, bf16[256,2048]{1,0:T(8,128)(2,1)}, u32[]{:S(2)}) copy-start(bf16[256,2048]{1,0:T(8,128)(2,1)} %get-tuple-element.43) | copy-start | bytes 3145732
  411.7 18.2 %copy-start.17 = (f32[2,256]{1,0:T(2,128)S(1)}, f32[2,256]{1,0:T(2,128)}, u32[]{:S(2)}) copy-start(f32[2,256]{1,0:T(2,128)} %get-tuple-element.45) | copy-start | bytes 6148
  411.7 22.1 %copy-start.1 = (f32[8,2,128,256]{3,2,1,0:T(8,128)S(1)}, f32[8,2,128,256]{3,2,1,0:T(8,128)}, u32[]{:S(2)}) copy-start(f32[8,2,128,256]{3,2,1,0:T(8,128)} %dw_v.1) | copy-start | bytes 6291460
  430.5 9.6 %all-to-all-start.6 = ((f32[8,2,256]{2,1,0:T(2,128)}), f32[8,2,256]{2,1,0:T(2,128)S(1)}, u32[]{:S(2)}, u32[]{:S(2)}) async-start(f32[8,2,256]{2,1,0:T(2,128)} %broadcast_in_dim.5), calls=%async_computation.6 | async-start | bytes 32768 | tf_op jit(solution)/shard_map/all_to_all | solution.py:279
  440.1 3.8 copy-start.11
  440.1 41.8 %all-to-all-start.9 = ((f32[8,128,256]{2,1,0:T(8,128)}), f32[8,128,256]{2,1,0:T(8,128)S(1)}, u32[]{:S(2)}, u32[]{:S(2)}) async-start(f32[8,128,256]{2,1,0:T(8,128)} %bitcast_add_fusion.1), calls=%async_computation.9 | async-start | bytes 2097152 | tf_op jit(solution)/shard_map/all_to_all | solution.py:279
  456.8 2.4 copy-start.7
  459.2 20.0 %collective-permute-start.5 = (f32[8,128,256]{2,1,0:T(8,128)}, f32[8,128,256]{2,1,0:T(8,128)}, u32[]{:S(2)}, u32[]{:S(2)}) collective-permute-start(f32[8,128,256]{2,1,0:T(8,128)} %dynamic-slice_bitcast_fusion.3), channel_id=1, source_target_pairs={{0,1},{1,0},{2,3},{3,2},{4,5},{5,4},{6,7},{7,6},{8,9},{9,8},{10,11... | collective-permute-start | bytes 3145736 | tf_op jit(solution)/shard_map/ppermute | solution.py:273
  465.9 30.9 %collective-permute-start.3 = (bf16[128,2048]{1,0:T(8,128)(2,1)}, bf16[128,2048]{1,0:T(8,128)(2,1)S(1)}, u32[]{:S(2)}, u32[]{:S(2)}) collective-permute-start(bf16[128,2048]{1,0:T(8,128)(2,1)} %get-tuple-element.92), channel_id=1, source_target_pairs={{0,1},{1,0},{2,3},{3,2},{4,5},{5,4},{6,7},{7,6},{8,9},{9,8},{10,11... | collective-permute-start | bytes 1572872 | tf_op jit(solution)/shard_map/ppermute | solution.py:273
  481.9 31.6 %all-to-all-start.7 = ((f32[8,128,256]{2,1,0:T(8,128)}), f32[8,128,256]{2,1,0:T(8,128)}, u32[]{:S(2)}, u32[]{:S(2)}) async-start(f32[8,128,256]{2,1,0:T(8,128)} %bitcast_add_fusion.3), calls=%async_computation.7 | async-start | bytes 2097152 | tf_op jit(solution)/shard_map/all_to_all | solution.py:279
  487.8 1.9 copy-start.20
  489.3 8.6 %collective-permute-start.6 = (f32[8,128,256]{2,1,0:T(8,128)S(1)}, f32[8,128,256]{2,1,0:T(8,128)S(1)}, u32[]{:S(2)}, u32[]{:S(2)}) collective-permute-start(f32[8,128,256]{2,1,0:T(8,128)S(1)} %dynamic-slice_bitcast_fusion.2), channel_id=1, source_target_pairs={{0,1},{1,0},{2,3},{3,2},{4,5},{5,4},{6,7},{7,6},{8,9},{9,8},{10,11... | collective-permute-start | bytes 3145736 | tf_op jit(solution)/shard_map/ppermute | solution.py:273
  495.5 2.4 copy-start.4
  495.6 3.1 copy-start.5
  496.6 26.0 %collective-permute-start.8 = (f32[128,2048]{1,0:T(8,128)}, f32[128,2048]{1,0:T(8,128)}, u32[]{:S(2)}, u32[]{:S(2)}) collective-permute-start(f32[128,2048]{1,0:T(8,128)} %dynamic-slice_bitcast_fusion), channel_id=1, source_target_pairs={{0,1},{1,0},{2,3},{3,2},{4,5},{5,4},{6,7},{7,6},{8,9},{9,8},{10,11... | collective-permute-start | bytes 3145736 | tf_op jit(solution)/shard_map/ppermute | solution.py:273
  497.9 20.1 %copy-start = (bf16[256,2048]{1,0:T(8,128)(2,1)S(1)}, bf16[256,2048]{1,0:T(8,128)(2,1)}, u32[]{:S(2)}) copy-start(bf16[256,2048]{1,0:T(8,128)(2,1)} %maximum_select_fusion.2) | copy-start | bytes 3145732
  513.5 30.1 %all-to-all-start.8 = ((f32[8,128,256]{2,1,0:T(8,128)}), f32[8,128,256]{2,1,0:T(8,128)}, u32[]{:S(2)}, u32[]{:S(2)}) async-start(f32[8,128,256]{2,1,0:T(8,128)} %bitcast_add_fusion.2), calls=%async_computation.8 | async-start | bytes 2097152 | tf_op jit(solution)/shard_map/all_to_all | solution.py:279
  520.5 5.8 %collective-permute-start.4 = (bf16[128,2048]{1,0:T(8,128)(2,1)S(1)}, bf16[128,2048]{1,0:T(8,128)(2,1)S(1)}, u32[]{:S(2)}, u32[]{:S(2)}) collective-permute-start(bf16[128,2048]{1,0:T(8,128)(2,1)S(1)} %get-tuple-element.90), channel_id=1, source_target_pairs={{0,1},{1,0},{2,3},{3,2},{4,5},{5,4},{6,7},{7,6},{8,9},{9,8},{10,11... | collective-permute-start | bytes 1572872 | tf_op jit(solution)/shard_map/ppermute | solution.py:273
  522.0 3.7 collective-permute-start.9
Sparse Core Ops, SparseCore 0:
  12.7 126.9 all-gather.3
  141.8 139.6 all-gather.5

commit v2 on v1

--- a/solution.py
+++ b/solution.py
@@ -11,18 +11,18 @@
 ROPE_BASE = 10000.0
 NEG_BIG = -1e30
 LOG2E = 1.4426950408889634
-FWD_BLOCK = 1024
+FWD_BLOCK = 512
+CHUNKS = 4
 BWD_BLOCK = 512
 F32, BF = jnp.float32, jnp.bfloat16
 NT = (((1,), (1,)), ((), ()))
 
 
-def rope_tables(positions):
+def rope_rows():
     half = HEAD_DIM // 2
     inv_freq = ROPE_BASE ** (-jnp.arange(half, dtype=F32) * (2.0 / HEAD_DIM))
-    angles = positions.astype(F32)[:, None] * inv_freq
-    cos_t, sin_t = jnp.cos(angles), jnp.sin(angles)
-    return jnp.concatenate([cos_t, cos_t], 1), jnp.concatenate([-sin_t, sin_t], 1)
+    sign = jnp.concatenate([-jnp.ones(half, F32), jnp.ones(half, F32)])
+    return jnp.stack([jnp.concatenate([inv_freq, inv_freq]), sign])
 
 
 def column(row):
@@ -35,21 +35,6 @@
 
 def half_roll(u):
     return pltpu.roll(u, HEAD_DIM // 2, 1)
-
-
-def proj_kernel(h_ref, w_ref, st_ref, c_ref, s_ref, g_ref, q_ref, k_ref, v_ref, qh_ref, kh_ref):
-    h = h_ref[0]
-    cols = q_ref.shape[1]
-    for idx, (out, hat_out) in enumerate(((q_ref, qh_ref), (k_ref, kh_ref))):
-        raw = mm32(h, w_ref[:, idx * cols:(idx + 1) * cols])
-        inv = column(st_ref[0, idx:idx + 1, :])
-        for lo in range(0, cols, HEAD_DIM):
-            hs = slice(lo, lo + HEAD_DIM)
-            hat = raw[:, hs] * inv
-            hat_out[:, hs] = hat
-            u = hat * g_ref[idx:idx + 1, hs]
-            out[:, hs] = (u * c_ref[...] + half_roll(u) * s_ref[...]).astype(BF)
-    v_ref[...] = mm32(h, w_ref[:, 2 * cols:]).astype(BF)
 
 
 def tok_kernel(dq_ref, dk_ref, qr_ref, kr_ref, st_ref, c_ref, s_ref, g_ref, qo_ref, ko_ref, row_ref, nrm_ref):
@@ -72,7 +57,7 @@
 
 
 def dw_qk_kernel(d_ref, hat_ref, st_ref, row_ref, c_ref, s_ref, g_ref, h_ref, out_ref, dg_ref, dt_ref, *, idx):
-    n_chip, rows = st_ref.shape[0], st_ref.shape[2]
+    n_chip, rows = row_ref.shape[0], row_ref.shape[2]
     cols = d_ref.shape[1]
 
     @pl.when(pl.program_id(0) == 0)
@@ -80,7 +65,7 @@
         dg_ref[...] = jnp.zeros_like(dg_ref)
         for p in range(n_chip):
             ts = slice(p * rows, (p + 1) * rows)
-            inv = column(st_ref[p, idx:idx + 1, :])
+            inv = column(st_ref[idx * n_chip + p:idx * n_chip + p + 1, :])
             row = column(row_ref[p, idx:idx + 1, :])
             for lo in range(0, cols, HEAD_DIM):
                 hs = slice(lo, lo + HEAD_DIM)
@@ -109,40 +94,239 @@
     out_ref[0, 1] = dw[half:]
 
 
-def attn_fwd_kernel(q_ref,k_ref,v_ref,o_ref,ot_ref,lse_ref,vt_ref,*,blk,heads):
-    n=q_ref.shape[0]; nb=n//blk
-    c=HEAD_DIM**-0.5*LOG2E
-    for h in range(heads):
-        vt_ref[h*HEAD_DIM:(h+1)*HEAD_DIM,:]=v_ref[:,h*HEAD_DIM:(h+1)*HEAD_DIM].T
-    causal=(lax.broadcasted_iota(jnp.int32,(blk,blk),0)<=lax.broadcasted_iota(jnp.int32,(blk,blk),1))
-    def qstep(j,_):
-        qs=pl.ds(pl.multiple_of(j*blk,blk),blk)
-        qb=[q_ref[qs,h*HEAD_DIM:(h+1)*HEAD_DIM] for h in range(heads)]
-        def tile(i,carry,diag):
-            ks=pl.ds(pl.multiple_of(i*blk,blk),blk)
-            out=[]
-            for h in range(heads):
-                m,l,acc=carry[h]
-                s=mm32_nt(k_ref[ks,h*HEAD_DIM:(h+1)*HEAD_DIM],qb[h])
-                if diag: s=jnp.where(causal,s,NEG_BIG)
-                mn=jnp.maximum(m,jnp.max(s,axis=0,keepdims=True))
-                al=jnp.exp2((m-mn)*c)
-                p=jnp.exp2((s-mn)*c)
-                l=al*l+jnp.sum(p,axis=0,keepdims=True)
-                acc=al*acc+mm32(vt_ref[h*HEAD_DIM:(h+1)*HEAD_DIM,ks],p.astype(BF))
-                out.append((mn,l,acc))
+def front_kernel(h_ref, gy_ref, pos_ref, w_ref, wrow_ref, g_ref, f_ref,
+                 hall_ref, q_ref, k_ref, v_ref, qh_ref, kh_ref, ot_ref, lse_ref, atok_ref, datt_ref, dwo_ref, c_ref, s_ref, inv_ref,
+                 buf, att_ref, vt_ref, pos_all, ssq, ssq_all,
+                 load_sem, out_sem, ssem, rsem, ps_sem, pr_sem, qs_sem, qr_sem, as_sem, ar_sem):
+    me = lax.axis_index('sp')
+    chip, core = me // 2, lax.rem(me, 2)
+    n_chip, rows, dim = hall_ref.shape
+    cols = q_ref.shape[1]
+    part = rows // CHUNKS
+    half = n_chip // 2
+    heads = [slice(lo, lo + HEAD_DIM) for lo in range(0, cols, HEAD_DIM)]
+
+    def spot(p):
+        z, y = p // 2, lax.rem(p, 2)
+        return z + y * (n_chip - 1 - 2 * z)
+
+    def chip_at(r):
+        y = r // half
+        return 2 * (r + y * (n_chip - 1 - 2 * r)) + y
+
+    ring = spot(chip)
+
+    def slot_at(dr, dist):
+        step = dist if dr == 0 else -dist
+        return chip_at(lax.rem(ring - step + 2 * n_chip, n_chip))
+
+    def dev(p):
+        return {'sp': 2 * p + core}
+
+    right = dev(slot_at(1, 1))
+    left = dev(slot_at(0, 1))
+
+    def hop(t, dr, s, c, dist):
+        view = buf.at[t, slot_at(dr, dist), pl.ds(c * part, part)]
+        return pltpu.make_async_remote_copy(
+            src_ref=view, dst_ref=view, send_sem=ssem.at[t, dr, s, c], recv_sem=rsem.at[t, dr, s, c],
+            device_id=right if dr == 0 else left, device_id_type=pl.DeviceIdType.MESH)
+
+    def in_half(dr, c):
+        return (c < CHUNKS // 2) == (dr == 0)
+
+    def start_own(t):
+        for c in range(CHUNKS):
+            for dr in range(2):
+                hop(t, dr, 0, c, 0).start()
+
+    def stage(t, s):
+        for c in range(CHUNKS):
+            for dr in range(2):
+                hop(t, dr, s, c, s + 1).wait_recv()
+                if in_half(dr, c):
+                    hop(t, dr, s + 1, c, s + 1).start()
+                else:
+                    @pl.when(s < half - 2)
+                    def _():
+                        hop(t, dr, s + 1, c, s + 1).start()
+
+    def last_stage(t):
+        for c in range(CHUNKS):
+            for dr in range(2):
+                if in_half(dr, c):
+                    hop(t, dr, half - 1, c, half).wait_recv()
+
+    def drain(t):
+        for s in range(half):
+            for c in range(CHUNKS):
+                for dr in range(2):
+                    if s < half - 1 or in_half(dr, c):
+                        hop(t, dr, s, c, s).wait_send()
+
+    def to_peers(src, dst, s_sem, r_sem):
+        def make(p, owner):
+            return pltpu.make_async_remote_copy(
+                src_ref=src, dst_ref=dst.at[owner], send_sem=s_sem.at[p], recv_sem=r_sem.at[owner],
+                device_id=dev(p), device_id_type=pl.DeviceIdType.MESH)
+        return make
+
+    def each_peer(fn):
+        for p in range(n_chip):
+            @pl.when(p != chip)
+            def _():
+                fn(p)
+
+    loads = [pltpu.make_async_copy(src, buf.at[t, chip], load_sem.at[t]) for t, src in enumerate((h_ref, gy_ref))]
+    for ld in loads:
+        ld.start()
+    barrier = pltpu.get_barrier_semaphore()
+    each_peer(lambda p: pl.semaphore_signal(barrier, inc=1, device_id=dev(p), device_id_type=pl.DeviceIdType.MESH))
+    pl.semaphore_wait(barrier, n_chip - 1)
+    pos_copy = to_peers(pos_ref, pos_all, ps_sem, pr_sem)
+    each_peer(lambda p: pos_copy(p, chip).start())
+    pos_all[chip] = pos_ref[...]
+    loads[0].wait()
+    start_own(0)
+
+    def project(p):
+        ts = pl.ds(pl.multiple_of(p * rows, rows), rows)
+        h = buf[0, p]
+        for idx, out in enumerate((qh_ref, kh_ref)):
+            raw = mm32(h, w_ref[:, idx * cols:(idx + 1) * cols])
+            out[ts, :] = raw
+            ssq[pl.ds(idx * n_chip + p, 1), :] = as_row(jnp.sum(raw * raw, axis=1, keepdims=True))
+        v_ref[ts, :] = mm32(h, w_ref[:, 2 * cols:]).astype(BF)
+
+    project(chip)
+    each_peer(lambda p: pos_copy(p, p).wait_recv())
+    for p in range(n_chip):
+        angles = column(pos_all[p, 0:1, :]) * f_ref[0:1, :]
+        c_ref[p * rows:(p + 1) * rows, :] = jnp.cos(angles)
+        s_ref[p * rows:(p + 1) * rows, :] = jnp.sin(angles) * f_ref[1:2, :]
+
+    def gather_step(s, _):
+        stage(0, s)
+
+        def both(dr, _):
+            dist = (s + 1) * (1 - 2 * dr)
+            project(chip_at(lax.rem(ring - dist + 2 * n_chip, n_chip)))
+            return 0
+
+        lax.fori_loop(0, 2, both, 0)
+        return 0
+
+    lax.fori_loop(0, half - 1, gather_step, 0)
+    loads[1].wait()
+    start_own(1)
+    last_stage(0)
+    project(slot_at(0, half))
+    hall_copy = pltpu.make_async_copy(buf.at[0], hall_ref, out_sem)
+    hall_copy.start()
+    for hs in heads:
+        vt_ref[hs, :] = v_ref[:, hs].T
+    ssq_copy = to_peers(ssq, ssq_all, qs_sem, qr_sem)
+    each_peer(lambda p: ssq_copy(p, chip).start())
+    ssq_all[chip] = ssq[...]
+    each_peer(lambda p: ssq_copy(p, p).wait_recv())
+    total = ssq_all[0]
+    for p in range(1, n_chip):
+        total = total + ssq_all[p]
+    inv_ref[...] = lax.rsqrt(total / dim + NORM_EPS)
+
+    def finish_qk(p, _):
+        ts = pl.ds(pl.multiple_of(p * rows, rows), rows)
+        for idx, (hat_ref, out) in enumerate(((qh_ref, q_ref), (kh_ref, k_ref))):
+            inv = column(inv_ref[pl.ds(idx * n_chip + p, 1), :])
+            for hs in heads:
+                hat = hat_ref[ts, hs] * inv
+                hat_ref[ts, hs] = hat
+                u = hat * g_ref[idx:idx + 1, hs]
+                out[ts, hs] = (u * c_ref[ts, :] + half_roll(u) * s_ref[ts, :]).astype(BF)
+        return 0
+
+    lax.fori_loop(0, n_chip, finish_qk, 0)
+
+    blk = FWD_BLOCK
+    scale = HEAD_DIM ** -0.5 * LOG2E
+    causal = lax.broadcasted_iota(jnp.int32, (blk, blk), 0) <= lax.broadcasted_iota(jnp.int32, (blk, blk), 1)
+
+    def attend(j, _):
+        qs = pl.ds(pl.multiple_of(j * blk, blk), blk)
+        qb = [q_ref[qs, hs] for hs in heads]
+
+        def tile(i, carry, diag):
+            ks = pl.ds(pl.multiple_of(i * blk, blk), blk)
+            out = []
+            for h, hs in enumerate(heads):
+                m, l, acc = carry[h]
+                s = mm32_nt(k_ref[ks, hs], qb[h])
+                if diag:
+                    s = jnp.where(causal, s, NEG_BIG)
+                mn = jnp.maximum(m, jnp.max(s, axis=0, keepdims=True))
+                al = jnp.exp2((m - mn) * scale)
+                p = jnp.exp2((s - mn) * scale)
+                l = al * l + jnp.sum(p, axis=0, keepdims=True)
+                out.append((mn, l, al * acc + mm32(vt_ref[hs, ks], p.astype(BF))))
             return tuple(out)
-        init=tuple((jnp.full((1,blk),NEG_BIG,F32),jnp.zeros((1,blk),F32),jnp.zeros((HEAD_DIM,blk),F32)) for _ in range(heads))
-        st=lax.fori_loop(0,j,lambda i,cr:tile(i,cr,False),init)
-        st=tile(j,st,True)
-        for h in range(heads):
-            m,l,acc=st[h]
-            ot=acc/l
-            ot_ref[h*HEAD_DIM:(h+1)*HEAD_DIM,qs]=ot
-            o_ref[qs,h*HEAD_DIM:(h+1)*HEAD_DIM]=ot.T.astype(BF)
-            lse_ref[h:h+1,qs]=m*c+jnp.log2(l)
+
+        st = tuple((jnp.full((1, blk), NEG_BIG, F32), jnp.zeros((1, blk), F32), jnp.zeros((HEAD_DIM, blk), F32)) for _ in heads)
+        st = lax.fori_loop(0, j, lambda i, cr: tile(i, cr, False), st)
+        st = tile(j, st, True)
+        for h, hs in enumerate(heads):
+            m, l, acc = st[h]
+            ot = acc / l
+            ot_ref[hs, qs] = ot
+            att_ref[qs, hs] = ot.T.astype(BF)
+            lse_ref[h:h + 1, qs] = m * scale + jnp.log2(l)
         return 0
-    lax.fori_loop(0,nb,qstep,0)
+
+    def att_copy(p, owner):
+        return pltpu.make_async_remote_copy(
+            src_ref=att_ref.at[pl.ds(p * rows, rows)], dst_ref=atok_ref.at[owner], send_sem=as_sem.at[p], recv_sem=ar_sem.at[owner],
+            device_id=dev(p), device_id_type=pl.DeviceIdType.MESH)
+
+    def send_att(lo, hi):
+        for p in range(lo, hi):
+            @pl.when(p != chip)
+            def _():
+                att_copy(p, chip).start()
+
+    def use_gy(p):
+        ts = pl.ds(pl.multiple_of(p * rows, rows), rows)
+        gy = buf[1, p]
+        datt_ref[ts, :] = mm32_nt(gy, wrow_ref[...]).astype(BF)
+        dwo_ref[...] += mm32(ot_ref[:, ts].astype(BF), gy)
+
+    n_att = n_chip * rows // blk
+    lax.fori_loop(0, n_att // 2, attend, 0)
+    stage(1, 0)
+    send_att(0, half)
+    lax.fori_loop(n_att // 2, n_att, attend, 0)
+    stage(1, 1)
+    send_att(half, n_chip)
+    atok_ref[chip] = att_ref[pl.ds(pl.multiple_of(chip * rows, rows), rows), :]
+    dwo_ref[...] = jnp.zeros_like(dwo_ref)
+
+    def use_ring(n, _):
+        dist = ((n + 1) // 2) * (2 * lax.rem(n, 2) - 1)
+        use_gy(chip_at(lax.rem(ring - dist + 2 * n_chip, n_chip)))
+        return 0
+
+    lax.fori_loop(0, n_chip - 3, use_ring, 0)
+    stage(1, half - 2)
+    lax.fori_loop(n_chip - 3, n_chip - 1, use_ring, 0)
+    last_stage(1)
+    use_gy(slot_at(0, half))
+
+    each_peer(lambda p: att_copy(p, p).wait_recv())
+    each_peer(lambda p: att_copy(p, chip).wait_send())
+    each_peer(lambda p: pos_copy(p, chip).wait_send())
+    each_peer(lambda p: ssq_copy(p, chip).wait_send())
+    drain(0)
+    drain(1)
+    hall_copy.wait()
+
 
 def attn_bwd_kernel(q_ref,k_ref,v_ref,do_ref,ot_ref,lse_ref,dq_ref,dk_ref,dv_ref,kt_ref,dka_ref,dva_ref,*,blk,heads):
     n=q_ref.shape[0]; nb=n//blk
@@ -184,17 +368,6 @@
 VM = pl.BlockSpec(memory_space=pltpu.VMEM)
 
 
-def attn_fwd(q, k, v):
-    n, d = q.shape
-    heads = d // HEAD_DIM
-    return pl.pallas_call(
-        functools.partial(attn_fwd_kernel, blk=FWD_BLOCK, heads=heads),
-        out_shape=(jax.ShapeDtypeStruct((n, d), BF), jax.ShapeDtypeStruct((d, n), F32), jax.ShapeDtypeStruct((heads, n), F32)),
-        in_specs=[VM] * 3, out_specs=(VM,) * 3, scratch_shapes=[pltpu.VMEM((d, n), BF)], name='attn_fwd',
-        cost_estimate=pl.CostEstimate(flops=8 * n * n * d, bytes_accessed=12 * n * d, transcendentals=n * n * heads // 2),
-    )(q, k, v)
-
-
 def attn_bwd(q, k, v, do, ot, lse):
     n, d = q.shape
     heads = d // HEAD_DIM
@@ -219,19 +392,27 @@
     return pl.BlockSpec(shape, lambda p: (0,) * len(shape))
 
 
-def project_heads(hid, w_cat, stats, cos_a, sin_a, gains):
-    n_chip, rows, dim = hid.shape
-    cols = w_cat.shape[1] // 3
+def front(hid, gy, pos, w_cat, w_rows, gains, freq, n_chip):
+    rows, dim = hid.shape
+    cols = w_rows.shape[0]
     n = n_chip * rows
-    block = pl.BlockSpec((rows, cols), lambda p: (p, 0))
-    table = pl.BlockSpec((rows, HEAD_DIM), lambda p: (p, 0))
+    heads = cols // HEAD_DIM
+    any_spec = pl.BlockSpec(memory_space=pl.ANY)
+    half = n_chip // 2
+    dma = pltpu.SemaphoreType.DMA
+    outs = [((n_chip, rows, dim), BF), ((n, cols), BF), ((n, cols), BF), ((n, cols), BF), ((n, cols), F32), ((n, cols), F32), ((cols, n), F32), ((heads, n), F32),
+            ((n_chip, rows, cols), BF), ((n, cols), BF), ((cols, dim), F32), ((n, HEAD_DIM), F32), ((n, HEAD_DIM), F32), ((2 * n_chip, rows), F32)]
     return pl.pallas_call(
-        proj_kernel, grid=(n_chip,), name='proj',
-        out_shape=(jax.ShapeDtypeStruct((n, cols), BF),) * 3 + (jax.ShapeDtypeStruct((n, cols), F32),) * 2,
-        in_specs=[pl.BlockSpec((1, rows, dim), lambda p: (p, 0, 0)), whole(w_cat.shape), pl.BlockSpec((1,) + stats.shape[1:], lambda p: (p, 0, 0)), table, table, whole(gains.shape)],
-        out_specs=(block,) * 5,
-        cost_estimate=pl.CostEstimate(flops=6 * n * dim * cols, bytes_accessed=2 * n * dim + 20 * n * cols, transcendentals=0),
-    )(hid, w_cat, stats, cos_a, sin_a, gains)
+        front_kernel, name='front', out_shape=tuple(jax.ShapeDtypeStruct(s, d) for s, d in outs),
+        in_specs=[any_spec, any_spec] + [VM] * 5, out_specs=(any_spec,) + (VM,) * 13,
+        scratch_shapes=[
+            pltpu.VMEM((2, n_chip, rows, dim), BF), pltpu.VMEM((n, cols), BF), pltpu.VMEM((cols, n), BF),
+            pltpu.VMEM((n_chip, 8, rows), F32), pltpu.VMEM((2 * n_chip, rows), F32), pltpu.VMEM((n_chip, 2 * n_chip, rows), F32),
+            dma((2,)), dma(()), dma((2, 2, half, CHUNKS)), dma((2, 2, half, CHUNKS)),
+            dma((n_chip,)), dma((n_chip,)), dma((n_chip,)), dma((n_chip,)), dma((n_chip,)), dma((n_chip,))],
+        compiler_params=pltpu.CompilerParams(collective_id=0, has_side_effects=True, vmem_limit_bytes=67043328),
+        cost_estimate=pl.CostEstimate(flops=400 * n * dim * cols, bytes_accessed=40 * n * dim, transcendentals=n * n * heads // 2),
+    )(hid, gy, pos, w_cat, w_rows, gains, freq)
 
 
 def token_back(dq, dk, q_raw, k_raw, st, cos_t, sin_t, gains):
@@ -272,9 +453,6 @@
     def swap(t):
         return lax.ppermute(t, 'sp', pairs)
 
-    def gather(t):
-        return lax.all_gather(t, 'sp', axis=0, axis_index_groups=same_core)
-
     def exchange(t):
         return lax.all_to_all(t, 'sp', split_axis=0, concat_axis=0, axis_index_groups=same_core)
 
@@ -315,21 +493,22 @@
         x_inv = inv_of(x_f)
         x_hat = x_f * x_inv
         hidden = (x_hat * g_norm.astype(F32)).astype(BF)
-        hid_all = gather(hidden)
-        gy_tied, _ = lax.optimization_barrier((gy, hidden))
-        gy_all = gather(gy_tied).reshape(n_chip * rows, dim)
-        q_raw, k_raw = mm32(hidden, w_query), mm32(hidden, w_key)
-        st = jnp.stack([inv_of(q_raw)[:, 0], inv_of(k_raw)[:, 0], pos.astype(F32)])
-        cos_t, sin_t = rope_tables(pos)
-        stats = spread(st)
-
-        cos_a, sin_a = rope_tables(stats[:, 2].reshape(n_chip * rows))
+        pos_f = jnp.broadcast_to(pos.astype(F32)[None], (8, rows))
         gains = jnp.stack([g_query, g_key]).astype(F32)
         gains_h = lax.dynamic_slice_in_dim(gains, chip * cols, cols, axis=1)
         w_cat = jnp.concatenate([my_cols(w_query), my_cols(w_key), my_cols(w_value)], 1)
-        q, k, v, qh_hat, kh_hat = project_heads(hid_all, w_cat, stats, cos_a, sin_a, gains_h)
+        w_rows = lax.dynamic_slice_in_dim(w_out, chip * cols, cols, axis=0)
+        hid_all, q, k, v, qh_hat, kh_hat, att_t, lse, att_tok, d_att, dwo, cos_a, sin_a, inv_all = front(
+            hidden, gy, pos_f, w_cat, w_rows, gains_h, rope_rows(), n_chip)
         hid_all = hid_all.reshape(n_chip * rows, dim)
-        att, att_t, lse = attn_fwd(q, k, v)
+
+        def mine_of(t):
+            return lax.dynamic_slice_in_dim(t, chip * rows, rows, axis=0)
+
+        cos_t, sin_t = mine_of(cos_a), mine_of(sin_a)
+        st = lax.dynamic_index_in_dim(inv_all.reshape(2, n_chip, rows), chip, 1, keepdims=False)
+        hidden, _ = lax.optimization_barrier((hidden, inv_all))
+        q_raw, k_raw = mm32(hidden, w_query), mm32(hidden, w_key)
 
         def to_tokens(t):
             return exchange(t.reshape(n_chip, rows, cols))
@@ -337,15 +516,11 @@
         def flat(t):
             return jnp.moveaxis(t, 0, 1).reshape(rows, dim)
 
-        att_tok = to_tokens(att)
-        att_tok, gy_all = lax.optimization_barrier((att_tok, gy_all))
         y = (x_f + mm32(flat(att_tok), w_out)).astype(BF)
-        w_rows = lax.dynamic_slice_in_dim(w_out, chip * cols, cols, axis=0)
-        d_att = mm32_nt(gy_all, w_rows).astype(BF)
         dq, dk, dv = attn_bwd(q, k, v, d_att, att_t, lse)
         dq_tok, dk_tok, dv_tok = to_tokens(dq), to_tokens(dk), to_tokens(dv)
 
-        dwo = mm32(att_t.astype(BF), gy_all).reshape(2, loc, dim)
+        dwo = dwo.reshape(2, loc, dim)
         dwo = pick(dwo, core) + swap(pick(dwo, 1 - core))
 
         def finish_cols(part):
@@ -356,8 +531,8 @@
         dwv = finish_cols(weight_back(dv, hid_all))
         dq_raw, dk_raw, rowst = token_back(dq_tok, dk_tok, q_raw, k_raw, st, cos_t, sin_t, gains)
         row_all = spread(rowst)
-        dwq, dgq = weight_back(dq, hid_all, (qh_hat, stats, row_all, cos_a, sin_a, gains_h), 0)
-        dwk, dgk = weight_back(dk, hid_all, (kh_hat, stats, row_all, cos_a, sin_a, gains_h), 1)
+        dwq, dgq = weight_back(dq, hid_all, (qh_hat, inv_all, row_all, cos_a, sin_a, gains_h), 0)
+        dwk, dgk = weight_back(dk, hid_all, (kh_hat, inv_all, row_all, cos_a, sin_a, gains_h), 1)
         dwq, dwk = finish_cols(dwq), finish_cols(dwk)
         dg = jnp.stack([dgq[0], dgk[0]]).reshape(2, 2, loc)
         dg = jnp.moveaxis(dg, 1, 0)

time: 561 us -> 481 us (0.86)
  waiting for transfers between devices: 264 us -> 63.6 us
  Pallas kernels: 88.3 us -> 267 us
  blocking collectives: 39.4 us -> 11.9 us
  between operations: 15 us -> 1.34 us
  matrix products: 51.5 us -> 39 us
  other arithmetic: 26.5 us -> 20.3 us
    all_gather x2 -> x0, waiting for transfers between devices: 195 us -> none  [gather(): return lax.all_gather(t, 'sp', axis=0, axis_index_groups=same_core)]
    pallas_call x2 -> x1, Pallas kernels: 25.8 us -> 203 us  [front(): pl.pallas_call(front_kernel, name='front', out_shape=tuple((jax.ShapeDtyp...]
    all_to_all x1 -> x0, blocking collectives: 29.1 us -> none  [exchange(): lax.all_to_all(t, 'sp', split_axis=0, concat_axis=0, axis_index_groups=sa...]
    dot_general x4 -> x3, matrix products: 29 us -> 17.6 us  [mm32_nt(): return lax.dot_general(a, b, NT, preferred_element_type=F32)]
    all_to_all x8 -> x7, starting transfers between devices: 36.7 us -> 33.6 us  [exchange(): lax.all_to_all(t, 'sp', split_axis=0, concat_axis=0, axis_index_groups=sa...]
    all_to_all x8 -> x7, waiting for transfers between devices: 65.1 us -> 62.2 us  [exchange(): lax.all_to_all(t, 'sp', split_axis=0, concat_axis=0, axis_index_groups=sa...]
    dot_general x4 -> x3, matrix products: 22.6 us -> 21.4 us  [mm32(): return jnp.dot(a, b, preferred_element_type=F32)]
  transfers between devices with their start and end apart: 20 -> 17, of which waited for: 10 -> 7; matrix products, arithmetic and copies ran while one was open for 17% -> 18% of each run, Pallas kernels for 12% -> 9%
where the time goes in v2:
time: 481 us; the launch traced here: 474 us
  Pallas kernels  267 us (56%)
  waiting for transfers between devices  63.6 us (13%)
  matrix products  39 us (8%)
  starting transfers between devices  36.1 us (8%)
  local copies, waits for them, and re-layouts  35.4 us (7%)
  other arithmetic  20.3 us (4%)
  blocking collectives  11.9 us (2%)
    pallas_call x1, Pallas kernels, front(): pl.pallas_call(front_kernel, name='front', out_shape=tuple((jax.ShapeDtyp...  203 us
    all_to_all x7, waiting for transfers between devices, exchange(): lax.all_to_all(t, 'sp', split_axis=0, concat_axis=0, axis_index_groups=sa...  62.2 us
    all_to_all x7, starting transfers between devices, exchange(): lax.all_to_all(t, 'sp', split_axis=0, concat_axis=0, axis_index_groups=sa...  33.6 us
    pallas_call x2, Pallas kernels, weight_back(): pl.pallas_call(functools.partial(dw_qk_kernel, idx=idx), grid=(n_chip,),...  25.8 us
    pallas_call x1, Pallas kernels, attn_bwd(): pl.pallas_call(functools.partial(attn_bwd_kernel, blk=BWD_BLOCK, heads=he...  21.5 us
    dot_general x3, matrix products, mm32(): return jnp.dot(a, b, preferred_element_type=F32)  21.4 us
    dot_general x3, matrix products, mm32_nt(): return lax.dot_general(a, b, NT, preferred_element_type=F32)  17.6 us
    all_to_all x1, blocking collectives, device_step(): lax.all_to_all(dgn, 'sp', split_axis=0, concat_axis=0)  11.9 us
  transfers between devices with their start and end apart: 17, of which 7 were waited for; matrix products, arithmetic and copies ran while one was open for 18% of the time, Pallas kernels for 9%

profile of v2, /device:TPU:0, one launch (start us, length us, event | category | flops | bytes accessed | tf_op | source)
XLA Modules:
  0.0 474.5 jit_solution(16644090078295848371)
XLA Ops:
  0.7 2.2 dynamic-slice_bitcast_fusion.7
  3.4 0.9 dynamic-slice_bitcast_fusion.8
  4.9 1.3 constant_dynamic-slice_fusion.10
  6.2 1.3 constant_dynamic-slice_fusion.11
  7.5 1.3 constant_dynamic-slice_fusion.9
  8.8 2.3 constant_dynamic-slice_fusion.8.wrow_ref
  11.8 1.7 pad_maximum_fusion.w_ref
  13.5 0.6 pad_maximum_fusion.2.f_ref
  14.5 1.2 maximum_select_fusion.1.gy_ref
  15.8 1.5 fusion.5.h_ref
  17.3 0.6 broadcast_in_dim.4.pos_ref
  17.9 203.4 %front.1 = (bf16[8,256,2048]{2,1,0:T(8,128)(2,1)}, bf16[2048,256]{1,0:T(8,128)(2,1)}, bf16[2048,256]{1,0:T(8,128)(2,1)}, bf16[2048,256]{1,0:T(8,128)(2,1)}, f32[...) custom-call(bf16[256,2048]{1,0:T(8,128)(2,1)} %fusion.5.h_ref, ...), custom_call_target="tpu_custom_call" | custom-call | flops 429496729600 | bytes 167772160 | tf_op jit(solution)/shard_map/front/pallas_call | solution.py:405
  221.3 21.5 %attn_bwd.1 = (bf16[2048,256]{1,0:T(8,128)(2,1)}, bf16[2048,256]{1,0:T(8,128)(2,1)}, bf16[2048,256]{1,0:T(8,128)(2,1)}) custom-call(bf16[2048,256]{1,0:T(8,128)(2,1)} %get-tuple-element.35.q_ref, bf16[2048,256]{1,0:T(8,128)(2,1)} %get-tuple-element.36.k_ref, bf16[2048,256]{1,0:T(8,128)(2,1)} %get-tuple-element.37.v_ref, ...), custom_call_target="tpu_custom_call" | custom-call | flops 12884901888 | bytes 10485760 | tf_op jit(solution)/shard_map/attn_bwd/pallas_call | solution.py:374
  242.8 9.4 %all-to-all-start.1 = ((bf16[8,256,256]{2,1,0:T(8,128)(2,1)}), bf16[8,256,256]{2,1,0:T(8,128)(2,1)S(1)}, u32[]{:S(2)}, u32[]{:S(2)}) async-start(bf16[8,256,256]{2,1,0:T(8,128)(2,1)} %bitcast.81), calls=%async_computation.1 | async-start | bytes 2097152 | tf_op jit(solution)/shard_map/all_to_all | solution.py:457
  252.2 1.3 copy.42
  253.5 24.3 %all-to-all-done.1.dq_ref = bf16[8,256,256]{2,1,0:T(8,128)(2,1)S(1)} async-done(((bf16[8,256,256]{2,1,0:T(8,128)(2,1)}), bf16[8,256,256]{2,1,0:T(8,128)(2,1)S(1)}, u32[]{:S(2)}, u32[]{:S(2)}) %all-to-all-start.1) | async-done | bytes 1048608 | tf_op jit(solution)/shard_map/all_to_all | solution.py:457
  277.8 3.6 all-to-all-start
  281.4 0.7 constant_dynamic-slice_fusion.5
  282.1 0.6 copy.53
  282.7 7.0 %fusion.17.qr_ref = f32[256,2048]{1,0:T(8,128)} fusion(bf16[256,2048]{1,0:T(8,128)(2,1)S(1)} %copy-done.13, bf16[2048,2048]{1,0:T(8,128)(2,1)} %param.14), kind=kOutput, calls=%fused_computation.66 | convolution fusion | flops 2147483648 | bytes 11534336 | tf_op jit(solution)/shard_map/dot_general | solution.py:384
  289.7 17.2 %all-to-all-done = bf16[8,256,256]{1,2,0:T(8,128)(2,1)S(1)} async-done(((bf16[8,256,256]{1,2,0:T(8,128)(2,1)}), bf16[8,256,256]{1,2,0:T(8,128)(2,1)S(1)}, u32[]{:S(2)}, u32[]{:S(2)}) %all-to-all-start) | async-done | bytes 1048608 | tf_op jit(solution)/shard_map/all_to_all | solution.py:457
  307.0 3.6 all-to-all-start.2
  310.5 9.7 %dw_v.1 = f32[8,2,128,256]{3,2,1,0:T(8,128)} custom-call(bf16[2048,256]{1,0:T(8,128)(2,1)} %get-tuple-element.41.d_ref, bf16[2048,2048]{1,0:T(8,128)(2,1)} %bitcast.78), custom_call_target="tpu_custom_call" | custom-call | flops 2147483648 | bytes 10485760 | tf_op jit(solution)/shard_map/dw_v/pallas_call | solution.py:438
  320.2 2.4 dynamic-slice_bitcast_fusion.1
  322.6 1.7 constant_dynamic-slice_fusion.3
  324.3 7.2 %fusion.18.kr_ref = f32[256,2048]{1,0:T(8,128)} fusion(bf16[256,2048]{1,0:T(8,128)(2,1)S(1)} %copy-done.13, bf16[2048,2048]{1,0:T(8,128)(2,1)} %param.15), kind=kOutput, calls=%fused_computation.67 | convolution fusion | flops 2147483648 | bytes 11534336 | tf_op jit(solution)/shard_map/dot_general | solution.py:384
  331.5 3.7 fusion.16
  335.3 0.8 all-to-all-done.2.dk_ref
  336.1 1.0 copy-done.7
  337.1 6.4 %tok_back.1 = (bf16[256,2048]{1,0:T(8,128)(2,1)}, bf16[256,2048]{1,0:T(8,128)(2,1)}, f32[2,256]{1,0:T(2,128)}) custom-call(bf16[8,256,256]{2,1,0:T(8,128)(2,1)} %copy-done.6, bf16[8,256,256]{2,1,0:T(8,128)(2,1)} %copy-done.7, f32[256,2048]{1,0:T(8,128)} %fusion.17.qr_ref, f32[256,2048]{1,0:T(8,128)} %fusion.18.kr_ref, f32[2,256]{1,0:T(2,128)} %bitcast.99, ...), custom_call_target="tpu_custom_call" | custom-call | flops 104857600 | bytes 8388608 | tf_op jit(solution)/shard_map/tok_back/pallas_call | solution.py:420
  343.5 6.2 %convolution_add_fusion.1 = f32[256,2048]{1,0:T(8,128)S(1)} fusion(f32[256,2048]{1,0:T(8,128)S(1)} %copy-done.29, bf16[256,2048]{1,0:T(8,128)(2,1)} %get-tuple-element.48, bf16[2048,2048]{1,0:T(8,128)(2,1)} %param.14), kind=kOutput, calls=%fused_computation.9 | convolution fusion | flops 2148007936 | bytes 13631488 | tf_op jit(solution)/shard_map/dot_general | solution.py:388
  349.8 7.7 %fusion.11 = (f32[2048]{0:T(1024)S(1)}, f32[256]{0:T(256)S(1)}, f32[256,2048]{1,0:T(8,128)}) fusion(f32[256]{0:T(256)S(1)} %copy-done.21, bf16[128,2048]{1,0:T(8,128)(2,1)S(1)} %copy-done.1, bf16[128,2048]{1,0:T(8,128)(2,1)S(1)} %copy-done.4, pred[]{:T(512)S(6)} %eq.5, f32[2048]{0:T(1024)S(1)} %copy-done.19, f32[256,2048]{1,0:T(8,128)S(1)} %convolution_add_fusion.1, ...), kind=kOutput, calls=%fused_computation.17 | convolution fusion | flops 2156394240 | bytes 14698497 | tf_op jit(solution)/shard_map/dot_general | solution.py:388
  357.4 11.9 %all_to_all.44 = f32[16,1,128]{2,1,0:T(1,128)S(1)} all-to-all(f32[16,1,128]{2,1,0:T(1,128)S(1)} %bitcast.100), channel_id=1, replica_groups=mesh['dp'=2,'sp'=16] {'sp'}, dimensions={0} | all-to-all | bytes 16384 | tf_op jit(solution)/shard_map/all_to_all | solution.py:546
  369.3 0.6 broadcast_in_dim.5
  369.9 3.3 all-to-all-start.4
  373.3 2.3 bitcast_add_fusion.1
  375.6 3.9 all-to-all-done.4.row_ref
  379.6 3.6 all-to-all-start.7
  383.1 12.9 %dw_qk.3 = (f32[8,2,128,256]{3,2,1,0:T(8,128)}, f32[8,256]{1,0:T(8,128)}) custom-call(bf16[2048,256]{1,0:T(8,128)(2,1)} %get-tuple-element.43.d_ref, f32[2048,256]{1,0:T(8,128)} %get-tuple-element.54.hat_ref, f32[16,256]{1,0:T(8,128)} %get-tuple-element.44.st_ref, f32[8,2,256]{2,1,0:T(2,128)} %copy-done.16, f32[2048,128]{1,0:T(8,128)} %get-tuple-element.46.c_ref, ...), custom_call_target="tpu_custom_call" | custom-call | flops 2147483648 | bytes 10485760 | tf_op jit(solution)/shard_map/dw_qk/pallas_call | solution.py:439
  396.0 1.3 dynamic-slice_bitcast_fusion.2
  397.4 2.3 copy.41
  399.7 7.2 %fusion.4 = bf16[256,2048]{1,0:T(8,128)(2,1)} fusion(bf16[256,2048]{0,1:T(8,128)(2,1)} %bitcast.92, bf16[2048,2048]{1,0:T(8,128)(2,1)} %param.17, bf16[128,2048]{1,0:T(8,128)(2,1)S(1)} %copy-done.1, bf16[128,2048]{1,0:T(8,128)(2,1)S(1)} %copy-done.4, pred[]{:T(512)S(6)} %eq.5), kind=kOutput, calls=%fused_computation.10 | convolution fusion | flops 2153775104 | bytes 11534337 | tf_op jit(solution)/shard_map/dot_general | solution.py:384
  406.9 2.3 bitcast_add_fusion.2
  409.3 5.9 %all-to-all-start.6 = ((f32[8,128,256]{2,1,0:T(8,128)}), f32[8,128,256]{2,1,0:T(8,128)}, u32[]{:S(2)}, u32[]{:S(2)}) async-start(f32[8,128,256]{2,1,0:T(8,128)} %bitcast_add_fusion.2), calls=%async_computation.6 | async-start | bytes 2097152 | tf_op jit(solution)/shard_map/all_to_all | solution.py:457
  415.2 12.9 %dw_qk.2 = (f32[8,2,128,256]{3,2,1,0:T(8,128)}, f32[8,256]{1,0:T(8,128)}) custom-call(bf16[2048,256]{1,0:T(8,128)(2,1)} %get-tuple-element.42.d_ref, f32[2048,256]{1,0:T(8,128)} %get-tuple-element.50.hat_ref, f32[16,256]{1,0:T(8,128)} %get-tuple-element.44.st_ref, f32[8,2,256]{2,1,0:T(2,128)} %copy-done.16, f32[2048,128]{1,0:T(8,128)} %get-tuple-element.46.c_ref, ...), custom_call_target="tpu_custom_call" | custom-call | flops 2147483648 | bytes 10485760 | tf_op jit(solution)/shard_map/dw_qk/pallas_call | solution.py:439
  428.1 1.5 dynamic-slice_bitcast_fusion.3
  430.3 1.0 dynamic-slice_bitcast_fusion
  431.5 1.5 collective-permute-done.3
  433.0 1.1 maximum_select_fusion.2
  434.1 1.1 bitcast_add_fusion.3
  435.2 6.4 %all-to-all-done.6 = f32[8,128,256]{2,1,0:T(8,128)} async-done(((f32[8,128,256]{2,1,0:T(8,128)}), f32[8,128,256]{2,1,0:T(8,128)}, u32[]{:S(2)}, u32[]{:S(2)}) %all-to-all-start.6) | async-done | bytes 1048608 | tf_op jit(solution)/shard_map/all_to_all | solution.py:457
  441.7 4.3 all-to-all-start.5
  446.0 2.4 fusion.10
  448.4 1.0 constant_dynamic-slice_fusion.2
  449.4 0.7 slice.13
  450.1 0.7 slice.12
  451.4 2.3 bitcast_add_fusion
  454.8 2.7 maximum_select_fusion.3
  457.8 1.3 copy.50
  459.1 1.6 copy.46
  460.6 1.3 copy.49
  462.0 9.4 %all-to-all-done.5 = f32[8,128,256]{2,1,0:T(8,128)} async-done(((f32[8,128,256]{2,1,0:T(8,128)}), f32[8,128,256]{2,1,0:T(8,128)}, u32[]{:S(2)}, u32[]{:S(2)}) %all-to-all-start.5) | async-done | bytes 1048608 | tf_op jit(solution)/shard_map/all_to_all | solution.py:457
  471.4 1.6 copy.45
  472.9 1.3 copy.48
  (104 shorter events, 5.3 us)
Async XLA Ops:
  0.6 2.7 copy-start.14
  0.7 3.6 copy-start.26
  2.9 11.7 %collective-permute-start.1 = (bf16[128,2048]{1,0:T(8,128)(2,1)}, bf16[128,2048]{1,0:T(8,128)(2,1)S(1)}, u32[]{:S(2)}, u32[]{:S(2)}) collective-permute-start(bf16[128,2048]{1,0:T(8,128)(2,1)} %get-tuple-element.93), channel_id=1, source_target_pairs={{0,1},{1,0},{2,3},{3,2},{4,5},{5,4},{6,7},{7,6},{8,9},{9,8},{10,11... | collective-permute-start | bytes 1572872 | tf_op jit(solution)/shard_map/ppermute | solution.py:454
  4.3 11.5 %copy-start = (bf16[128,2048]{1,0:T(8,128)(2,1)}, bf16[128,2048]{1,0:T(8,128)(2,1)S(1)}, u32[]{:S(2)}) copy-start(bf16[128,2048]{1,0:T(8,128)(2,1)S(1)} %get-tuple-element.95) | copy-start | bytes 1572868
  4.3 9.9 %collective-permute-start = (bf16[128,2048]{1,0:T(8,128)(2,1)}, bf16[128,2048]{1,0:T(8,128)(2,1)S(1)}, u32[]{:S(2)}, u32[]{:S(2)}) collective-permute-start(bf16[128,2048]{1,0:T(8,128)(2,1)} %get-tuple-element.94), channel_id=1, source_target_pairs={{0,1},{1,0},{2,3},{3,2},{4,5},{5,4},{6,7},{7,6},{8,9},{9,8},{10,11... | collective-permute-start | bytes 1572872 | tf_op jit(solution)/shard_map/ppermute | solution.py:454
  4.3 9.8 %collective-permute-start.2 = (s32[128]{0:T(128)S(1)}, s32[128]{0:T(128)S(1)}, u32[]{:S(2)}, u32[]{:S(2)}) collective-permute-start(s32[128]{0:T(128)S(1)} %get-tuple-element.101), channel_id=1, source_target_pairs={{0,1},{1,0},{2,3},{3,2},{4,5},{5,4},{6,7},{7,6},{8,9},{9,8},{10,11... | collective-permute-start | bytes 1544 | tf_op jit(solution)/shard_map/ppermute | solution.py:454
  7.5 3.6 copy-start.22
  7.5 3.6 copy-start.23
  11.2 2.3 copy-start.17
  11.8 1.7 copy-start.27
  11.8 2.3 copy-start.24
  14.1 3.2 copy-start.18
  14.1 3.1 copy-start.3
  14.5 2.8 copy-start.20
  242.8 9.4 %copy-start.8 = (bf16[2048,256]{1,0:T(8,128)(2,1)S(1)}, bf16[2048,256]{1,0:T(8,128)(2,1)}, u32[]{:S(2)}) copy-start(bf16[2048,256]{1,0:T(8,128)(2,1)} %get-tuple-element.41.d_ref) | copy-start | bytes 3145732
  242.8 35.0 %all-to-all-start.1 = ((bf16[8,256,256]{2,1,0:T(8,128)(2,1)}), bf16[8,256,256]{2,1,0:T(8,128)(2,1)S(1)}, u32[]{:S(2)}, u32[]{:S(2)}) async-start(bf16[8,256,256]{2,1,0:T(8,128)(2,1)} %bitcast.81), calls=%async_computation.1 | async-start | bytes 2097152 | tf_op jit(solution)/shard_map/all_to_all | solution.py:457
  252.2 30.5 %copy-start.13 = (bf16[256,2048]{1,0:T(8,128)(2,1)S(1)}, bf16[256,2048]{1,0:T(8,128)(2,1)}, u32[]{:S(2)}) copy-start(bf16[256,2048]{1,0:T(8,128)(2,1)} %fusion.5.h_ref) | copy-start | bytes 3145732
  277.8 11.9 %copy-start.6 = (bf16[8,256,256]{2,1,0:T(8,128)(2,1)}, bf16[8,256,256]{2,1,0:T(8,128)(2,1)S(1)}, u32[]{:S(2)}) copy-start(bf16[8,256,256]{2,1,0:T(8,128)(2,1)S(1)} %all-to-all-done.1.dq_ref) | copy-start | bytes 3145732
  277.8 29.2 %all-to-all-start = ((bf16[8,256,256]{1,2,0:T(8,128)(2,1)}), bf16[8,256,256]{1,2,0:T(8,128)(2,1)S(1)}, u32[]{:S(2)}, u32[]{:S(2)}) async-start(bf16[8,256,256]{1,2,0:T(8,128)(2,1)} %copy.42), calls=%async_computation | async-start | bytes 2097152 | tf_op jit(solution)/shard_map/all_to_all | solution.py:457
  307.0 29.1 %all-to-all-start.2 = ((bf16[8,256,256]{2,1,0:T(8,128)(2,1)}), bf16[8,256,256]{2,1,0:T(8,128)(2,1)S(1)}, u32[]{:S(2)}, u32[]{:S(2)}) async-start(bf16[8,256,256]{2,1,0:T(8,128)(2,1)} %bitcast.16), calls=%async_computation.2 | async-start | bytes 2097152 | tf_op jit(solution)/shard_map/all_to_all | solution.py:457
  320.2 11.3 %slice-start = ((s8[8388608]{0:T(1024)(128)(4,1)}), s8[4194304]{0:T(1024)(128)(4,1)S(1)}, s32[]{:S(2)}) async-start(s8[8388608]{0:T(1024)(128)(4,1)} %bitcast.95), calls=%async_computation.8 | async-start | bytes 8388608
  322.6 50.6 %collective-permute-start.7 = (f32[8,128,256]{2,1,0:T(8,128)}, f32[8,128,256]{2,1,0:T(8,128)}, u32[]{:S(2)}, u32[]{:S(2)}) collective-permute-start(f32[8,128,256]{2,1,0:T(8,128)} %dynamic-slice_bitcast_fusion.1), channel_id=1, source_target_pairs={{0,1},{1,0},{2,3},{3,2},{4,5},{5,4},{6,7},{7,6},{8,9},{9,8},{10,11... | collective-permute-start | bytes 3145736 | tf_op jit(solution)/shard_map/ppermute | solution.py:454
  324.3 7.2 %slice-start.1 = ((s8[8388608]{0:T(1024)(128)(4,1)}), s8[4194304]{0:T(1024)(128)(4,1)S(1)}, s32[]{:S(2)}) async-start(s8[8388608]{0:T(1024)(128)(4,1)} %bitcast.95), calls=%async_computation.9 | async-start | bytes 8388608
  336.1 1.0 copy-start.7
  337.1 6.4 %copy-start.29 = (f32[256,2048]{1,0:T(8,128)S(1)}, f32[256,2048]{1,0:T(8,128)}, u32[]{:S(2)}) copy-start(f32[256,2048]{1,0:T(8,128)} %fusion.16) | copy-start | bytes 6291460
  343.5 6.3 %copy-start.1 = (bf16[128,2048]{1,0:T(8,128)(2,1)S(1)}, bf16[128,2048]{1,0:T(8,128)(2,1)}, u32[]{:S(2)}) copy-start(bf16[128,2048]{1,0:T(8,128)(2,1)} %copy-done) | copy-start | bytes 1572868
  343.5 6.3 %copy-start.4 = (bf16[128,2048]{1,0:T(8,128)(2,1)S(1)}, bf16[128,2048]{1,0:T(8,128)(2,1)}, u32[]{:S(2)}) copy-start(bf16[128,2048]{1,0:T(8,128)(2,1)} %copy-done.3) | copy-start | bytes 1572868
  343.5 6.3 %copy-start.19 = (f32[2048]{0:T(1024)S(1)}, f32[2048]{0:T(1024)}, u32[]{:S(2)}) copy-start(f32[2048]{0:T(1024)} %copy-done.18) | copy-start | bytes 24580
  343.5 6.3 %copy-start.21 = (f32[256]{0:T(256)S(1)}, f32[256]{0:T(256)}, u32[]{:S(2)}) copy-start(f32[256]{0:T(256)} %copy-done.20) | copy-start | bytes 3076
  343.5 6.3 %copy-start.28 = (bf16[256,2048]{1,0:T(8,128)(2,1)S(1)}, bf16[256,2048]{1,0:T(8,128)(2,1)}, u32[]{:S(2)}) copy-start(bf16[256,2048]{1,0:T(8,128)(2,1)} %get-tuple-element.49) | copy-start | bytes 3145732
  349.8 19.6 %copy-start.25 = (f32[2,256]{1,0:T(2,128)S(1)}, f32[2,256]{1,0:T(2,128)}, u32[]{:S(2)}) copy-start(f32[2,256]{1,0:T(2,128)} %get-tuple-element.51) | copy-start | bytes 6148
  349.8 23.5 %copy-start.2 = (f32[8,2,128,256]{3,2,1,0:T(8,128)S(1)}, f32[8,2,128,256]{3,2,1,0:T(8,128)}, u32[]{:S(2)}) copy-start(f32[8,2,128,256]{3,2,1,0:T(8,128)} %dw_v.1) | copy-start | bytes 6291460
  369.9 9.6 %all-to-all-start.4 = ((f32[8,2,256]{2,1,0:T(2,128)}), f32[8,2,256]{2,1,0:T(2,128)S(1)}, u32[]{:S(2)}, u32[]{:S(2)}) async-start(f32[8,2,256]{2,1,0:T(2,128)} %broadcast_in_dim.5), calls=%async_computation.4 | async-start | bytes 32768 | tf_op jit(solution)/shard_map/all_to_all | solution.py:457
  379.6 3.6 copy-start.16
  379.6 29.7 %all-to-all-start.7 = ((f32[8,128,256]{2,1,0:T(8,128)}), f32[8,128,256]{2,1,0:T(8,128)S(1)}, u32[]{:S(2)}, u32[]{:S(2)}) async-start(f32[8,128,256]{2,1,0:T(8,128)} %bitcast_add_fusion.1), calls=%async_computation.7 | async-start | bytes 2097152 | tf_op jit(solution)/shard_map/all_to_all | solution.py:457
  397.4 9.6 %collective-permute-start.6 = (f32[8,128,256]{2,1,0:T(8,128)S(1)}, f32[8,128,256]{2,1,0:T(8,128)}, u32[]{:S(2)}, u32[]{:S(2)}) collective-permute-start(f32[8,128,256]{2,1,0:T(8,128)S(1)} %dynamic-slice_bitcast_fusion.2), channel_id=1, source_target_pairs={{0,1},{1,0},{2,3},{3,2},{4,5},{5,4},{6,7},{7,6},{8,9},{9,8},{10,11... | collective-permute-start | bytes 3145736 | tf_op jit(solution)/shard_map/ppermute | solution.py:454
  399.7 7.2 %copy-start.12 = (f32[8,2,128,256]{3,2,1,0:T(8,128)S(1)}, f32[8,2,128,256]{3,2,1,0:T(8,128)}, u32[]{:S(2)}) copy-start(f32[8,2,128,256]{3,2,1,0:T(8,128)} %get-tuple-element.55) | copy-start | bytes 6291460
  409.3 32.4 %all-to-all-start.6 = ((f32[8,128,256]{2,1,0:T(8,128)}), f32[8,128,256]{2,1,0:T(8,128)}, u32[]{:S(2)}, u32[]{:S(2)}) async-start(f32[8,128,256]{2,1,0:T(8,128)} %bitcast_add_fusion.2), calls=%async_computation.6 | async-start | bytes 2097152 | tf_op jit(solution)/shard_map/all_to_all | solution.py:457
  428.0 1.7 copy-start.15
  428.0 2.2 copy-start.9
  429.5 4.6 collective-permute-start.5
  429.9 3.1 collective-permute-start.3
  430.3 3.9 copy-start.11
  431.3 20.1 %collective-permute-start.8 = (f32[128,2048]{1,0:T(8,128)}, f32[128,2048]{1,0:T(8,128)}, u32[]{:S(2)}, u32[]{:S(2)}) collective-permute-start(f32[128,2048]{1,0:T(8,128)} %dynamic-slice_bitcast_fusion), channel_id=1, source_target_pairs={{0,1},{1,0},{2,3},{3,2},{4,5},{5,4},{6,7},{7,6},{8,9},{9,8},{10,11... | collective-permute-start | bytes 3145736 | tf_op jit(solution)/shard_map/ppermute | solution.py:454
  434.1 11.8 %copy-start.5 = (bf16[256,2048]{1,0:T(8,128)(2,1)S(1)}, bf16[256,2048]{1,0:T(8,128)(2,1)}, u32[]{:S(2)}) copy-start(bf16[256,2048]{1,0:T(8,128)(2,1)} %maximum_select_fusion.1.gy_ref) | copy-start | bytes 3145732
  441.7 29.7 %all-to-all-start.5 = ((f32[8,128,256]{2,1,0:T(8,128)}), f32[8,128,256]{2,1,0:T(8,128)}, u32[]{:S(2)}, u32[]{:S(2)}) async-start(f32[8,128,256]{2,1,0:T(8,128)} %bitcast_add_fusion.3), calls=%async_computation.5 | async-start | bytes 2097152 | tf_op jit(solution)/shard_map/all_to_all | solution.py:457
  448.3 3.1 copy-start.10
  449.4 5.4 %collective-permute-start.4 = (bf16[128,2048]{1,0:T(8,128)(2,1)}, bf16[128,2048]{1,0:T(8,128)(2,1)}, u32[]{:S(2)}, u32[]{:S(2)}) collective-permute-start(bf16[128,2048]{1,0:T(8,128)(2,1)} %get-tuple-element.89), channel_id=1, source_target_pairs={{0,1},{1,0},{2,3},{3,2},{4,5},{5,4},{6,7},{7,6},{8,9},{9,8},{10,11... | collective-permute-start | bytes 1572872 | tf_op jit(solution)/shard_map/ppermute | solution.py:454
  450.8 3.4 collective-permute-start.9

commit v3 on v2

v3 whole, which is shorter than its diff:
```python
import functools
import jax
import jax.numpy as jnp
from jax import lax
from jax.experimental import pallas as pl
from jax.experimental.pallas import tpu as pltpu
from jax.sharding import PartitionSpec as P

HEAD_DIM = 128
NORM_EPS = 1e-5
ROPE_BASE = 10000.0
NEG_BIG = -1e30
LOG2E = 1.4426950408889634
FWD_BLOCK = 512
CHUNKS = 4
BWD_BLOCK = 512
F32, BF = jnp.float32, jnp.bfloat16
NT = (((1,), (1,)), ((), ()))


def rope_rows():
    half = HEAD_DIM // 2
    inv_freq = ROPE_BASE ** (-jnp.arange(half, dtype=F32) * (2.0 / HEAD_DIM))
    sign = jnp.concatenate([-jnp.ones(half, F32), jnp.ones(half, F32)])
    return jnp.stack([jnp.concatenate([inv_freq, inv_freq]), sign])


def column(row):
    return jnp.broadcast_to(row, (HEAD_DIM, row.shape[1])).T


def as_row(col):
    return jnp.broadcast_to(col, (col.shape[0], HEAD_DIM)).T[0:1, :]


def half_roll(u):
    return pltpu.roll(u, HEAD_DIM // 2, 1)


def front_kernel(h_ref, gy_ref, wq_ref, wk_ref, pos_ref, w_ref, wrow_ref, g_ref, f_ref,
                 hall_ref, q_ref, k_ref, v_ref, qh_ref, kh_ref, ot_ref, lse_ref, atok_ref, datt_ref, dwo_ref, c_ref, s_ref, inv_ref, qr_ref, kr_ref,
                 buf, att_ref, vt_ref, pos_all, ssq, ssq_all, wbuf,
                 w_sem, load_sem, out_sem, ssem, rsem, ps_sem, pr_sem, qs_sem, qr_sem, as_sem, ar_sem):
    me = lax.axis_index('sp')
    chip, core = me // 2, lax.rem(me, 2)
    n_chip, rows, dim = hall_ref.shape
    cols = q_ref.shape[1]
    part = rows // CHUNKS
    half = n_chip // 2
    heads = [slice(lo, lo + HEAD_DIM) for lo in range(0, cols, HEAD_DIM)]

    def spot(p):
        z, y = p // 2, lax.rem(p, 2)
        return z + y * (n_chip - 1 - 2 * z)

    def chip_at(r):
        y = r // half
        return 2 * (r + y * (n_chip - 1 - 2 * r)) + y

    ring = spot(chip)

    def slot_at(dr, dist):
        step = dist if dr == 0 else -dist
        return chip_at(lax.rem(ring - step + 2 * n_chip, n_chip))

    def dev(p):
        return {'sp': 2 * p + core}

    right = dev(slot_at(1, 1))
    left = dev(slot_at(0, 1))

    def hop(t, dr, s, c, dist):
        view = buf.at[t, slot_at(dr, dist), pl.ds(c * part, part)]
        return pltpu.make_async_remote_copy(
            src_ref=view, dst_ref=view, send_sem=ssem.at[t, dr, s, c], recv_sem=rsem.at[t, dr, s, c],
            device_id=right if dr == 0 else left, device_id_type=pl.DeviceIdType.MESH)

    def in_half(dr, c):
        return (c < CHUNKS // 2) == (dr == 0)

    def start_own(t):
        for c in range(CHUNKS):
            for dr in range(2):
                hop(t, dr, 0, c, 0).start()

    def stage(t, s):
        for c in range(CHUNKS):
            for dr in range(2):
                hop(t, dr, s, c, s + 1).wait_recv()
                if in_half(dr, c):
                    hop(t, dr, s + 1, c, s + 1).start()
                else:
                    @pl.when(s < half - 2)
                    def _():
                        hop(t, dr, s + 1, c, s + 1).start()

    def last_stage(t):
        for c in range(CHUNKS):
            for dr in range(2):
                if in_half(dr, c):
                    hop(t, dr, half - 1, c, half).wait_recv()

    def drain(t):
        for s in range(half):
            for c in range(CHUNKS):
                for dr in range(2):
                    if s < half - 1 or in_half(dr, c):
                        hop(t, dr, s, c, s).wait_send()

    def to_peers(src, dst, s_sem, r_sem):
        def make(p, owner):
            return pltpu.make_async_remote_copy(
                src_ref=src, dst_ref=dst.at[owner], send_sem=s_sem.at[p], recv_sem=r_sem.at[owner],
                device_id=dev(p), device_id_type=pl.DeviceIdType.MESH)
        return make

    def each_peer(fn):
        for p in range(n_chip):
            @pl.when(p != chip)
            def _():
                fn(p)

    loads = [pltpu.make_async_copy(src, buf.at[t, chip], load_sem.at[t]) for t, src in enumerate((h_ref, gy_ref))]
    for ld in loads:
        ld.start()
    barrier = pltpu.get_barrier_semaphore()
    each_peer(lambda p: pl.semaphore_signal(barrier, inc=1, device_id=dev(p), device_id_type=pl.DeviceIdType.MESH))
    pl.semaphore_wait(barrier, n_chip - 1)
    pos_copy = to_peers(pos_ref, pos_all, ps_sem, pr_sem)
    each_peer(lambda p: pos_copy(p, chip).start())
    pos_all[chip] = pos_ref[...]
    loads[0].wait()
    start_own(0)

    def project(p):
        ts = pl.ds(pl.multiple_of(p * rows, rows), rows)
        h = buf[0, p]
        for idx, out in enumerate((qh_ref, kh_ref)):
            raw = mm32(h, w_ref[:, idx * cols:(idx + 1) * cols])
            out[ts, :] = raw
            ssq[pl.ds(idx * n_chip + p, 1), :] = as_row(jnp.sum(raw * raw, axis=1, keepdims=True))
        v_ref[ts, :] = mm32(h, w_ref[:, 2 * cols:]).astype(BF)

    project(chip)
    each_peer(lambda p: pos_copy(p, p).wait_recv())
    for p in range(n_chip):
        angles = column(pos_all[p, 0:1, :]) * f_ref[0:1, :]
        c_ref[p * rows:(p + 1) * rows, :] = jnp.cos(angles)
        s_ref[p * rows:(p + 1) * rows, :] = jnp.sin(angles) * f_ref[1:2, :]

    def gather_step(s, _):
        stage(0, s)

        def both(dr, _):
            dist = (s + 1) * (1 - 2 * dr)
            project(chip_at(lax.rem(ring - dist + 2 * n_chip, n_chip)))
            return 0

        lax.fori_loop(0, 2, both, 0)
        return 0

    lax.fori_loop(0, half - 1, gather_step, 0)
    loads[1].wait()
    start_own(1)
    last_stage(0)
    project(slot_at(0, half))
    hall_copy = pltpu.make_async_copy(buf.at[0], hall_ref, out_sem)
    hall_copy.start()
    for hs in heads:
        vt_ref[hs, :] = v_ref[:, hs].T
    ssq_copy = to_peers(ssq, ssq_all, qs_sem, qr_sem)
    each_peer(lambda p: ssq_copy(p, chip).start())
    ssq_all[chip] = ssq[...]
    each_peer(lambda p: ssq_copy(p, p).wait_recv())
    total = ssq_all[0]
    for p in range(1, n_chip):
        total = total + ssq_all[p]
    inv_ref[...] = lax.rsqrt(total / dim + NORM_EPS)

    def finish_qk(p, _):
        ts = pl.ds(pl.multiple_of(p * rows, rows), rows)
        for idx, (hat_ref, out) in enumerate(((qh_ref, q_ref), (kh_ref, k_ref))):
            inv = column(inv_ref[pl.ds(idx * n_chip + p, 1), :])
            for hs in heads:
                hat = hat_ref[ts, hs] * inv
                hat_ref[ts, hs] = hat
                u = hat * g_ref[idx:idx + 1, hs]
                out[ts, hs] = (u * c_ref[ts, :] + half_roll(u) * s_ref[ts, :]).astype(BF)
        return 0

    lax.fori_loop(0, n_chip, finish_qk, 0)

    blk = FWD_BLOCK
    scale = HEAD_DIM ** -0.5 * LOG2E
    causal = lax.broadcasted_iota(jnp.int32, (blk, blk), 0) <= lax.broadcasted_iota(jnp.int32, (blk, blk), 1)

    def attend(j, _):
        qs = pl.ds(pl.multiple_of(j * blk, blk), blk)
        qb = [q_ref[qs, hs] for hs in heads]

        def tile(i, carry, diag):
            ks = pl.ds(pl.multiple_of(i * blk, blk), blk)
            out = []
            for h, hs in enumerate(heads):
                m, l, acc = carry[h]
                s = mm32_nt(k_ref[ks, hs], qb[h])
                if diag:
                    s = jnp.where(causal, s, NEG_BIG)
                mn = jnp.maximum(m, jnp.max(s, axis=0, keepdims=True))
                al = jnp.exp2((m - mn) * scale)
                p = jnp.exp2((s - mn) * scale)
                l = al * l + jnp.sum(p, axis=0, keepdims=True)
                out.append((mn, l, al * acc + mm32(vt_ref[hs, ks], p.astype(BF))))
            return tuple(out)

        st = tuple((jnp.full((1, blk), NEG_BIG, F32), jnp.zeros((1, blk), F32), jnp.zeros((HEAD_DIM, blk), F32)) for _ in heads)
        st = lax.fori_loop(0, j, lambda i, cr: tile(i, cr, False), st)
        st = tile(j, st, True)
        for h, hs in enumerate(heads):
            m, l, acc = st[h]
            ot = acc / l
            ot_ref[hs, qs] = ot
            att_ref[qs, hs] = ot.T.astype(BF)
            lse_ref[h:h + 1, qs] = m * scale + jnp.log2(l)
        return 0

    def att_copy(p, owner):
        return pltpu.make_async_remote_copy(
            src_ref=att_ref.at[pl.ds(p * rows, rows)], dst_ref=atok_ref.at[:, pl.ds(pl.multiple_of(owner * cols, cols), cols)], send_sem=as_sem.at[p], recv_sem=ar_sem.at[owner],
            device_id=dev(p), device_id_type=pl.DeviceIdType.MESH)

    def send_att(lo, hi):
        for p in range(lo, hi):
            @pl.when(p != chip)
            def _():
                att_copy(p, chip).start()

    def use_gy(p):
        ts = pl.ds(pl.multiple_of(p * rows, rows), rows)
        gy = buf[1, p]
        datt_ref[ts, :] = mm32_nt(gy, wrow_ref[...]).astype(BF)
        dwo_ref[...] += mm32(ot_ref[:, ts].astype(BF), gy)

    n_att = n_chip * rows // blk
    lax.fori_loop(0, n_att // 2, attend, 0)
    stage(1, 0)
    send_att(0, half)
    lax.fori_loop(n_att // 2, n_att, attend, 0)

    def raw_of(w, out):
        def load(m, slot):
            return pltpu.make_async_copy(w.at[:, pl.ds(pl.multiple_of(m * cols, cols), cols)], wbuf.at[slot], w_sem.at[slot])

        load(0, 0).start()

        def step(m, _):
            slot = lax.rem(m, 2)
            load(m, slot).wait()

            @pl.when(m + 1 < n_chip)
            def _():
                load(m + 1, 1 - slot).start()
            out[:, pl.ds(pl.multiple_of(m * cols, cols), cols)] = mm32(buf[0, chip], wbuf[slot])
            return 0

        lax.fori_loop(0, n_chip, step, 0)

    raw_of(wq_ref, qr_ref)
    raw_of(wk_ref, kr_ref)
    stage(1, 1)
    send_att(half, n_chip)
    atok_ref[:, pl.ds(pl.multiple_of(chip * cols, cols), cols)] = att_ref[pl.ds(pl.multiple_of(chip * rows, rows), rows), :]
    dwo_ref[...] = jnp.zeros_like(dwo_ref)

    def use_ring(n, _):
        dist = ((n + 1) // 2) * (2 * lax.rem(n, 2) - 1)
        use_gy(chip_at(lax.rem(ring - dist + 2 * n_chip, n_chip)))
        return 0

    lax.fori_loop(0, n_chip - 3, use_ring, 0)
    stage(1, half - 2)
    lax.fori_loop(n_chip - 3, n_chip - 1, use_ring, 0)
    last_stage(1)
    use_gy(slot_at(0, half))

    each_peer(lambda p: att_copy(p, p).wait_recv())
    each_peer(lambda p: att_copy(p, chip).wait_send())
    each_peer(lambda p: pos_copy(p, chip).wait_send())
    each_peer(lambda p: ssq_copy(p, chip).wait_send())
    drain(0)
    drain(1)
    hall_copy.wait()


def back_kernel(q_ref, k_ref, v_ref, do_ref, ot_ref, lse_ref, g_ref, gt_ref, inv_ref,
                hall_ref, qh_hbm, kh_hbm, c_hbm, s_hbm, qr_hbm, kr_hbm, wq_ref, wk_ref, wv_ref, dwo_ref,
                dwq_ref, dwk_ref, dwv_ref, dwo_out, dhid_ref, dg_ref,
                dq_ref, dk_ref, dv_ref, dka_ref, dva_ref, kt_ref, qh_ref, kh_ref, c_ref, s_ref, qr_ref, kr_ref,
                tok, pairs, pair_in, dt_ref, hblk, wblk, dwo_in, row_ref, row_all,
                load_sem, h_sem, w_sem, xs_sem, xr_sem, ps_sem, pr_sem, rs_sem, rr_sem, own_sem, do_sem):
    me = lax.axis_index('sp')
    chip, core = me // 2, lax.rem(me, 2)
    n, cols = q_ref.shape
    rows, dim = qr_ref.shape
    n_chip = n // rows
    partner = {'sp': me + 1 - 2 * core}
    heads = [slice(lo, lo + HEAD_DIM) for lo in range(0, cols, HEAD_DIM)]
    own_rows = pl.ds(pl.multiple_of(chip * rows, rows), rows)
    own_cols = pl.ds(pl.multiple_of(chip * cols, cols), cols)
    MESH = pl.DeviceIdType.MESH

    def dev(p):
        return {'sp': 2 * p + core}

    def each_peer(fn):
        for p in range(n_chip):
            @pl.when(p != chip)
            def _():
                fn(p)

    sides = ((qh_hbm, qh_ref), (kh_hbm, kh_ref), (c_hbm, c_ref), (s_hbm, s_ref), (qr_hbm, qr_ref), (kr_hbm, kr_ref), (dwo_ref.at[core], dwo_out))
    loads = [pltpu.make_async_copy(src, dst, load_sem.at[i]) for i, (src, dst) in enumerate(sides)]
    for ld in loads:
        ld.start()

    def load_h(p, slot):
        return pltpu.make_async_copy(hall_ref.at[:, pl.ds(pl.multiple_of(p * cols, cols), cols)], hblk.at[slot], h_sem.at[slot])

    load_h(0, 0).start()
    barrier = pltpu.get_barrier_semaphore()
    each_peer(lambda p: pl.semaphore_signal(barrier, inc=1, device_id=dev(p), device_id_type=MESH))
    pl.semaphore_signal(barrier, inc=1, device_id=partner, device_id_type=MESH)
    pl.semaphore_wait(barrier, n_chip)

    dwo_copy = pltpu.make_async_remote_copy(
        src_ref=dwo_ref.at[1 - core], dst_ref=dwo_in, send_sem=do_sem.at[0], recv_sem=do_sem.at[1], device_id=partner, device_id_type=MESH)
    dwo_copy.start()

    def tok_copy(t, p, owner):
        src = (dq_ref, dk_ref, dv_ref)[t].at[pl.ds(pl.multiple_of(p * rows, rows), rows)]
        dst = tok.at[t, :, pl.ds(pl.multiple_of(owner * cols, cols), cols)]
        return pltpu.make_async_remote_copy(src_ref=src, dst_ref=dst, send_sem=xs_sem.at[t, p], recv_sem=xr_sem.at[t, owner], device_id=dev(p), device_id_type=MESH)

    blk = BWD_BLOCK
    span = blk // rows
    n_blk = n // blk
    sc = HEAD_DIM ** -0.5
    scale = sc * LOG2E
    for hs in heads:
        kt_ref[hs, :] = k_ref[:, hs].T
    dka_ref[...] = jnp.zeros_like(dka_ref)
    dva_ref[...] = jnp.zeros_like(dva_ref)
    causal = lax.broadcasted_iota(jnp.int32, (blk, blk), 0) <= lax.broadcasted_iota(jnp.int32, (blk, blk), 1)

    def send_dq(j):
        for u in range(span):
            p = j * span + u

            @pl.when(p != chip)
            def _():
                tok_copy(0, p, chip).start()

    def q_step(j, _):
        qs = pl.ds(pl.multiple_of(j * blk, blk), blk)
        qb = [q_ref[qs, hs] for hs in heads]
        dob = [do_ref[qs, hs] for hs in heads]
        lse = [lse_ref[h:h + 1, qs] for h in range(len(heads))]
        dl = [jnp.sum(ot_ref[hs, qs] * dob[h].astype(F32).T, axis=0, keepdims=True) for h, hs in enumerate(heads)]

        def tile(i, carry, diag):
            ks = pl.ds(pl.multiple_of(i * blk, blk), blk)
            out = []
            for h, hs in enumerate(heads):
                s = mm32_nt(k_ref[ks, hs], qb[h])
                dp = mm32_nt(v_ref[ks, hs], dob[h])
                p = jnp.exp2(s * scale - lse[h])
                if diag:
                    p = jnp.where(causal, p, 0.0)
                ds = (p * (dp - dl[h])).astype(BF)
                dva_ref[ks, hs] += mm32(p.astype(BF), dob[h])
                dka_ref[ks, hs] += mm32(ds, qb[h])
                out.append(carry[h] + mm32(kt_ref[hs, ks], ds))
            return tuple(out)

        st = tuple(jnp.zeros((HEAD_DIM, blk), F32) for _ in heads)
        st = lax.fori_loop(0, j, lambda i, cr: tile(i, cr, False), st)
        st = tile(j, st, True)
        for h, hs in enumerate(heads):
            dq_ref[qs, hs] = (st[h] * sc).T.astype(BF)

        @pl.when(j > 0)
        def _():
            send_dq(j - 1)
        return 0

    lax.fori_loop(0, n_blk, q_step, 0)
    dk_ref[...] = (dka_ref[...] * sc).astype(BF)
    dv_ref[...] = dva_ref[...].astype(BF)
    send_dq(n_blk - 1)
    for t, src in enumerate((dq_ref, dk_ref, dv_ref)):
        tok[t, :, own_cols] = src[own_rows, :]
    for t in (1, 2):
        each_peer(lambda p: tok_copy(t, p, chip).start())

    def pair_copy(w, p):
        return pltpu.make_async_remote_copy(
            src_ref=pairs.at[w, p, 1 - core], dst_ref=pair_in.at[w, p], send_sem=ps_sem.at[w, p], recv_sem=pr_sem.at[w, p], device_id=partner, device_id_type=MESH)

    grads = (dwq_ref, dwk_ref, dwv_ref)

    def dw_copy(w, p, owner):
        dst = grads[w].at[:, pl.ds(pl.multiple_of(owner * cols, cols), cols)]
        return pltpu.make_async_remote_copy(src_ref=pairs.at[w, p, core], dst_ref=dst, send_sem=xs_sem.at[3 + w, p], recv_sem=xr_sem.at[3 + w, owner], device_id=dev(p), device_id_type=MESH)

    def own_copy(w):
        return pltpu.make_async_copy(pairs.at[w, chip, core], grads[w].at[:, own_cols], own_sem.at[w])

    def partial(w, slot_t, h, p):
        dw = mm32(dt_ref[slot_t], h).T
        pairs[w, p, 0] = dw[:rows // 2]
        pairs[w, p, 1] = dw[rows // 2:]

    def merge(w, p):
        pair_copy(w, p).wait_recv()
        pairs[w, p, core] += pair_in[w, p]

    def send_dw(w, p):
        @pl.when(p != chip)
        def _():
            dw_copy(w, p, chip).start()

        @pl.when(p == chip)
        def _():
            own_copy(w).start()

    def each_h(ws, tail_fn):
        def step(p, _):
            slot = lax.rem(p, 2)
            load_h(p, slot).wait()

            @pl.when(p + 1 < n_chip)
            def _():
                load_h(p + 1, 1 - slot).start()
            for w, slot_t in ws:
                partial(w, slot_t, hblk[slot], p)
            tail_fn(p)
            for w, _ in ws:
                pair_copy(w, p).start()
            return 0

        lax.fori_loop(0, n_chip, step, 0)

    dt_ref[0] = dv_ref[...].T
    each_h(((2, 0),), lambda p: None)
    load_h(0, 0).start()
    for ld in loads:
        ld.wait()

    hats = ((qr_ref, 0), (kr_ref, 1))
    row_ref[...] = jnp.zeros_like(row_ref)
    inv_t = [column(inv_ref[pl.ds(idx * n_chip + chip, 1), :]) for idx in range(2)]
    c_t, s_t = c_ref[own_rows, :], s_ref[own_rows, :]

    def normed(idx, hs):
        d = tok[idx, :, hs].astype(F32)
        return (d * c_t - half_roll(d) * s_t) * gt_ref[idx:idx + 1, hs]

    row_cols = []
    for raw_ref, idx in hats:
        each_peer(lambda p: tok_copy(idx, p, p).wait_recv())
        acc = jnp.zeros((rows, HEAD_DIM), F32)
        for lo in range(0, dim, HEAD_DIM):
            hs = slice(lo, lo + HEAD_DIM)
            acc += normed(idx, hs) * (raw_ref[:, hs] * inv_t[idx])
        row = jnp.sum(acc, axis=1, keepdims=True) / dim
        row_ref[idx:idx + 1, :] = as_row(row)
        row_cols.append(row)

    def row_copy(p, owner):
        return pltpu.make_async_remote_copy(src_ref=row_ref, dst_ref=row_all.at[owner], send_sem=rs_sem.at[p], recv_sem=rr_sem.at[owner], device_id=dev(p), device_id_type=MESH)

    for raw_ref, idx in hats:
        for lo in range(0, dim, HEAD_DIM):
            hs = slice(lo, lo + HEAD_DIM)
            tok[idx, :, hs] = (inv_t[idx] * (normed(idx, hs) - raw_ref[:, hs] * inv_t[idx] * row_cols[idx])).astype(BF)
        if idx == 0:
            each_peer(lambda p: row_copy(p, chip).start())
            row_all[chip] = row_ref[...]

    def merge_v(p, _):
        merge(2, p)
        return 0

    def send_v(p, _):
        send_dw(2, p)
        return 0

    lax.fori_loop(0, n_chip, merge_v, 0)

    def load_w(m, slot):
        return [pltpu.make_async_copy(w.at[pl.ds(pl.multiple_of(m * cols, cols), cols)], wblk.at[slot, i], w_sem.at[slot, i]) for i, w in enumerate((wq_ref, wk_ref, wv_ref))]

    for ld in load_w(0, 0):
        ld.start()
    lax.fori_loop(0, n_chip, send_v, 0)
    each_peer(lambda p: row_copy(p, p).wait_recv())

    dg_ref[...] = jnp.zeros_like(dg_ref)

    def head_step(p, _):
        ts = pl.ds(pl.multiple_of(p * rows, rows), rows)
        for idx, (d_ref, hat_ref) in enumerate(((dq_ref, qh_ref), (dk_ref, kh_ref))):
            inv = column(inv_ref[pl.ds(idx * n_chip + p, 1), :])
            row = column(row_all[p, idx:idx + 1, :])
            for hs in heads:
                d = d_ref[ts, hs].astype(F32)
                rot = d * c_ref[ts, :] - half_roll(d) * s_ref[ts, :]
                hat = hat_ref[ts, hs]
                raw = inv * (rot * g_ref[idx:idx + 1, hs] - hat * row)
                dt_ref[idx, hs, ts] = raw.astype(BF).T
                dg_ref[idx:idx + 1, hs] += jnp.sum(rot * hat, axis=0, keepdims=True)
        return 0

    lax.fori_loop(0, n_chip, head_step, 0)

    def lagged(p):
        @pl.when(p > 0)
        def _():
            for w in range(2):
                merge(w, p - 1)

        @pl.when(p > 1)
        def _():
            for w in range(2):
                send_dw(w, p - 2)

    each_h(((0, 0), (1, 1)), lagged)
    for w in range(2):
        send_dw(w, n_chip - 2)
        merge(w, n_chip - 1)
    dwo_copy.wait_recv()
    dwo_out[...] += dwo_in[...]
    for w in range(2):
        send_dw(w, n_chip - 1)

    each_peer(lambda p: tok_copy(2, p, p).wait_recv())

    def hid_step(m, _):
        slot = lax.rem(m, 2)
        for ld in load_w(m, slot):
            ld.wait()

        @pl.when(m + 1 < n_chip)
        def _():
            for ld in load_w(m + 1, 1 - slot):
                ld.start()
        out = pl.ds(pl.multiple_of(m * cols, cols), cols)
        dhid_ref[:, out] = mm32_nt(tok[0], wblk[slot, 0]) + mm32_nt(tok[1], wblk[slot, 1]) + mm32_nt(tok[2], wblk[slot, 2])
        return 0

    lax.fori_loop(0, n_chip, hid_step, 0)

    for w in range(3):
        each_peer(lambda p: dw_copy(w, p, p).wait_recv())
        each_peer(lambda p: dw_copy(w, p, chip).wait_send())
        each_peer(lambda p: tok_copy(w, p, chip).wait_send())
        own_copy(w).wait()
        for p in range(n_chip):
            pair_copy(w, p).wait_send()
    each_peer(lambda p: row_copy(p, chip).wait_send())
    dwo_copy.wait_send()


VM = pl.BlockSpec(memory_space=pltpu.VMEM)


def mm32(a, b):
    return jnp.dot(a, b, preferred_element_type=F32)


def mm32_nt(a, b):
    return lax.dot_general(a, b, NT, preferred_element_type=F32)


def front(hid, gy, w_query, w_key, pos, w_cat, w_rows, gains, freq, n_chip):
    rows, dim = hid.shape
    cols = w_rows.shape[0]
    n = n_chip * rows
    heads = cols // HEAD_DIM
    any_spec = pl.BlockSpec(memory_space=pl.ANY)
    half = n_chip // 2
    dma = pltpu.SemaphoreType.DMA
    outs = [((n_chip, rows, dim), BF), ((n, cols), BF), ((n, cols), BF), ((n, cols), BF), ((n, cols), F32), ((n, cols), F32), ((cols, n), F32), ((heads, n), F32),
            ((rows, dim), BF), ((n, cols), BF), ((cols, dim), F32), ((n, HEAD_DIM), F32), ((n, HEAD_DIM), F32), ((2 * n_chip, rows), F32), ((rows, dim), F32), ((rows, dim), F32)]
    return pl.pallas_call(
        front_kernel, name='front', out_shape=tuple(jax.ShapeDtypeStruct(s, d) for s, d in outs),
        in_specs=[any_spec] * 4 + [VM] * 5, out_specs=(any_spec,) + (VM,) * 15,
        scratch_shapes=[
            pltpu.VMEM((2, n_chip, rows, dim), BF), pltpu.VMEM((n, cols), BF), pltpu.VMEM((cols, n), BF),
            pltpu.VMEM((n_chip, 8, rows), F32), pltpu.VMEM((2 * n_chip, rows), F32), pltpu.VMEM((n_chip, 2 * n_chip, rows), F32), pltpu.VMEM((2, dim, cols), BF),
            dma((2,)), dma((2,)), dma(()), dma((2, 2, half, CHUNKS)), dma((2, 2, half, CHUNKS)),
            dma((n_chip,)), dma((n_chip,)), dma((n_chip,)), dma((n_chip,)), dma((n_chip,)), dma((n_chip,))],
        compiler_params=pltpu.CompilerParams(collective_id=0, has_side_effects=True, vmem_limit_bytes=67043328),
        cost_estimate=pl.CostEstimate(flops=400 * n * dim * cols, bytes_accessed=40 * n * dim, transcendentals=n * n * heads // 2),
    )(hid, gy, w_query, w_key, pos, w_cat, w_rows, gains, freq)


def back(q, k, v, d_att, att_t, lse, gains_h, gains, inv, hid, qh, kh, cos_a, sin_a, q_raw, k_raw, w_query, w_key, w_value, dwo):
    n, cols = q.shape
    rows, dim = q_raw.shape
    n_chip = n // rows
    any_spec = pl.BlockSpec(memory_space=pl.ANY)
    dma = pltpu.SemaphoreType.DMA
    grad = jax.ShapeDtypeStruct((rows // 2, dim), F32)
    vmem = pltpu.VMEM
    return pl.pallas_call(
        back_kernel, name='back', in_specs=[VM] * 9 + [any_spec] * 11, out_specs=(any_spec,) * 3 + (VM,) * 3,
        out_shape=(grad,) * 4 + (jax.ShapeDtypeStruct((rows, dim), F32), jax.ShapeDtypeStruct((8, cols), F32)),
        scratch_shapes=[
            vmem((n, cols), BF), vmem((n, cols), BF), vmem((n, cols), BF), vmem((n, cols), F32), vmem((n, cols), F32), vmem((cols, n), BF),
            vmem((n, cols), F32), vmem((n, cols), F32), vmem((n, HEAD_DIM), F32), vmem((n, HEAD_DIM), F32), vmem((rows, dim), F32), vmem((rows, dim), F32),
            vmem((3, rows, dim), BF), vmem((3, n_chip, 2, rows // 2, cols), F32), vmem((3, n_chip, rows // 2, cols), F32),
            vmem((2, cols, n), BF), vmem((2, n, cols), BF), vmem((2, 3, cols, dim), BF), vmem((rows // 2, dim), F32),
            vmem((8, rows), F32), vmem((n_chip, 8, rows), F32),
            dma((7,)), dma((2,)), dma((2, 3)), dma((6, n_chip)), dma((6, n_chip)), dma((3, n_chip)), dma((3, n_chip)),
            dma((n_chip,)), dma((n_chip,)), dma((3,)), dma((2,))],
        compiler_params=pltpu.CompilerParams(collective_id=1, has_side_effects=True, vmem_limit_bytes=67043328),
        cost_estimate=pl.CostEstimate(flops=400 * n * dim * cols, bytes_accessed=40 * n * dim, transcendentals=n * n),
    )(q, k, v, d_att, att_t, lse, gains_h, gains, inv, hid, qh, kh, cos_a, sin_a, q_raw, k_raw, w_query, w_key, w_value, dwo)


def solution(mesh):
    n_sp = mesh.shape['sp']
    n_chip = n_sp // 2
    pairs = [(i, i ^ 1) for i in range(n_sp)]

    def swap(t):
        return lax.ppermute(t, 'sp', pairs)

    def device_step(x_loc, gy_loc, positions, g_norm, w_query, w_key, w_value, w_out, g_query, g_key):
        me = lax.axis_index('sp')
        chip, core = me // 2, me % 2
        first = core == 0
        loc, dim = x_loc.shape[1], x_loc.shape[2]
        rows = 2 * loc
        cols = dim // n_chip

        def pick(t, idx):
            return lax.dynamic_index_in_dim(t, idx, 0, keepdims=False)

        def join(mine, other):
            return jnp.where(first, jnp.concatenate([mine, other], 0), jnp.concatenate([other, mine], 0))

        def to_core(t):
            return join(pick(t, core), swap(pick(t, 1 - core)))

        def from_core(t):
            halves = t.reshape(2, loc, dim)
            mine, other = pick(halves, core), swap(pick(halves, 1 - core))
            return jnp.where(first, jnp.stack([mine, other]), jnp.stack([other, mine]))

        def my_cols(w):
            return lax.dynamic_slice_in_dim(w, chip * cols, cols, axis=1)

        def inv_of(raw):
            return lax.rsqrt(jnp.mean(raw * raw, axis=-1, keepdims=True) + NORM_EPS)

        x_f = to_core(x_loc).astype(F32)
        gy = to_core(gy_loc)
        pos = to_core(positions)
        x_inv = inv_of(x_f)
        x_hat = x_f * x_inv
        hidden = (x_hat * g_norm.astype(F32)).astype(BF)
        pos_f = jnp.broadcast_to(pos.astype(F32)[None], (8, rows))
        gains = jnp.stack([g_query, g_key]).astype(F32)
        gains_h = lax.dynamic_slice_in_dim(gains, chip * cols, cols, axis=1)
        w_cat = jnp.concatenate([my_cols(w_query), my_cols(w_key), my_cols(w_value)], 1)
        w_rows = lax.dynamic_slice_in_dim(w_out, chip * cols, cols, axis=0)
        hid_all, q, k, v, qh_hat, kh_hat, att_t, lse, att_tok, d_att, dwo, cos_a, sin_a, inv_all, q_raw, k_raw = front(
            hidden, gy, w_query, w_key, pos_f, w_cat, w_rows, gains_h, rope_rows(), n_chip)
        dwq, dwk, dwv, dwo, d_hid, dg = back(
            q, k, v, d_att, att_t, lse, gains_h, gains, inv_all, hid_all.reshape(n_chip * rows, dim), qh_hat, kh_hat, cos_a, sin_a,
            q_raw, k_raw, w_query, w_key, w_value, dwo.reshape(2, loc, dim))
        y = (x_f + mm32(att_tok, w_out)).astype(BF)
        dg = jnp.moveaxis(dg[:2].reshape(2, 2, loc), 1, 0)
        dg = pick(dg, core) + swap(pick(dg, 1 - core))

        d_nrm = d_hid * g_norm.astype(F32)
        dxn = x_inv * (d_nrm - x_hat * jnp.mean(d_nrm * x_hat, axis=-1, keepdims=True))
        grad_x = (gy.astype(F32) + dxn).astype(BF)
        dgn = jnp.sum(d_hid * x_hat, axis=0).reshape(n_sp, loc)
        dgn = jnp.sum(lax.all_to_all(dgn, 'sp', split_axis=0, concat_axis=0), axis=0)
        return from_core(y), from_core(grad_x), dgn, dwq, dwk, dwv, dwo, dg[0], dg[1]

    seq_spec = P('dp', 'sp', None)
    mat_rep = P(None, None)
    vec_rep = P(None)
    row_spec = P(('dp', 'sp'), None)
    vec_spec = P(('dp', 'sp'))
    return jax.shard_map(device_step, mesh=mesh, in_specs=(seq_spec, seq_spec, P('dp', 'sp'), vec_rep, mat_rep, mat_rep, mat_rep, mat_rep, vec_rep, vec_rep), out_specs=(seq_spec, seq_spec, vec_spec, row_spec, row_spec, row_spec, row_spec, vec_spec, vec_spec), check_vma=False)
```

time: 481 us -> 435 us (0.904); the launches traced: 474 us -> 434 us
  Pallas kernels: 267 us -> 364 us
  waiting for transfers between devices: 63.6 us -> 5.8 us
  matrix products: 39 us -> 6.66 us
  local copies, waits for them, and re-layouts: 35.4 us -> 16 us
  blocking collectives: 11.9 us -> 0 us
  starting transfers between devices: 36.1 us -> 24.3 us
  other arithmetic: 20.3 us -> 15.4 us
    pallas_call x5 -> x1, Pallas kernels: 63.3 us -> 160 us  [back(): pl.pallas_call(back_kernel, name='back', in_specs=[VM] * 9 + [any_spec] *...]
    all_to_all x7 -> x1, waiting for transfers between devices: 62.2 us -> 5.79 us  [device_step(): lax.all_to_all(dgn, 'sp', split_axis=0, concat_axis=0)]
    dot_general x3 -> x0, matrix products: 17.6 us -> none  [mm32_nt(): return lax.dot_general(a, b, NT, preferred_element_type=F32)]
    dot_general x3 -> x1, matrix products: 21.4 us -> 6.66 us  [mm32(): return jnp.dot(a, b, preferred_element_type=F32)]
    all_to_all x1 -> x0, blocking collectives: 11.9 us -> none  [device_step(): lax.all_to_all(dgn, 'sp', split_axis=0, concat_axis=0)]
    all_to_all x7 -> x1, starting transfers between devices: 33.6 us -> 22.6 us  [device_step(): lax.all_to_all(dgn, 'sp', split_axis=0, concat_axis=0)]
    add x4 -> x0, other arithmetic: 8.09 us -> none  [the longest x3 5.78 us: finish_cols(): return jnp.moveaxis(exchange(mine + swap(other)), 0, 1).reshape(loc, dim)]
    transpose x4 -> x0, local copies, waits for them, and re-layouts: 5.69 us -> none  [the longest x3 3.43 us: finish_cols(): return jnp.moveaxis(exchange(mine + swap(other)), 0, 1).reshape(loc, dim)]
  transfers between devices with their start and end apart: 17 -> 7, of which waited for: 7 -> 1; matrix products, arithmetic and copies ran while one was open for 18% -> 5% of each run, Pallas kernels for 9% -> 37%
where the time goes in v3:
time: 435 us; the launch traced here: 434 us
  Pallas kernels  364 us (84%)
  starting transfers between devices  24.3 us (6%)
  local copies, waits for them, and re-layouts  16 us (4%)
  other arithmetic  15.4 us (4%)
  matrix products  6.66 us (2%)
  waiting for transfers between devices  5.8 us (1%)
    pallas_call x1, Pallas kernels, front(): pl.pallas_call(front_kernel, name='front', out_shape=tuple((jax.ShapeDtyp...  205 us
    pallas_call x1, Pallas kernels, back(): pl.pallas_call(back_kernel, name='back', in_specs=[VM] * 9 + [any_spec] *...  160 us
    all_to_all x1, starting transfers between devices, device_step(): lax.all_to_all(dgn, 'sp', split_axis=0, concat_axis=0)  22.6 us
  transfers between devices with their start and end apart: 7, of which 1 were waited for; matrix products, arithmetic and copies ran while one was open for 5% of the time, Pallas kernels for 37%

profile of v3, /device:TPU:0, one launch (start us, length us, event | category | flops | bytes accessed | tf_op | source)
XLA Modules:
  0.0 433.6 jit_solution(2394293763317534043)
XLA Ops:
  0.6 0.0 copy-start.10
  0.7 0.8 fusion.14
  1.5 0.6 collective-permute-start.2
  2.0 2.1 dynamic-slice_bitcast_fusion.4
  4.1 0.0 collective-permute-start
  4.2 0.0 copy-done.10
  4.2 0.1 dynamic-slice_bitcast_fusion.3
  4.3 0.6 collective-permute-start.1
  4.8 0.1 maximum_bitcast_fusion
  4.9 0.0 copy-done.16
  4.9 0.0 copy-done.17
  5.0 0.0 copy-start.13
  5.0 0.5 constant_dynamic-slice_fusion.4.g_ref
  5.5 2.3 constant_dynamic-slice_fusion.5.wrow_ref
  7.8 1.3 constant_dynamic-slice_fusion.8
  9.1 0.0 copy-done.13
  9.2 1.7 constant_dynamic-slice_fusion.6
  10.9 0.0 copy-start.19
  10.9 0.0 copy-start.18
  10.9 1.8 pad_maximum_fusion.w_ref
  12.7 0.0 copy-done.19
  12.7 0.5 pad_maximum_fusion.1.f_ref
  13.2 0.0 copy-done.18
  13.2 0.0 collective-permute-done.2
  13.3 0.0 collective-permute-done
  13.3 0.0 copy-start.3
  13.3 0.4 fusion.12
  13.7 0.0 copy-done
  13.7 0.0 copy-start.14
  13.7 1.5 fusion.5.h_ref
  15.2 0.0 collective-permute-done.1
  15.2 1.2 maximum_select_fusion.1.gy_ref
  16.4 0.0 copy-done.11
  16.4 0.0 copy-done.3
  16.4 0.0 copy-done.14
  16.4 0.6 broadcast_in_dim.2.pos_ref
  17.0 204.7 %front.1 = (bf16[8,256,2048]{2,1,0:T(8,128)(2,1)}, bf16[2048,256]{1,0:T(8,128)(2,1)}, bf16[2048,256]{1,0:T(8,128)(2,1)}, bf16[2048,256]{1,0:T(8,128)(2,1)}, f32[...) custom-call(bf16[256,2048]{1,0:T(8,128)(2,1)} %fusion.5.h_ref, ...), custom_call_target="tpu_custom_call" | custom-call | flops 429496729600 | bytes 167772160 | tf_op jit(solution)/shard_map/front/pallas_call | solution.py:595
  221.7 6.7 %fusion.4 = bf16[256,2048]{1,0:T(8,128)(2,1)S(1)} fusion(bf16[256,2048]{1,0:T(8,128)(2,1)} %get-tuple-element.31, bf16[2048,2048]{1,0:T(8,128)(2,1)} %param.17, bf16[128,2048]{1,0:T(8,128)(2,1)} %copy-done, bf16[128,2048]{1,0:T(8,128)(2,1)} %copy-done.3, pred[]{:T(512)S(6)} %eq.5), kind=kOutput, calls=%fused_computation.8 | convolution fusion | flops 2153775104 | bytes 11534337 | tf_op jit(solution)/shard_map/dot_general | solution.py:578
  228.4 1.1 constant_dynamic-slice_fusion.3
  229.5 0.0 collective-permute-start.3
  229.5 159.8 %back.1 = (f32[128,2048]{1,0:T(8,128)}, f32[128,2048]{1,0:T(8,128)}, f32[128,2048]{1,0:T(8,128)}, f32[128,2048]{1,0:T(8,128)}, f32[256,2048]{1,0:T(8,128)}, /*index=5*/f32[8,256]{1,0:T(8,128)}) custom-call(bf16[2048,256]{1,0:T(8,128)(2,1)} %get-tuple-element.32.q_ref, bf16[2048,256]{1,0:T(8,128)(2,1)} %get-tuple-element.33.k_ref, ...), custom_call_target="tpu_custom_call" | custom-call | flops 429496729600 | bytes 167772160 | tf_op jit(solution)/shard_map/back/pallas_call | solution.py:616
  389.3 0.0 copy-start.1
  389.3 0.0 copy-start.2
  389.3 0.0 copy-start.4
  389.3 0.8 slice.9
  390.2 3.7 fusion.11
  393.9 2.0 fusion.10
  396.0 0.0 copy-start.5
  396.0 0.1 constant_dynamic-slice_fusion.2
  396.1 0.1 collective-permute-start.4
  396.2 0.5 collective-permute-start.5
  396.7 22.6 %all-to-all-start = ((f32[16,1,128]{2,1,0:T(1,128)}), f32[16,1,128]{2,1,0:T(1,128)S(1)}, u32[]{:S(2)}, u32[]{:S(2)}) async-start(f32[16,1,128]{2,1,0:T(1,128)} %bitcast.15), calls=%async_computation | async-start | bytes 16384 | tf_op jit(solution)/shard_map/all_to_all | solution.py:692
  419.3 0.0 collective-permute-done.5
  419.3 0.5 slice_bitcast_fusion
  419.9 5.8 %all-to-all-done = f32[16,1,128]{2,1,0:T(1,128)S(1)} async-done(((f32[16,1,128]{2,1,0:T(1,128)}), f32[16,1,128]{2,1,0:T(1,128)S(1)}, u32[]{:S(2)}, u32[]{:S(2)}) %all-to-all-start) | async-done | bytes 8224 | tf_op jit(solution)/shard_map/all_to_all | solution.py:692
  425.6 0.5 reduce_sum.39
  426.2 0.0 collective-permute-done.3
  426.2 2.4 maximum_select_fusion.2
  428.6 0.0 collective-permute-done.4
  428.6 1.1 maximum_select_fusion.3
  429.7 1.0 copy.24
  430.7 1.0 copy.25
  431.7 1.0 copy.26
  432.7 1.0 copy.27
  (31 shorter events, 0.1 us)
Async XLA Ops:
  0.6 3.5 copy-start.10
  1.5 3.4 copy-start.16
  1.5 3.5 copy-start.17
  1.5 11.8 %collective-permute-start.2 = (s32[128]{0:T(128)S(1)}, s32[128]{0:T(128)S(1)}, u32[]{:S(2)}, u32[]{:S(2)}) collective-permute-start(s32[128]{0:T(128)S(1)} %get-tuple-element.68), channel_id=1, source_target_pairs={{0,1},{1,0},{2,3},{3,2},{4,5},{5,4},{6,7},{7,6},{8,9},{9,8},{10,11... | collective-permute-start | bytes 1544 | tf_op jit(solution)/shard_map/ppermute | solution.py:638
  4.1 9.5 %copy-start = (bf16[128,2048]{1,0:T(8,128)(2,1)}, bf16[128,2048]{1,0:T(8,128)(2,1)S(1)}, u32[]{:S(2)}) copy-start(bf16[128,2048]{1,0:T(8,128)(2,1)S(1)} %get-tuple-element.62) | copy-start | bytes 1572868
  4.1 9.1 %collective-permute-start = (bf16[128,2048]{1,0:T(8,128)(2,1)}, bf16[128,2048]{1,0:T(8,128)(2,1)S(1)}, u32[]{:S(2)}, u32[]{:S(2)}) collective-permute-start(bf16[128,2048]{1,0:T(8,128)(2,1)} %get-tuple-element.61), channel_id=1, source_target_pairs={{0,1},{1,0},{2,3},{3,2},{4,5},{5,4},{6,7},{7,6},{8,9},{9,8},{10,11... | collective-permute-start | bytes 1572872 | tf_op jit(solution)/shard_map/ppermute | solution.py:638
  4.3 10.9 %collective-permute-start.1 = (bf16[128,2048]{1,0:T(8,128)(2,1)S(1)}, bf16[128,2048]{1,0:T(8,128)(2,1)S(1)}, u32[]{:S(2)}, u32[]{:S(2)}) collective-permute-start(bf16[128,2048]{1,0:T(8,128)(2,1)S(1)} %get-tuple-element.60), channel_id=1, source_target_pairs={{0,1},{1,0},{2,3},{3,2},{4,5},{5,4},{6,7},{7,6},{8,9},{9,8},{10,11... | collective-permute-start | bytes 1572872 | tf_op jit(solution)/shard_map/ppermute | solution.py:638
  5.0 4.2 copy-start.13
  10.9 1.8 copy-start.19
  10.9 2.4 copy-start.18
  13.2 3.2 copy-start.11
  13.3 3.1 copy-start.3
  13.7 2.8 copy-start.14
  229.5 196.7 %collective-permute-start.3 = (bf16[128,2048]{1,0:T(8,128)(2,1)}, bf16[128,2048]{1,0:T(8,128)(2,1)}, u32[]{:S(2)}, u32[]{:S(2)}) collective-permute-start(bf16[128,2048]{1,0:T(8,128)(2,1)} %get-tuple-element.58), channel_id=1, source_target_pairs={{0,1},{1,0},{2,3},{3,2},{4,5},{5,4},{6,7},{7,6},{8,9},{9,8},{10,11... | collective-permute-start | bytes 1572872 | tf_op jit(solution)/shard_map/ppermute | solution.py:638
  389.3 4.6 %copy-start.1 = (bf16[128,2048]{1,0:T(8,128)(2,1)S(1)}, bf16[128,2048]{1,0:T(8,128)(2,1)}, u32[]{:S(2)}) copy-start(bf16[128,2048]{1,0:T(8,128)(2,1)} %copy-done) | copy-start | bytes 1572868
  389.3 4.6 %copy-start.2 = (f32[256,2048]{1,0:T(8,128)S(1)}, f32[256,2048]{1,0:T(8,128)}, u32[]{:S(2)}) copy-start(f32[256,2048]{1,0:T(8,128)} %get-tuple-element.47) | copy-start | bytes 6291460
  389.3 4.6 %copy-start.4 = (bf16[128,2048]{1,0:T(8,128)(2,1)S(1)}, bf16[128,2048]{1,0:T(8,128)(2,1)}, u32[]{:S(2)}) copy-start(bf16[128,2048]{1,0:T(8,128)(2,1)} %copy-done.3) | copy-start | bytes 1572868
  389.3 4.6 %copy-start.12 = (f32[2048]{0:T(1024)S(1)}, f32[2048]{0:T(1024)}, u32[]{:S(2)}) copy-start(f32[2048]{0:T(1024)} %copy-done.11) | copy-start | bytes 24580
  389.3 4.6 %copy-start.15 = (f32[256]{0:T(256)S(1)}, f32[256]{0:T(256)}, u32[]{:S(2)}) copy-start(f32[256]{0:T(256)} %copy-done.14) | copy-start | bytes 3076
  396.0 30.2 %copy-start.5 = (bf16[1,128,2048]{2,1,0:T(8,128)(2,1)S(1)}, bf16[1,128,2048]{2,1,0:T(8,128)(2,1)}, u32[]{:S(2)}) copy-start(bf16[1,128,2048]{2,1,0:T(8,128)(2,1)} %get-tuple-element.57) | copy-start | bytes 1572868
  396.1 32.5 %collective-permute-start.4 = (bf16[128,2048]{1,0:T(8,128)(2,1)S(1)}, bf16[128,2048]{1,0:T(8,128)(2,1)S(1)}, u32[]{:S(2)}, u32[]{:S(2)}) collective-permute-start(bf16[128,2048]{1,0:T(8,128)(2,1)S(1)} %get-tuple-element.56), channel_id=1, source_target_pairs={{0,1},{1,0},{2,3},{3,2},{4,5},{5,4},{6,7},{7,6},{8,9},{9,8},{10,11... | collective-permute-start | bytes 1572872 | tf_op jit(solution)/shard_map/ppermute | solution.py:638
  396.2 23.1 %collective-permute-start.5 = (f32[2,128]{1,0:T(2,128)S(1)}, f32[2,128]{1,0:T(2,128)S(1)}, u32[]{:S(2)}, u32[]{:S(2)}) collective-permute-start(f32[2,128]{1,0:T(2,128)S(1)} %bitcast.39), channel_id=1, source_target_pairs={{0,1},{1,0},{2,3},{3,2},{4,5},{5,4},{6,7},{7,6},{8,9},{9,8},{10,11... | collective-permute-start | bytes 3080 | tf_op jit(solution)/shard_map/ppermute | solution.py:638
  396.7 29.0 %all-to-all-start = ((f32[16,1,128]{2,1,0:T(1,128)}), f32[16,1,128]{2,1,0:T(1,128)S(1)}, u32[]{:S(2)}, u32[]{:S(2)}) async-start(f32[16,1,128]{2,1,0:T(1,128)} %bitcast.15), calls=%async_computation | async-start | bytes 16384 | tf_op jit(solution)/shard_map/all_to_all | solution.py:692
  426.2 3.6 copy-start.9
  428.6 2.1 copy-start.8
  429.7 1.9 copy-start.7
  430.7 1.9 copy-start.6

commit v4 on v3

--- a/solution.py
+++ b/solution.py
@@ -37,10 +37,10 @@
     return pltpu.roll(u, HEAD_DIM // 2, 1)
 
 
-def front_kernel(h_ref, gy_ref, wq_ref, wk_ref, pos_ref, w_ref, wrow_ref, g_ref, f_ref,
-                 hall_ref, q_ref, k_ref, v_ref, qh_ref, kh_ref, ot_ref, lse_ref, atok_ref, datt_ref, dwo_ref, c_ref, s_ref, inv_ref, qr_ref, kr_ref,
-                 buf, att_ref, vt_ref, pos_all, ssq, ssq_all, wbuf,
-                 w_sem, load_sem, out_sem, ssem, rsem, ps_sem, pr_sem, qs_sem, qr_sem, as_sem, ar_sem):
+def front_kernel(x_ref, gy_ref, wq_ref, wk_ref, wv_ref, wo_ref, pos_ref, g_ref, gt_ref, f_ref,
+                 hall_ref, q_ref, k_ref, v_ref, qh_ref, kh_ref, ot_ref, lse_ref, atok_ref, datt_ref, dwo_ref, c_ref, s_ref, inv_ref, qr_ref, kr_ref, xs_ref, gys_ref,
+                 buf, w_ref, wrow_ref, att_ref, vt_ref, pos_all, ssq, ssq_all, wbuf,
+                 w_sem, load_sem, swap_sem, out_sem, ssem, rsem, ps_sem, pr_sem, qs_sem, qr_sem, as_sem, ar_sem):
     me = lax.axis_index('sp')
     chip, core = me // 2, lax.rem(me, 2)
     n_chip, rows, dim = hall_ref.shape
@@ -120,33 +120,63 @@
             def _():
                 fn(p)
 
-    loads = [pltpu.make_async_copy(src, buf.at[t, chip], load_sem.at[t]) for t, src in enumerate((h_ref, gy_ref))]
+    partner = {'sp': me + 1 - 2 * core}
+    own_cols = pl.ds(pl.multiple_of(chip * cols, cols), cols)
+    gy_own = buf.at[1, chip, pl.ds(pl.multiple_of(core * (rows // 2), rows // 2), rows // 2)]
+    local = [(x_ref.at[core], xs_ref.at[core]), (gy_ref.at[core], gy_own)]
+    local += [(w.at[:, own_cols], w_ref.at[i]) for i, w in enumerate((wq_ref, wk_ref, wv_ref))] + [(wo_ref.at[own_cols], wrow_ref)]
+    loads = [pltpu.make_async_copy(src, dst, load_sem.at[i]) for i, (src, dst) in enumerate(local)]
     for ld in loads:
         ld.start()
     barrier = pltpu.get_barrier_semaphore()
     each_peer(lambda p: pl.semaphore_signal(barrier, inc=1, device_id=dev(p), device_id_type=pl.DeviceIdType.MESH))
-    pl.semaphore_wait(barrier, n_chip - 1)
-    pos_copy = to_peers(pos_ref, pos_all, ps_sem, pr_sem)
+    pl.semaphore_signal(barrier, inc=1, device_id=partner, device_id_type=pl.DeviceIdType.MESH)
+    pl.semaphore_wait(barrier, n_chip)
+
+    swaps = [pltpu.make_async_remote_copy(
+        src_ref=src, dst_ref=dst, send_sem=swap_sem.at[0, i], recv_sem=swap_sem.at[1, i], device_id=partner, device_id_type=pl.DeviceIdType.MESH)
+        for i, (src, dst) in enumerate(((x_ref.at[1 - core], xs_ref.at[core]), (pos_ref.at[1 - core], pos_all.at[chip, core]), (gy_ref.at[1 - core], gy_own)))]
+    for sw in swaps:
+        sw.start()
+    pos_copy = to_peers(pos_all.at[chip], pos_all, ps_sem, pr_sem)
+    pos_all[chip, core] = pos_ref[core]
+    loads[0].wait()
+    swaps[0].wait_recv()
+    for c in range(CHUNKS):
+        top = (c * part) % (rows // 2)
+        piece, ts = c * part // (rows // 2), slice(top, top + part)
+        acc = jnp.zeros((part, HEAD_DIM), F32)
+        for lo in range(0, dim, HEAD_DIM):
+            x = xs_ref[piece, ts, lo:lo + HEAD_DIM].astype(F32)
+            acc += x * x
+        inv = lax.rsqrt(jnp.sum(acc, axis=1, keepdims=True) / dim + NORM_EPS)
+        for lo in range(0, dim, HEAD_DIM):
+            hs = slice(lo, lo + HEAD_DIM)
+            x = xs_ref[piece, ts, hs].astype(F32)
+            buf[0, chip, c * part:(c + 1) * part, hs] = (x * inv * gt_ref[2:3, hs]).astype(BF)
+    swaps[1].wait_recv()
     each_peer(lambda p: pos_copy(p, chip).start())
-    pos_all[chip] = pos_ref[...]
-    loads[0].wait()
     start_own(0)
+    for ld in loads[2:]:
+        ld.wait()
 
     def project(p):
         ts = pl.ds(pl.multiple_of(p * rows, rows), rows)
         h = buf[0, p]
         for idx, out in enumerate((qh_ref, kh_ref)):
-            raw = mm32(h, w_ref[:, idx * cols:(idx + 1) * cols])
+            raw = mm32(h, w_ref[idx])
             out[ts, :] = raw
             ssq[pl.ds(idx * n_chip + p, 1), :] = as_row(jnp.sum(raw * raw, axis=1, keepdims=True))
-        v_ref[ts, :] = mm32(h, w_ref[:, 2 * cols:]).astype(BF)
+        v_ref[ts, :] = mm32(h, w_ref[2]).astype(BF)
 
     project(chip)
     each_peer(lambda p: pos_copy(p, p).wait_recv())
     for p in range(n_chip):
-        angles = column(pos_all[p, 0:1, :]) * f_ref[0:1, :]
-        c_ref[p * rows:(p + 1) * rows, :] = jnp.cos(angles)
-        s_ref[p * rows:(p + 1) * rows, :] = jnp.sin(angles) * f_ref[1:2, :]
+        for u in range(2):
+            ts = slice(p * rows + u * (rows // 2), p * rows + (u + 1) * (rows // 2))
+            angles = column(pos_all[p, u, 0:1, :]) * f_ref[0:1, :]
+            c_ref[ts, :] = jnp.cos(angles)
+            s_ref[ts, :] = jnp.sin(angles) * f_ref[1:2, :]
 
     def gather_step(s, _):
         stage(0, s)
@@ -161,10 +191,13 @@
 
     lax.fori_loop(0, half - 1, gather_step, 0)
     loads[1].wait()
+    swaps[2].wait_recv()
     start_own(1)
+    gys_copy = pltpu.make_async_copy(buf.at[1, chip], gys_ref, out_sem.at[1])
+    gys_copy.start()
     last_stage(0)
     project(slot_at(0, half))
-    hall_copy = pltpu.make_async_copy(buf.at[0], hall_ref, out_sem)
+    hall_copy = pltpu.make_async_copy(buf.at[0], hall_ref, out_sem.at[0])
     hall_copy.start()
     for hs in heads:
         vt_ref[hs, :] = v_ref[:, hs].T
@@ -287,17 +320,21 @@
     each_peer(lambda p: att_copy(p, chip).wait_send())
     each_peer(lambda p: pos_copy(p, chip).wait_send())
     each_peer(lambda p: ssq_copy(p, chip).wait_send())
+    for sw in swaps:
+        sw.wait_send()
     drain(0)
     drain(1)
     hall_copy.wait()
+    gys_copy.wait()
 
 
 def back_kernel(q_ref, k_ref, v_ref, do_ref, ot_ref, lse_ref, g_ref, gt_ref, inv_ref,
-                hall_ref, qh_hbm, kh_hbm, c_hbm, s_hbm, qr_hbm, kr_hbm, wq_ref, wk_ref, wv_ref, dwo_ref,
-                dwq_ref, dwk_ref, dwv_ref, dwo_out, dhid_ref, dg_ref,
+                hall_ref, qh_hbm, kh_hbm, c_hbm, s_hbm, qr_hbm, kr_hbm, wq_ref, wk_ref, wv_ref, dwo_ref, wo_ref, at_hbm, x_hbm, gy_hbm,
+                dwq_ref, dwk_ref, dwv_ref, y_ref, gx_ref, dwo_out, dg_out, dgn_out,
                 dq_ref, dk_ref, dv_ref, dka_ref, dva_ref, kt_ref, qh_ref, kh_ref, c_ref, s_ref, qr_ref, kr_ref,
                 tok, pairs, pair_in, dt_ref, hblk, wblk, dwo_in, row_ref, row_all,
-                load_sem, h_sem, w_sem, xs_sem, xr_sem, ps_sem, pr_sem, rs_sem, rr_sem, own_sem, do_sem):
+                dhid_ref, dg_ref, at_ref, x_ref, gy_ref, ys_ref, gxs_ref, dgp, dgp_in, gpart, gpair_in, gsel, gsel_in,
+                sw_sem, gs_sem, gr_sem, load_sem, h_sem, w_sem, xs_sem, xr_sem, ps_sem, pr_sem, rs_sem, rr_sem, own_sem, do_sem):
     me = lax.axis_index('sp')
     chip, core = me // 2, lax.rem(me, 2)
     n, cols = q_ref.shape
@@ -318,7 +355,7 @@
             def _():
                 fn(p)
 
-    sides = ((qh_hbm, qh_ref), (kh_hbm, kh_ref), (c_hbm, c_ref), (s_hbm, s_ref), (qr_hbm, qr_ref), (kr_hbm, kr_ref), (dwo_ref.at[core], dwo_out))
+    sides = ((qh_hbm, qh_ref), (kh_hbm, kh_ref), (c_hbm, c_ref), (s_hbm, s_ref), (qr_hbm, qr_ref), (kr_hbm, kr_ref), (dwo_ref.at[core], dwo_out), (at_hbm, at_ref), (x_hbm, x_ref), (gy_hbm, gy_ref))
     loads = [pltpu.make_async_copy(src, dst, load_sem.at[i]) for i, (src, dst) in enumerate(sides)]
     for ld in loads:
         ld.start()
@@ -326,7 +363,11 @@
     def load_h(p, slot):
         return pltpu.make_async_copy(hall_ref.at[:, pl.ds(pl.multiple_of(p * cols, cols), cols)], hblk.at[slot], h_sem.at[slot])
 
+    def load_o(m, slot):
+        return pltpu.make_async_copy(wo_ref.at[pl.ds(pl.multiple_of(m * cols, cols), cols)], wblk.at[slot, 0], w_sem.at[slot, 0])
+
     load_h(0, 0).start()
+    load_o(0, 0).start()
     barrier = pltpu.get_barrier_semaphore()
     each_peer(lambda p: pl.semaphore_signal(barrier, inc=1, device_id=dev(p), device_id_type=MESH))
     pl.semaphore_signal(barrier, inc=1, device_id=partner, device_id_type=MESH)
@@ -335,6 +376,16 @@
     dwo_copy = pltpu.make_async_remote_copy(
         src_ref=dwo_ref.at[1 - core], dst_ref=dwo_in, send_sem=do_sem.at[0], recv_sem=do_sem.at[1], device_id=partner, device_id_type=MESH)
     dwo_copy.start()
+
+    def to_partner(src, dst, i):
+        return pltpu.make_async_remote_copy(src_ref=src, dst_ref=dst, send_sem=sw_sem.at[0, i], recv_sem=sw_sem.at[1, i], device_id=partner, device_id_type=MESH)
+
+    y_swap = to_partner(ys_ref.at[1 - core], y_ref.at[core], 0)
+    gx_swap = to_partner(gxs_ref.at[1 - core], gx_ref.at[core], 1)
+    dg_swap = to_partner(dgp.at[1 - core], dgp_in, 2)
+    gn_swap = to_partner(gpart.at[1 - core], gpair_in, 3)
+    y_own = pltpu.make_async_copy(ys_ref.at[core], y_ref.at[core], sw_sem.at[0, 4])
+    gx_own = pltpu.make_async_copy(gxs_ref.at[core], gx_ref.at[core], sw_sem.at[1, 4])
 
     def tok_copy(t, p, owner):
         src = (dq_ref, dk_ref, dv_ref)[t].at[pl.ds(pl.multiple_of(p * rows, rows), rows)]
@@ -456,6 +507,23 @@
     for ld in loads:
         ld.wait()
 
+    dhid_ref[...] = x_ref[...].astype(F32)
+
+    def y_step(m, _):
+        slot = lax.rem(m, 2)
+        load_o(m, slot).wait()
+
+        @pl.when(m + 1 < n_chip)
+        def _():
+            load_o(m + 1, 1 - slot).start()
+        dhid_ref[...] += mm32(at_ref[:, pl.ds(pl.multiple_of(m * cols, cols), cols)], wblk[slot, 0])
+        return 0
+
+    lax.fori_loop(0, n_chip, y_step, 0)
+    half = rows // 2
+    for u in range(2):
+        ys_ref[u] = dhid_ref[u * half:(u + 1) * half, :].astype(BF)
+
     hats = ((qr_ref, 0), (kr_ref, 1))
     row_ref[...] = jnp.zeros_like(row_ref)
     inv_t = [column(inv_ref[pl.ds(idx * n_chip + chip, 1), :]) for idx in range(2)]
@@ -475,6 +543,9 @@
         row = jnp.sum(acc, axis=1, keepdims=True) / dim
         row_ref[idx:idx + 1, :] = as_row(row)
         row_cols.append(row)
+
+    y_swap.start()
+    y_own.start()
 
     def row_copy(p, owner):
         return pltpu.make_async_remote_copy(src_ref=row_ref, dst_ref=row_all.at[owner], send_sem=rs_sem.at[p], recv_sem=rr_sem.at[owner], device_id=dev(p), device_id_type=MESH)
@@ -522,6 +593,9 @@
         return 0
 
     lax.fori_loop(0, n_chip, head_step, 0)
+    dgp[...] = jnp.zeros_like(dgp)
+    for u in range(2):
+        dgp[u, 0:2, :] = dg_ref[0:2, u * half:(u + 1) * half]
 
     def lagged(p):
         @pl.when(p > 0)
@@ -542,6 +616,7 @@
     dwo_out[...] += dwo_in[...]
     for w in range(2):
         send_dw(w, n_chip - 1)
+    dg_swap.start()
 
     each_peer(lambda p: tok_copy(2, p, p).wait_recv())
 
@@ -559,6 +634,49 @@
         return 0
 
     lax.fori_loop(0, n_chip, hid_step, 0)
+
+    blocks = [slice(lo, lo + HEAD_DIM) for lo in range(0, dim, HEAD_DIM)]
+    acc = jnp.zeros((rows, HEAD_DIM), F32)
+    dot = jnp.zeros((rows, HEAD_DIM), F32)
+    for hs in blocks:
+        x = x_ref[:, hs].astype(F32)
+        acc += x * x
+        dot += x * dhid_ref[:, hs] * gt_ref[2:3, hs]
+    x_inv = lax.rsqrt(jnp.sum(acc, axis=1, keepdims=True) / dim + NORM_EPS)
+    mean = jnp.sum(dot, axis=1, keepdims=True) * x_inv / dim
+    gpart[...] = jnp.zeros_like(gpart)
+    for i, hs in enumerate(blocks):
+        x_hat = x_ref[:, hs].astype(F32) * x_inv
+        d = dhid_ref[:, hs]
+        gx = (gy_ref[:, hs].astype(F32) + x_inv * (d * gt_ref[2:3, hs] - x_hat * mean)).astype(BF)
+        gxs_ref[0, :, hs] = gx[:half]
+        gxs_ref[1, :, hs] = gx[half:]
+        gpart[i % 2, i // 2, 0:1, :] = jnp.sum(d * x_hat, axis=0, keepdims=True)
+    gn_swap.start()
+    gx_swap.start()
+    gx_own.start()
+    dg_swap.wait_recv()
+    dg_out[...] = dgp[core] + dgp_in[...]
+    gn_swap.wait_recv()
+    gsel[...] = gpart[core] + gpair_in[...]
+
+    def gn_copy(p, owner):
+        return pltpu.make_async_remote_copy(src_ref=gsel.at[p], dst_ref=gsel_in.at[owner], send_sem=gs_sem.at[p], recv_sem=gr_sem.at[owner], device_id=dev(p), device_id_type=MESH)
+
+    each_peer(lambda p: gn_copy(p, chip).start())
+    gsel_in[chip] = gsel[chip]
+    each_peer(lambda p: gn_copy(p, p).wait_recv())
+    total = gsel_in[0]
+    for p in range(1, n_chip):
+        total = total + gsel_in[p]
+    dgn_out[...] = total
+    each_peer(lambda p: gn_copy(p, chip).wait_send())
+    for sw in (y_swap, gx_swap):
+        sw.wait_recv()
+    for sw in (y_swap, gx_swap, dg_swap, gn_swap):
+        sw.wait_send()
+    y_own.wait()
+    gx_own.wait()
 
     for w in range(3):
         each_peer(lambda p: dw_copy(w, p, p).wait_recv())
@@ -582,115 +700,77 @@
     return lax.dot_general(a, b, NT, preferred_element_type=F32)
 
 
-def front(hid, gy, w_query, w_key, pos, w_cat, w_rows, gains, freq, n_chip):
-    rows, dim = hid.shape
-    cols = w_rows.shape[0]
+def front(x, gy, w_query, w_key, w_value, w_out, pos, gains_h, gains, freq, n_chip):
+    loc, dim = x.shape[1:]
+    rows = 2 * loc
+    cols = gains_h.shape[1]
     n = n_chip * rows
     heads = cols // HEAD_DIM
     any_spec = pl.BlockSpec(memory_space=pl.ANY)
     half = n_chip // 2
-    dma = pltpu.SemaphoreType.DMA
+    dma, vmem = pltpu.SemaphoreType.DMA, pltpu.VMEM
     outs = [((n_chip, rows, dim), BF), ((n, cols), BF), ((n, cols), BF), ((n, cols), BF), ((n, cols), F32), ((n, cols), F32), ((cols, n), F32), ((heads, n), F32),
-            ((rows, dim), BF), ((n, cols), BF), ((cols, dim), F32), ((n, HEAD_DIM), F32), ((n, HEAD_DIM), F32), ((2 * n_chip, rows), F32), ((rows, dim), F32), ((rows, dim), F32)]
+            ((rows, dim), BF), ((n, cols), BF), ((cols, dim), F32), ((n, HEAD_DIM), F32), ((n, HEAD_DIM), F32), ((2 * n_chip, rows), F32), ((rows, dim), F32), ((rows, dim), F32),
+            ((2, loc, dim), BF), ((rows, dim), BF)]
     return pl.pallas_call(
         front_kernel, name='front', out_shape=tuple(jax.ShapeDtypeStruct(s, d) for s, d in outs),
-        in_specs=[any_spec] * 4 + [VM] * 5, out_specs=(any_spec,) + (VM,) * 15,
+        in_specs=[any_spec] * 6 + [VM] * 4, out_specs=(any_spec,) + (VM,) * 16 + (any_spec,),
         scratch_shapes=[
-            pltpu.VMEM((2, n_chip, rows, dim), BF), pltpu.VMEM((n, cols), BF), pltpu.VMEM((cols, n), BF),
-            pltpu.VMEM((n_chip, 8, rows), F32), pltpu.VMEM((2 * n_chip, rows), F32), pltpu.VMEM((n_chip, 2 * n_chip, rows), F32), pltpu.VMEM((2, dim, cols), BF),
-            dma((2,)), dma((2,)), dma(()), dma((2, 2, half, CHUNKS)), dma((2, 2, half, CHUNKS)),
+            vmem((2, n_chip, rows, dim), BF), vmem((3, dim, cols), BF), vmem((cols, dim), BF), vmem((n, cols), BF), vmem((cols, n), BF),
+            vmem((n_chip, 2, 8, loc), F32), vmem((2 * n_chip, rows), F32), vmem((n_chip, 2 * n_chip, rows), F32), vmem((2, dim, cols), BF),
+            dma((2,)), dma((6,)), dma((2, 3)), dma((2,)), dma((2, 2, half, CHUNKS)), dma((2, 2, half, CHUNKS)),
             dma((n_chip,)), dma((n_chip,)), dma((n_chip,)), dma((n_chip,)), dma((n_chip,)), dma((n_chip,))],
         compiler_params=pltpu.CompilerParams(collective_id=0, has_side_effects=True, vmem_limit_bytes=67043328),
         cost_estimate=pl.CostEstimate(flops=400 * n * dim * cols, bytes_accessed=40 * n * dim, transcendentals=n * n * heads // 2),
-    )(hid, gy, w_query, w_key, pos, w_cat, w_rows, gains, freq)
-
-
-def back(q, k, v, d_att, att_t, lse, gains_h, gains, inv, hid, qh, kh, cos_a, sin_a, q_raw, k_raw, w_query, w_key, w_value, dwo):
+    )(x, gy, w_query, w_key, w_value, w_out, pos, gains_h, gains, freq)
+
+
+def back(q, k, v, d_att, att_t, lse, gains_h, gains, inv, hid, qh, kh, cos_a, sin_a, q_raw, k_raw, w_query, w_key, w_value, dwo, w_out, att_tok, x, gy):
     n, cols = q.shape
     rows, dim = q_raw.shape
     n_chip = n // rows
     any_spec = pl.BlockSpec(memory_space=pl.ANY)
     dma = pltpu.SemaphoreType.DMA
     grad = jax.ShapeDtypeStruct((rows // 2, dim), F32)
+    seq = jax.ShapeDtypeStruct((2, rows // 2, dim), BF)
+    small = jax.ShapeDtypeStruct((8, cols // 2), F32)
+    tile = (n_chip, 8, cols // 2)
     vmem = pltpu.VMEM
     return pl.pallas_call(
-        back_kernel, name='back', in_specs=[VM] * 9 + [any_spec] * 11, out_specs=(any_spec,) * 3 + (VM,) * 3,
-        out_shape=(grad,) * 4 + (jax.ShapeDtypeStruct((rows, dim), F32), jax.ShapeDtypeStruct((8, cols), F32)),
+        back_kernel, name='back', in_specs=[VM] * 9 + [any_spec] * 15, out_specs=(any_spec,) * 5 + (VM,) * 3,
+        out_shape=(grad,) * 3 + (seq, seq, grad, small, small),
         scratch_shapes=[
             vmem((n, cols), BF), vmem((n, cols), BF), vmem((n, cols), BF), vmem((n, cols), F32), vmem((n, cols), F32), vmem((cols, n), BF),
             vmem((n, cols), F32), vmem((n, cols), F32), vmem((n, HEAD_DIM), F32), vmem((n, HEAD_DIM), F32), vmem((rows, dim), F32), vmem((rows, dim), F32),
             vmem((3, rows, dim), BF), vmem((3, n_chip, 2, rows // 2, cols), F32), vmem((3, n_chip, rows // 2, cols), F32),
             vmem((2, cols, n), BF), vmem((2, n, cols), BF), vmem((2, 3, cols, dim), BF), vmem((rows // 2, dim), F32),
             vmem((8, rows), F32), vmem((n_chip, 8, rows), F32),
-            dma((7,)), dma((2,)), dma((2, 3)), dma((6, n_chip)), dma((6, n_chip)), dma((3, n_chip)), dma((3, n_chip)),
+            vmem((rows, dim), F32), vmem((8, cols), F32), vmem((rows, dim), BF), vmem((rows, dim), BF), vmem((rows, dim), BF), vmem((2, rows // 2, dim), BF), vmem((2, rows // 2, dim), BF),
+            vmem((2, 8, cols // 2), F32), vmem((8, cols // 2), F32), vmem((2,) + tile, F32), vmem(tile, F32), vmem(tile, F32), vmem(tile, F32),
+            dma((2, 5)), dma((n_chip,)), dma((n_chip,)), dma((10,)), dma((2,)), dma((2, 3)), dma((6, n_chip)), dma((6, n_chip)), dma((3, n_chip)), dma((3, n_chip)),
             dma((n_chip,)), dma((n_chip,)), dma((3,)), dma((2,))],
         compiler_params=pltpu.CompilerParams(collective_id=1, has_side_effects=True, vmem_limit_bytes=67043328),
         cost_estimate=pl.CostEstimate(flops=400 * n * dim * cols, bytes_accessed=40 * n * dim, transcendentals=n * n),
-    )(q, k, v, d_att, att_t, lse, gains_h, gains, inv, hid, qh, kh, cos_a, sin_a, q_raw, k_raw, w_query, w_key, w_value, dwo)
+    )(q, k, v, d_att, att_t, lse, gains_h, gains, inv, hid, qh, kh, cos_a, sin_a, q_raw, k_raw, w_query, w_key, w_value, dwo, w_out, att_tok, x, gy)
 
 
 def solution(mesh):
-    n_sp = mesh.shape['sp']
-    n_chip = n_sp // 2
-    pairs = [(i, i ^ 1) for i in range(n_sp)]
-
-    def swap(t):
-        return lax.ppermute(t, 'sp', pairs)
+    n_chip = mesh.shape['sp'] // 2
 
     def device_step(x_loc, gy_loc, positions, g_norm, w_query, w_key, w_value, w_out, g_query, g_key):
-        me = lax.axis_index('sp')
-        chip, core = me // 2, me % 2
-        first = core == 0
+        chip = lax.axis_index('sp') // 2
         loc, dim = x_loc.shape[1], x_loc.shape[2]
         rows = 2 * loc
         cols = dim // n_chip
-
-        def pick(t, idx):
-            return lax.dynamic_index_in_dim(t, idx, 0, keepdims=False)
-
-        def join(mine, other):
-            return jnp.where(first, jnp.concatenate([mine, other], 0), jnp.concatenate([other, mine], 0))
-
-        def to_core(t):
-            return join(pick(t, core), swap(pick(t, 1 - core)))
-
-        def from_core(t):
-            halves = t.reshape(2, loc, dim)
-            mine, other = pick(halves, core), swap(pick(halves, 1 - core))
-            return jnp.where(first, jnp.stack([mine, other]), jnp.stack([other, mine]))
-
-        def my_cols(w):
-            return lax.dynamic_slice_in_dim(w, chip * cols, cols, axis=1)
-
-        def inv_of(raw):
-            return lax.rsqrt(jnp.mean(raw * raw, axis=-1, keepdims=True) + NORM_EPS)
-
-        x_f = to_core(x_loc).astype(F32)
-        gy = to_core(gy_loc)
-        pos = to_core(positions)
-        x_inv = inv_of(x_f)
-        x_hat = x_f * x_inv
-        hidden = (x_hat * g_norm.astype(F32)).astype(BF)
-        pos_f = jnp.broadcast_to(pos.astype(F32)[None], (8, rows))
-        gains = jnp.stack([g_query, g_key]).astype(F32)
+        pos = jnp.broadcast_to(positions.astype(F32)[:, None, :], (2, 8, loc))
+        gains = jnp.stack([g_query, g_key, g_norm]).astype(F32)
         gains_h = lax.dynamic_slice_in_dim(gains, chip * cols, cols, axis=1)
-        w_cat = jnp.concatenate([my_cols(w_query), my_cols(w_key), my_cols(w_value)], 1)
-        w_rows = lax.dynamic_slice_in_dim(w_out, chip * cols, cols, axis=0)
-        hid_all, q, k, v, qh_hat, kh_hat, att_t, lse, att_tok, d_att, dwo, cos_a, sin_a, inv_all, q_raw, k_raw = front(
-            hidden, gy, w_query, w_key, pos_f, w_cat, w_rows, gains_h, rope_rows(), n_chip)
-        dwq, dwk, dwv, dwo, d_hid, dg = back(
+        hid_all, q, k, v, qh_hat, kh_hat, att_t, lse, att_tok, d_att, dwo, cos_a, sin_a, inv_all, q_raw, k_raw, x_sw, gy_sw = front(
+            x_loc, gy_loc, w_query, w_key, w_value, w_out, pos, gains_h, gains, rope_rows(), n_chip)
+        dwq, dwk, dwv, y, grad_x, dwo, dg, dgn = back(
             q, k, v, d_att, att_t, lse, gains_h, gains, inv_all, hid_all.reshape(n_chip * rows, dim), qh_hat, kh_hat, cos_a, sin_a,
-            q_raw, k_raw, w_query, w_key, w_value, dwo.reshape(2, loc, dim))
-        y = (x_f + mm32(att_tok, w_out)).astype(BF)
-        dg = jnp.moveaxis(dg[:2].reshape(2, 2, loc), 1, 0)
-        dg = pick(dg, core) + swap(pick(dg, 1 - core))
-
-        d_nrm = d_hid * g_norm.astype(F32)
-        dxn = x_inv * (d_nrm - x_hat * jnp.mean(d_nrm * x_hat, axis=-1, keepdims=True))
-        grad_x = (gy.astype(F32) + dxn).astype(BF)
-        dgn = jnp.sum(d_hid * x_hat, axis=0).reshape(n_sp, loc)
-        dgn = jnp.sum(lax.all_to_all(dgn, 'sp', split_axis=0, concat_axis=0), axis=0)
-        return from_core(y), from_core(grad_x), dgn, dwq, dwk, dwv, dwo, dg[0], dg[1]
+            q_raw, k_raw, w_query, w_key, w_value, dwo.reshape(2, loc, dim), w_out, att_tok, x_sw.reshape(rows, dim), gy_sw)
+        return y, grad_x, dgn[0], dwq, dwk, dwv, dwo, dg[0], dg[1]
 
     seq_spec = P('dp', 'sp', None)
     mat_rep = P(None, None)

time: 435 us -> 398 us (0.915)
  starting transfers between devices: 24.3 us -> 0 us
  Pallas kernels: 364 us -> 381 us
  other arithmetic: 15.4 us -> 2.03 us
  matrix products: 6.66 us -> 0 us
  waiting for transfers between devices: 5.8 us -> 0 us
    all_to_all x1 -> x0, starting transfers between devices: 22.6 us -> none  [device_step(): lax.all_to_all(dgn, 'sp', split_axis=0, concat_axis=0)]
    pallas_call x1, Pallas kernels: 160 us -> 175 us  [back(): pl.pallas_call(back_kernel, name='back', in_specs=[VM] * 9 + [any_spec] *...]
    dot_general x1 -> x0, matrix products: 6.66 us -> none  [mm32(): return jnp.dot(a, b, preferred_element_type=F32)]
    dynamic_slice x5 -> x0, local copies, waits for them, and re-layouts: 6.49 us -> none  [the longest x2 2.99 us: my_cols(): return lax.dynamic_slice_in_dim(w, chip * cols, cols, axis=1)]
    all_to_all x1 -> x0, waiting for transfers between devices: 5.79 us -> none  [device_step(): lax.all_to_all(dgn, 'sp', split_axis=0, concat_axis=0)]
    select_n x3 -> x0, other arithmetic: 4.79 us -> none  [the longest x2 3.55 us: from_core(): return jnp.where(first, jnp.stack([mine, other]), jnp.stack([other, mine]))]
    reduce_sum x3 -> x0, other arithmetic: 4.61 us -> none  [the longest x1 3.72 us: device_step(): dgn = jnp.sum(d_hid * x_hat, axis=0).reshape(n_sp, loc)]
  transfers between devices with their start and end apart: 7 -> 0, of which waited for: 1 -> 0; matrix products, arithmetic and copies ran while one was open for 5% -> 0% of each run, Pallas kernels for 37% -> 0%
where the time goes in v4:
time: 398 us; the launch traced here: 397 us
  Pallas kernels  381 us (96%)
  local copies, waits for them, and re-layouts  12.4 us (3%)
    pallas_call x1, Pallas kernels, front(): pl.pallas_call(front_kernel, name='front', out_shape=tuple((jax.ShapeDtyp...  207 us
    pallas_call x1, Pallas kernels, back(): pl.pallas_call(back_kernel, name='back', in_specs=[VM] * 9 + [any_spec] *...  175 us

profile of v4, /device:TPU:0, one launch (start us, length us, event | category | flops | bytes accessed | tf_op | source)
XLA Modules:
  0.0 396.5 jit_solution(11464665487975780863)
XLA Ops:
  0.7 0.1 maximum_bitcast_fusion
  0.7 1.2 pad_maximum_fusion.f_ref
  2.0 0.7 convert_element_type.6
  2.7 0.6 broadcast_in_dim.2.pos_ref
  3.3 0.7 stack.20
  4.0 0.7 stack.18
  4.6 0.7 stack.19
  5.4 0.0 copy-start.5
  5.4 0.6 copy-done.5
  6.0 0.6 constant_dynamic-slice_fusion.g_ref
  6.6 206.7 %front.1 = (bf16[8,256,2048]{2,1,0:T(8,128)(2,1)}, bf16[2048,256]{1,0:T(8,128)(2,1)}, bf16[2048,256]{1,0:T(8,128)(2,1)}, bf16[2048,256]{1,0:T(8,128)(2,1)}, f32[...) custom-call(bf16[2,128,2048]{2,1,0:T(8,128)(2,1)} %x_ref.1, ...), custom_call_target="tpu_custom_call" | custom-call | flops 429496729600 | bytes 167772160 | tf_op jit(solution)/shard_map/front/pallas_call | solution.py:715
  213.3 174.7 %back.1 = (f32[128,2048]{1,0:T(8,128)}, f32[128,2048]{1,0:T(8,128)}, f32[128,2048]{1,0:T(8,128)}, bf16[2,128,2048]{2,1,0:T(8,128)(2,1)}, bf16[2,128,2048]{2,1,0:...) custom-call(bf16[2048,256]{1,0:T(8,128)(2,1)} %get-tuple-element.35.q_ref, ...), custom_call_target="tpu_custom_call" | custom-call | flops 429496729600 | bytes 167772160 | tf_op jit(solution)/shard_map/back/pallas_call | solution.py:739
  388.0 0.0 copy-start.4
  388.0 1.3 slice_bitcast_fusion
  389.3 0.0 copy-start.3
  389.3 2.4 copy.25
  391.7 0.0 copy-done.4
  391.7 0.0 copy-start.2
  391.7 1.0 copy.26
  392.6 0.0 copy-done.3
  392.6 0.0 copy-start.1
  392.6 1.0 copy.27
  393.6 0.0 copy-done.2
  393.6 0.0 copy-start
  393.6 1.0 copy.28
  394.6 0.0 copy-done.1
  394.6 1.0 copy.29
  395.6 0.0 copy-done
  395.6 1.0 copy.30
  (2 shorter events, 0.0 us)
Async XLA Ops:
  5.4 0.6 copy-start.5
  388.0 3.7 copy-start.4
  389.3 3.4 copy-start.3
  391.7 1.9 copy-start.2
  392.6 1.9 copy-start.1
  393.6 1.9 copy-start

commit v5 on v4

--- a/solution.py
+++ b/solution.py
@@ -13,6 +13,7 @@
 LOG2E = 1.4426950408889634
 FWD_BLOCK = 512
 CHUNKS = 4
+EARLY = 3
 BWD_BLOCK = 512
 F32, BF = jnp.float32, jnp.bfloat16
 NT = (((1,), (1,)), ((), ()))
@@ -37,10 +38,19 @@
     return pltpu.roll(u, HEAD_DIM // 2, 1)
 
 
+def flip(a, b, bits=3):
+    out = 0
+    for i in range(bits):
+        x, y = (a // 2 ** i) % 2, (b // 2 ** i) % 2
+        out = out + 2 ** i * (x + y - 2 * x * y)
+    return out
+
+
 def front_kernel(x_ref, gy_ref, wq_ref, wk_ref, wv_ref, wo_ref, pos_ref, g_ref, gt_ref, f_ref,
-                 hall_ref, q_ref, k_ref, v_ref, qh_ref, kh_ref, ot_ref, lse_ref, atok_ref, datt_ref, dwo_ref, c_ref, s_ref, inv_ref, qr_ref, kr_ref, xs_ref, gys_ref,
+                 hall_ref, q_out, k_out, v_out, qh_out, kh_out, ot_out, lse_ref, att_out, datt_ref, dwo_ref, c_out, s_out, inv_ref, qr_out, kr_out, xs_out, gys_ref,
+                 q_ref, k_ref, v_ref, qh_ref, kh_ref, ot_ref, c_ref, s_ref, qr_ref, kr_ref, xs_ref, flush_sem,
                  buf, w_ref, wrow_ref, att_ref, vt_ref, pos_all, ssq, ssq_all, wbuf,
-                 w_sem, load_sem, swap_sem, out_sem, ssem, rsem, ps_sem, pr_sem, qs_sem, qr_sem, as_sem, ar_sem):
+                 w_sem, load_sem, swap_sem, out_sem, ssem, rsem, ps_sem, pr_sem, qs_sem, qr_sem):
     me = lax.axis_index('sp')
     chip, core = me // 2, lax.rem(me, 2)
     n_chip, rows, dim = hall_ref.shape
@@ -115,10 +125,8 @@
         return make
 
     def each_peer(fn):
-        for p in range(n_chip):
-            @pl.when(p != chip)
-            def _():
-                fn(p)
+        for step in range(1, n_chip):
+            fn(flip(chip, step))
 
     partner = {'sp': me + 1 - 2 * core}
     own_cols = pl.ds(pl.multiple_of(chip * cols, cols), cols)
@@ -132,6 +140,14 @@
     each_peer(lambda p: pl.semaphore_signal(barrier, inc=1, device_id=dev(p), device_id_type=pl.DeviceIdType.MESH))
     pl.semaphore_signal(barrier, inc=1, device_id=partner, device_id_type=pl.DeviceIdType.MESH)
     pl.semaphore_wait(barrier, n_chip)
+
+    pending = []
+
+    def flush(*pairs):
+        for src, dst in pairs:
+            copy = pltpu.make_async_copy(src, dst, flush_sem.at[len(pending)])
+            copy.start()
+            pending.append(copy)
 
     swaps = [pltpu.make_async_remote_copy(
         src_ref=src, dst_ref=dst, send_sem=swap_sem.at[0, i], recv_sem=swap_sem.at[1, i], device_id=partner, device_id_type=pl.DeviceIdType.MESH)
@@ -222,12 +238,14 @@
         return 0
 
     lax.fori_loop(0, n_chip, finish_qk, 0)
+    flush((xs_ref, xs_out), (c_ref, c_out), (s_ref, s_out), (v_ref, v_out))
 
     blk = FWD_BLOCK
     scale = HEAD_DIM ** -0.5 * LOG2E
     causal = lax.broadcasted_iota(jnp.int32, (blk, blk), 0) <= lax.broadcasted_iota(jnp.int32, (blk, blk), 1)
 
-    def attend(j, _):
+    def attend(t, _):
+        j = flip(chip // 2, t, 2)
         qs = pl.ds(pl.multiple_of(j * blk, blk), blk)
         qb = [q_ref[qs, hs] for hs in heads]
 
@@ -257,17 +275,6 @@
             lse_ref[h:h + 1, qs] = m * scale + jnp.log2(l)
         return 0
 
-    def att_copy(p, owner):
-        return pltpu.make_async_remote_copy(
-            src_ref=att_ref.at[pl.ds(p * rows, rows)], dst_ref=atok_ref.at[:, pl.ds(pl.multiple_of(owner * cols, cols), cols)], send_sem=as_sem.at[p], recv_sem=ar_sem.at[owner],
-            device_id=dev(p), device_id_type=pl.DeviceIdType.MESH)
-
-    def send_att(lo, hi):
-        for p in range(lo, hi):
-            @pl.when(p != chip)
-            def _():
-                att_copy(p, chip).start()
-
     def use_gy(p):
         ts = pl.ds(pl.multiple_of(p * rows, rows), rows)
         gy = buf[1, p]
@@ -277,8 +284,9 @@
     n_att = n_chip * rows // blk
     lax.fori_loop(0, n_att // 2, attend, 0)
     stage(1, 0)
-    send_att(0, half)
     lax.fori_loop(n_att // 2, n_att, attend, 0)
+
+    flush((q_ref, q_out), (k_ref, k_out), (qh_ref, qh_out), (kh_ref, kh_out), (ot_ref, ot_out), (att_ref, att_out))
 
     def raw_of(w, out):
         def load(m, slot):
@@ -301,9 +309,8 @@
     raw_of(wq_ref, qr_ref)
     raw_of(wk_ref, kr_ref)
     stage(1, 1)
-    send_att(half, n_chip)
-    atok_ref[:, pl.ds(pl.multiple_of(chip * cols, cols), cols)] = att_ref[pl.ds(pl.multiple_of(chip * rows, rows), rows), :]
     dwo_ref[...] = jnp.zeros_like(dwo_ref)
+    flush((qr_ref, qr_out), (kr_ref, kr_out))
 
     def use_ring(n, _):
         dist = ((n + 1) // 2) * (2 * lax.rem(n, 2) - 1)
@@ -316,8 +323,6 @@
     last_stage(1)
     use_gy(slot_at(0, half))
 
-    each_peer(lambda p: att_copy(p, p).wait_recv())
-    each_peer(lambda p: att_copy(p, chip).wait_send())
     each_peer(lambda p: pos_copy(p, chip).wait_send())
     each_peer(lambda p: ssq_copy(p, chip).wait_send())
     for sw in swaps:
@@ -326,6 +331,8 @@
     drain(1)
     hall_copy.wait()
     gys_copy.wait()
+    for copy in pending:
+        copy.wait()
 
 
 def back_kernel(q_ref, k_ref, v_ref, do_ref, ot_ref, lse_ref, g_ref, gt_ref, inv_ref,
@@ -334,7 +341,7 @@
                 dq_ref, dk_ref, dv_ref, dka_ref, dva_ref, kt_ref, qh_ref, kh_ref, c_ref, s_ref, qr_ref, kr_ref,
                 tok, pairs, pair_in, dt_ref, hblk, wblk, dwo_in, row_ref, row_all,
                 dhid_ref, dg_ref, at_ref, x_ref, gy_ref, ys_ref, gxs_ref, dgp, dgp_in, gpart, gpair_in, gsel, gsel_in,
-                sw_sem, gs_sem, gr_sem, load_sem, h_sem, w_sem, xs_sem, xr_sem, ps_sem, pr_sem, rs_sem, rr_sem, own_sem, do_sem):
+                as_sem, ar_sem, sw_sem, gs_sem, gr_sem, load_sem, h_sem, w_sem, xs_sem, xr_sem, ps_sem, pr_sem, rs_sem, rr_sem, own_sem, do_sem):
     me = lax.axis_index('sp')
     chip, core = me // 2, lax.rem(me, 2)
     n, cols = q_ref.shape
@@ -350,12 +357,10 @@
         return {'sp': 2 * p + core}
 
     def each_peer(fn):
-        for p in range(n_chip):
-            @pl.when(p != chip)
-            def _():
-                fn(p)
-
-    sides = ((qh_hbm, qh_ref), (kh_hbm, kh_ref), (c_hbm, c_ref), (s_hbm, s_ref), (qr_hbm, qr_ref), (kr_hbm, kr_ref), (dwo_ref.at[core], dwo_out), (at_hbm, at_ref), (x_hbm, x_ref), (gy_hbm, gy_ref))
+        for step in range(1, n_chip):
+            fn(flip(chip, step))
+
+    sides = ((qh_hbm, qh_ref), (kh_hbm, kh_ref), (c_hbm, c_ref), (s_hbm, s_ref), (qr_hbm, qr_ref), (kr_hbm, kr_ref), (dwo_ref.at[core], dwo_out), (at_hbm.at[own_rows], at_ref.at[:, own_cols]), (x_hbm, x_ref), (gy_hbm, gy_ref))
     loads = [pltpu.make_async_copy(src, dst, load_sem.at[i]) for i, (src, dst) in enumerate(sides)]
     for ld in loads:
         ld.start()
@@ -366,7 +371,7 @@
     def load_o(m, slot):
         return pltpu.make_async_copy(wo_ref.at[pl.ds(pl.multiple_of(m * cols, cols), cols)], wblk.at[slot, 0], w_sem.at[slot, 0])
 
-    load_h(0, 0).start()
+    load_h(chip, 0).start()
     load_o(0, 0).start()
     barrier = pltpu.get_barrier_semaphore()
     each_peer(lambda p: pl.semaphore_signal(barrier, inc=1, device_id=dev(p), device_id_type=MESH))
@@ -376,6 +381,13 @@
     dwo_copy = pltpu.make_async_remote_copy(
         src_ref=dwo_ref.at[1 - core], dst_ref=dwo_in, send_sem=do_sem.at[0], recv_sem=do_sem.at[1], device_id=partner, device_id_type=MESH)
     dwo_copy.start()
+
+    def at_copy(p, owner):
+        src = at_hbm.at[pl.ds(pl.multiple_of(p * rows, rows), rows)]
+        dst = at_ref.at[:, pl.ds(pl.multiple_of(owner * cols, cols), cols)]
+        return pltpu.make_async_remote_copy(src_ref=src, dst_ref=dst, send_sem=as_sem.at[p], recv_sem=ar_sem.at[owner], device_id=dev(p), device_id_type=MESH)
+
+    each_peer(lambda p: at_copy(p, chip).start())
 
     def to_partner(src, dst, i):
         return pltpu.make_async_remote_copy(src_ref=src, dst_ref=dst, send_sem=sw_sem.at[0, i], recv_sem=sw_sem.at[1, i], device_id=partner, device_id_type=MESH)
@@ -450,8 +462,9 @@
     send_dq(n_blk - 1)
     for t, src in enumerate((dq_ref, dk_ref, dv_ref)):
         tok[t, :, own_cols] = src[own_rows, :]
-    for t in (1, 2):
-        each_peer(lambda p: tok_copy(t, p, chip).start())
+    each_peer(lambda p: tok_copy(1, p, chip).start())
+    for step in range(1, EARLY):
+        tok_copy(2, flip(chip, step), chip).start()
 
     def pair_copy(w, p):
         return pltpu.make_async_remote_copy(
@@ -485,16 +498,17 @@
             own_copy(w).start()
 
     def each_h(ws, tail_fn):
-        def step(p, _):
-            slot = lax.rem(p, 2)
+        def step(i, _):
+            p = flip(chip, i)
+            slot = lax.rem(i, 2)
             load_h(p, slot).wait()
 
-            @pl.when(p + 1 < n_chip)
+            @pl.when(i + 1 < n_chip)
             def _():
-                load_h(p + 1, 1 - slot).start()
+                load_h(flip(chip, i + 1), 1 - slot).start()
             for w, slot_t in ws:
                 partial(w, slot_t, hblk[slot], p)
-            tail_fn(p)
+            tail_fn(i)
             for w, _ in ws:
                 pair_copy(w, p).start()
             return 0
@@ -503,10 +517,11 @@
 
     dt_ref[0] = dv_ref[...].T
     each_h(((2, 0),), lambda p: None)
-    load_h(0, 0).start()
+    load_h(chip, 0).start()
     for ld in loads:
         ld.wait()
 
+    each_peer(lambda p: at_copy(p, p).wait_recv())
     dhid_ref[...] = x_ref[...].astype(F32)
 
     def y_step(m, _):
@@ -556,14 +571,16 @@
             tok[idx, :, hs] = (inv_t[idx] * (normed(idx, hs) - raw_ref[:, hs] * inv_t[idx] * row_cols[idx])).astype(BF)
         if idx == 0:
             each_peer(lambda p: row_copy(p, chip).start())
+            for step in range(EARLY, n_chip):
+                tok_copy(2, flip(chip, step), chip).start()
             row_all[chip] = row_ref[...]
 
     def merge_v(p, _):
         merge(2, p)
         return 0
 
-    def send_v(p, _):
-        send_dw(2, p)
+    def send_v(i, _):
+        send_dw(2, flip(chip, i))
         return 0
 
     lax.fori_loop(0, n_chip, merge_v, 0)
@@ -597,25 +614,25 @@
     for u in range(2):
         dgp[u, 0:2, :] = dg_ref[0:2, u * half:(u + 1) * half]
 
-    def lagged(p):
-        @pl.when(p > 0)
+    def lagged(i):
+        @pl.when(i > 0)
         def _():
             for w in range(2):
-                merge(w, p - 1)
-
-        @pl.when(p > 1)
+                merge(w, flip(chip, i - 1))
+
+        @pl.when(i > 1)
         def _():
             for w in range(2):
-                send_dw(w, p - 2)
+                send_dw(w, flip(chip, i - 2))
 
     each_h(((0, 0), (1, 1)), lagged)
     for w in range(2):
-        send_dw(w, n_chip - 2)
-        merge(w, n_chip - 1)
+        send_dw(w, flip(chip, n_chip - 2))
+        merge(w, flip(chip, n_chip - 1))
     dwo_copy.wait_recv()
     dwo_out[...] += dwo_in[...]
     for w in range(2):
-        send_dw(w, n_chip - 1)
+        send_dw(w, flip(chip, n_chip - 1))
     dg_swap.start()
 
     each_peer(lambda p: tok_copy(2, p, p).wait_recv())
@@ -686,6 +703,7 @@
         for p in range(n_chip):
             pair_copy(w, p).wait_send()
     each_peer(lambda p: row_copy(p, chip).wait_send())
+    each_peer(lambda p: at_copy(p, chip).wait_send())
     dwo_copy.wait_send()
 
 
@@ -710,22 +728,22 @@
     half = n_chip // 2
     dma, vmem = pltpu.SemaphoreType.DMA, pltpu.VMEM
     outs = [((n_chip, rows, dim), BF), ((n, cols), BF), ((n, cols), BF), ((n, cols), BF), ((n, cols), F32), ((n, cols), F32), ((cols, n), F32), ((heads, n), F32),
-            ((rows, dim), BF), ((n, cols), BF), ((cols, dim), F32), ((n, HEAD_DIM), F32), ((n, HEAD_DIM), F32), ((2 * n_chip, rows), F32), ((rows, dim), F32), ((rows, dim), F32),
+            ((n, cols), BF), ((n, cols), BF), ((cols, dim), F32), ((n, HEAD_DIM), F32), ((n, HEAD_DIM), F32), ((2 * n_chip, rows), F32), ((rows, dim), F32), ((rows, dim), F32),
             ((2, loc, dim), BF), ((rows, dim), BF)]
     return pl.pallas_call(
         front_kernel, name='front', out_shape=tuple(jax.ShapeDtypeStruct(s, d) for s, d in outs),
-        in_specs=[any_spec] * 6 + [VM] * 4, out_specs=(any_spec,) + (VM,) * 16 + (any_spec,),
-        scratch_shapes=[
+        in_specs=[any_spec] * 6 + [VM] * 4, out_specs=(any_spec,) * 7 + (VM,) + (any_spec,) + (VM,) * 2 + (any_spec,) * 2 + (VM,) + (any_spec,) * 4,
+        scratch_shapes=[vmem(*outs[i]) for i in (1, 2, 3, 4, 5, 6, 11, 12, 14, 15, 16)] + [dma((12,)),
             vmem((2, n_chip, rows, dim), BF), vmem((3, dim, cols), BF), vmem((cols, dim), BF), vmem((n, cols), BF), vmem((cols, n), BF),
             vmem((n_chip, 2, 8, loc), F32), vmem((2 * n_chip, rows), F32), vmem((n_chip, 2 * n_chip, rows), F32), vmem((2, dim, cols), BF),
             dma((2,)), dma((6,)), dma((2, 3)), dma((2,)), dma((2, 2, half, CHUNKS)), dma((2, 2, half, CHUNKS)),
-            dma((n_chip,)), dma((n_chip,)), dma((n_chip,)), dma((n_chip,)), dma((n_chip,)), dma((n_chip,))],
+            dma((n_chip,)), dma((n_chip,)), dma((n_chip,)), dma((n_chip,))],
         compiler_params=pltpu.CompilerParams(collective_id=0, has_side_effects=True, vmem_limit_bytes=67043328),
         cost_estimate=pl.CostEstimate(flops=400 * n * dim * cols, bytes_accessed=40 * n * dim, transcendentals=n * n * heads // 2),
     )(x, gy, w_query, w_key, w_value, w_out, pos, gains_h, gains, freq)
 
 
-def back(q, k, v, d_att, att_t, lse, gains_h, gains, inv, hid, qh, kh, cos_a, sin_a, q_raw, k_raw, w_query, w_key, w_value, dwo, w_out, att_tok, x, gy):
+def back(q, k, v, d_att, att_t, lse, gains_h, gains, inv, hid, qh, kh, cos_a, sin_a, q_raw, k_raw, w_query, w_key, w_value, dwo, w_out, att, x, gy):
     n, cols = q.shape
     rows, dim = q_raw.shape
     n_chip = n // rows
@@ -747,11 +765,11 @@
             vmem((8, rows), F32), vmem((n_chip, 8, rows), F32),
             vmem((rows, dim), F32), vmem((8, cols), F32), vmem((rows, dim), BF), vmem((rows, dim), BF), vmem((rows, dim), BF), vmem((2, rows // 2, dim), BF), vmem((2, rows // 2, dim), BF),
             vmem((2, 8, cols // 2), F32), vmem((8, cols // 2), F32), vmem((2,) + tile, F32), vmem(tile, F32), vmem(tile, F32), vmem(tile, F32),
-            dma((2, 5)), dma((n_chip,)), dma((n_chip,)), dma((10,)), dma((2,)), dma((2, 3)), dma((6, n_chip)), dma((6, n_chip)), dma((3, n_chip)), dma((3, n_chip)),
+            dma((n_chip,)), dma((n_chip,)), dma((2, 5)), dma((n_chip,)), dma((n_chip,)), dma((10,)), dma((2,)), dma((2, 3)), dma((6, n_chip)), dma((6, n_chip)), dma((3, n_chip)), dma((3, n_chip)),
             dma((n_chip,)), dma((n_chip,)), dma((3,)), dma((2,))],
         compiler_params=pltpu.CompilerParams(collective_id=1, has_side_effects=True, vmem_limit_bytes=67043328),
         cost_estimate=pl.CostEstimate(flops=400 * n * dim * cols, bytes_accessed=40 * n * dim, transcendentals=n * n),
-    )(q, k, v, d_att, att_t, lse, gains_h, gains, inv, hid, qh, kh, cos_a, sin_a, q_raw, k_raw, w_query, w_key, w_value, dwo, w_out, att_tok, x, gy)
+    )(q, k, v, d_att, att_t, lse, gains_h, gains, inv, hid, qh, kh, cos_a, sin_a, q_raw, k_raw, w_query, w_key, w_value, dwo, w_out, att, x, gy)
 
 
 def solution(mesh):
@@ -765,11 +783,11 @@
         pos = jnp.broadcast_to(positions.astype(F32)[:, None, :], (2, 8, loc))
         gains = jnp.stack([g_query, g_key, g_norm]).astype(F32)
         gains_h = lax.dynamic_slice_in_dim(gains, chip * cols, cols, axis=1)
-        hid_all, q, k, v, qh_hat, kh_hat, att_t, lse, att_tok, d_att, dwo, cos_a, sin_a, inv_all, q_raw, k_raw, x_sw, gy_sw = front(
+        hid_all, q, k, v, qh_hat, kh_hat, att_t, lse, att, d_att, dwo, cos_a, sin_a, inv_all, q_raw, k_raw, x_sw, gy_sw = front(
             x_loc, gy_loc, w_query, w_key, w_value, w_out, pos, gains_h, gains, rope_rows(), n_chip)
         dwq, dwk, dwv, y, grad_x, dwo, dg, dgn = back(
             q, k, v, d_att, att_t, lse, gains_h, gains, inv_all, hid_all.reshape(n_chip * rows, dim), qh_hat, kh_hat, cos_a, sin_a,
-            q_raw, k_raw, w_query, w_key, w_value, dwo.reshape(2, loc, dim), w_out, att_tok, x_sw.reshape(rows, dim), gy_sw)
+            q_raw, k_raw, w_query, w_key, w_value, dwo.reshape(2, loc, dim), w_out, att, x_sw.reshape(rows, dim), gy_sw)
         return y, grad_x, dgn[0], dwq, dwk, dwv, dwo, dg[0], dg[1]
 
     seq_spec = P('dp', 'sp', None)

time: 398 us -> 380 us (0.955)
  Pallas kernels: 381 us -> 363 us
    pallas_call x1, Pallas kernels: 207 us -> 192 us  [front(): pl.pallas_call(front_kernel, name='front', out_shape=tuple((jax.ShapeDtyp...]
where the time goes in v5:
time: 380 us; the launch traced here: 379 us
  Pallas kernels  363 us (96%)
  local copies, waits for them, and re-layouts  12.4 us (3%)
    pallas_call x1, Pallas kernels, front(): pl.pallas_call(front_kernel, name='front', out_shape=tuple((jax.ShapeDtyp...  192 us
    pallas_call x1, Pallas kernels, back(): pl.pallas_call(back_kernel, name='back', in_specs=[VM] * 9 + [any_spec] *...  172 us
    unnamed x18, local copies, waits for them, and re-layouts  7.87 us

profile of v5, /device:TPU:0, one launch (start us, length us, event | category | flops | bytes accessed | tf_op | source)
XLA Modules:
  0.0 378.6 jit_solution(7734766304027641885)
XLA Ops:
  0.7 0.1 maximum_bitcast_fusion
  0.7 1.2 pad_maximum_fusion.f_ref
  2.0 0.7 convert_element_type.6
  2.7 0.6 broadcast_in_dim.2.pos_ref
  3.3 0.7 stack.20
  4.0 0.7 stack.18
  4.6 0.7 stack.19
  5.4 0.0 copy-start.5
  5.4 0.6 copy-done.5
  6.0 0.6 constant_dynamic-slice_fusion.g_ref
  6.6 191.9 %front.1 = (bf16[8,256,2048]{2,1,0:T(8,128)(2,1)}, bf16[2048,256]{1,0:T(8,128)(2,1)}, bf16[2048,256]{1,0:T(8,128)(2,1)}, bf16[2048,256]{1,0:T(8,128)(2,1)}, f32[...) custom-call(bf16[2,128,2048]{2,1,0:T(8,128)(2,1)} %x_ref.1, ...), custom_call_target="tpu_custom_call" | custom-call | flops 429496729600 | bytes 167772160 | tf_op jit(solution)/shard_map/front/pallas_call | solution.py:733
  198.5 171.5 %back.1 = (f32[128,2048]{1,0:T(8,128)}, f32[128,2048]{1,0:T(8,128)}, f32[128,2048]{1,0:T(8,128)}, bf16[2,128,2048]{2,1,0:T(8,128)(2,1)}, bf16[2,128,2048]{2,1,0:...) custom-call(bf16[2048,256]{1,0:T(8,128)(2,1)} %get-tuple-element.35.q_ref, ...), custom_call_target="tpu_custom_call" | custom-call | flops 429496729600 | bytes 167772160 | tf_op jit(solution)/shard_map/back/pallas_call | solution.py:757
  370.0 0.0 copy-start.4
  370.0 1.3 slice_bitcast_fusion
  371.3 0.0 copy-start.3
  371.3 2.4 copy.25
  373.7 0.0 copy-done.4
  373.7 0.0 copy-start.2
  373.7 1.0 copy.26
  374.7 0.0 copy-done.3
  374.7 0.0 copy-start.1
  374.7 1.0 copy.27
  375.7 0.0 copy-done.2
  375.7 0.0 copy-start
  375.7 1.0 copy.28
  376.6 0.0 copy-done.1
  376.6 1.0 copy.29
  377.6 0.0 copy-done
  377.6 1.0 copy.30
  (2 shorter events, 0.0 us)
Async XLA Ops:
  5.4 0.6 copy-start.5
  370.0 3.7 copy-start.4
  371.3 3.4 copy-start.3
  373.7 1.9 copy-start.2
  374.7 1.9 copy-start.1
  375.7 1.9 copy-start

commit v6 on v5

--- a/solution.py
+++ b/solution.py
@@ -1,5 +1,5 @@
-import functools
 import jax
+import numpy as np
 import jax.numpy as jnp
 from jax import lax
 from jax.experimental import pallas as pl
@@ -21,9 +21,15 @@
 
 def rope_rows():
     half = HEAD_DIM // 2
-    inv_freq = ROPE_BASE ** (-jnp.arange(half, dtype=F32) * (2.0 / HEAD_DIM))
-    sign = jnp.concatenate([-jnp.ones(half, F32), jnp.ones(half, F32)])
-    return jnp.stack([jnp.concatenate([inv_freq, inv_freq]), sign])
+    inv_freq = ROPE_BASE ** (-np.arange(half) * (2.0 / HEAD_DIM))
+    sign = np.ones(half)
+    return jnp.asarray(np.stack([np.concatenate([inv_freq, inv_freq]), np.concatenate([-sign, sign])]).astype(np.float32))
+
+
+def fill_gains(ins, gt_ref, g_ref, own_cols):
+    for i, ref in enumerate(ins):
+        gt_ref[i:i + 1, :] = ref[...].astype(F32).reshape(1, -1)
+    g_ref[...] = gt_ref[0:2, own_cols]
 
 
 def column(row):
@@ -46,10 +52,10 @@
     return out
 
 
-def front_kernel(x_ref, gy_ref, wq_ref, wk_ref, wv_ref, wo_ref, pos_ref, g_ref, gt_ref, f_ref,
+def front_kernel(x_ref, gy_ref, wq_ref, wk_ref, wv_ref, wo_ref, pos_in, gq_in, gk_in, gn_in, f_ref,
                  hall_ref, q_out, k_out, v_out, qh_out, kh_out, ot_out, lse_ref, att_out, datt_ref, dwo_ref, c_out, s_out, inv_ref, qr_out, kr_out, xs_out, gys_ref,
                  q_ref, k_ref, v_ref, qh_ref, kh_ref, ot_ref, c_ref, s_ref, qr_ref, kr_ref, xs_ref, flush_sem,
-                 buf, w_ref, wrow_ref, att_ref, vt_ref, pos_all, ssq, ssq_all, wbuf,
+                 pos_ref, g_ref, gt_ref, buf, w_ref, wrow_ref, att_ref, vt_ref, pos_all, ssq, ssq_all, wbuf,
                  w_sem, load_sem, swap_sem, out_sem, ssem, rsem, ps_sem, pr_sem, qs_sem, qr_sem):
     me = lax.axis_index('sp')
     chip, core = me // 2, lax.rem(me, 2)
@@ -136,6 +142,9 @@
     loads = [pltpu.make_async_copy(src, dst, load_sem.at[i]) for i, (src, dst) in enumerate(local)]
     for ld in loads:
         ld.start()
+    fill_gains((gq_in, gk_in, gn_in), gt_ref, g_ref, own_cols)
+    for u in range(2):
+        pos_ref[u] = jnp.broadcast_to(pos_in[u:u + 1, :].astype(F32), pos_ref.shape[1:])
     barrier = pltpu.get_barrier_semaphore()
     each_peer(lambda p: pl.semaphore_signal(barrier, inc=1, device_id=dev(p), device_id_type=pl.DeviceIdType.MESH))
     pl.semaphore_signal(barrier, inc=1, device_id=partner, device_id_type=pl.DeviceIdType.MESH)
@@ -335,12 +344,12 @@
         copy.wait()
 
 
-def back_kernel(q_ref, k_ref, v_ref, do_ref, ot_ref, lse_ref, g_ref, gt_ref, inv_ref,
+def back_kernel(q_ref, k_ref, v_ref, do_ref, ot_ref, lse_ref, gq_in, gk_in, gn_in, inv_ref,
                 hall_ref, qh_hbm, kh_hbm, c_hbm, s_hbm, qr_hbm, kr_hbm, wq_ref, wk_ref, wv_ref, dwo_ref, wo_ref, at_hbm, x_hbm, gy_hbm,
                 dwq_ref, dwk_ref, dwv_ref, y_ref, gx_ref, dwo_out, dg_out, dgn_out,
                 dq_ref, dk_ref, dv_ref, dka_ref, dva_ref, kt_ref, qh_ref, kh_ref, c_ref, s_ref, qr_ref, kr_ref,
                 tok, pairs, pair_in, dt_ref, hblk, wblk, dwo_in, row_ref, row_all,
-                dhid_ref, dg_ref, at_ref, x_ref, gy_ref, ys_ref, gxs_ref, dgp, dgp_in, gpart, gpair_in, gsel, gsel_in,
+                g_ref, gt_ref, dhid_ref, dg_ref, at_ref, x_ref, gy_ref, ys_ref, gxs_ref, dgp, dgp_in, gpart, gpair_in, gsel, gsel_in,
                 as_sem, ar_sem, sw_sem, gs_sem, gr_sem, load_sem, h_sem, w_sem, xs_sem, xr_sem, ps_sem, pr_sem, rs_sem, rr_sem, own_sem, do_sem):
     me = lax.axis_index('sp')
     chip, core = me // 2, lax.rem(me, 2)
@@ -373,6 +382,7 @@
 
     load_h(chip, 0).start()
     load_o(0, 0).start()
+    fill_gains((gq_in, gk_in, gn_in), gt_ref, g_ref, own_cols)
     barrier = pltpu.get_barrier_semaphore()
     each_peer(lambda p: pl.semaphore_signal(barrier, inc=1, device_id=dev(p), device_id_type=MESH))
     pl.semaphore_signal(barrier, inc=1, device_id=partner, device_id_type=MESH)
@@ -718,10 +728,10 @@
     return lax.dot_general(a, b, NT, preferred_element_type=F32)
 
 
-def front(x, gy, w_query, w_key, w_value, w_out, pos, gains_h, gains, freq, n_chip):
+def front(x, gy, w_query, w_key, w_value, w_out, pos, gains, freq, n_chip):
     loc, dim = x.shape[1:]
     rows = 2 * loc
-    cols = gains_h.shape[1]
+    cols = dim // n_chip
     n = n_chip * rows
     heads = cols // HEAD_DIM
     any_spec = pl.BlockSpec(memory_space=pl.ANY)
@@ -732,18 +742,18 @@
             ((2, loc, dim), BF), ((rows, dim), BF)]
     return pl.pallas_call(
         front_kernel, name='front', out_shape=tuple(jax.ShapeDtypeStruct(s, d) for s, d in outs),
-        in_specs=[any_spec] * 6 + [VM] * 4, out_specs=(any_spec,) * 7 + (VM,) + (any_spec,) + (VM,) * 2 + (any_spec,) * 2 + (VM,) + (any_spec,) * 4,
+        in_specs=[any_spec] * 6 + [VM] * 5, out_specs=(any_spec,) * 7 + (VM,) + (any_spec,) + (VM,) * 2 + (any_spec,) * 2 + (VM,) + (any_spec,) * 4,
         scratch_shapes=[vmem(*outs[i]) for i in (1, 2, 3, 4, 5, 6, 11, 12, 14, 15, 16)] + [dma((12,)),
-            vmem((2, n_chip, rows, dim), BF), vmem((3, dim, cols), BF), vmem((cols, dim), BF), vmem((n, cols), BF), vmem((cols, n), BF),
+            vmem((2, 8, loc), F32), vmem((2, cols), F32), vmem((3, dim), F32), vmem((2, n_chip, rows, dim), BF), vmem((3, dim, cols), BF), vmem((cols, dim), BF), vmem((n, cols), BF), vmem((cols, n), BF),
             vmem((n_chip, 2, 8, loc), F32), vmem((2 * n_chip, rows), F32), vmem((n_chip, 2 * n_chip, rows), F32), vmem((2, dim, cols), BF),
             dma((2,)), dma((6,)), dma((2, 3)), dma((2,)), dma((2, 2, half, CHUNKS)), dma((2, 2, half, CHUNKS)),
             dma((n_chip,)), dma((n_chip,)), dma((n_chip,)), dma((n_chip,))],
         compiler_params=pltpu.CompilerParams(collective_id=0, has_side_effects=True, vmem_limit_bytes=67043328),
         cost_estimate=pl.CostEstimate(flops=400 * n * dim * cols, bytes_accessed=40 * n * dim, transcendentals=n * n * heads // 2),
-    )(x, gy, w_query, w_key, w_value, w_out, pos, gains_h, gains, freq)
-
-
-def back(q, k, v, d_att, att_t, lse, gains_h, gains, inv, hid, qh, kh, cos_a, sin_a, q_raw, k_raw, w_query, w_key, w_value, dwo, w_out, att, x, gy):
+    )(x, gy, w_query, w_key, w_value, w_out, pos, *gains, freq)
+
+
+def back(q, k, v, d_att, att_t, lse, gains, inv, hid, qh, kh, cos_a, sin_a, q_raw, k_raw, w_query, w_key, w_value, dwo, w_out, att, x, gy):
     n, cols = q.shape
     rows, dim = q_raw.shape
     n_chip = n // rows
@@ -755,7 +765,7 @@
     tile = (n_chip, 8, cols // 2)
     vmem = pltpu.VMEM
     return pl.pallas_call(
-        back_kernel, name='back', in_specs=[VM] * 9 + [any_spec] * 15, out_specs=(any_spec,) * 5 + (VM,) * 3,
+        back_kernel, name='back', in_specs=[VM] * 10 + [any_spec] * 15, out_specs=(any_spec,) * 5 + (VM,) * 3,
         out_shape=(grad,) * 3 + (seq, seq, grad, small, small),
         scratch_shapes=[
             vmem((n, cols), BF), vmem((n, cols), BF), vmem((n, cols), BF), vmem((n, cols), F32), vmem((n, cols), F32), vmem((cols, n), BF),
@@ -763,31 +773,42 @@
             vmem((3, rows, dim), BF), vmem((3, n_chip, 2, rows // 2, cols), F32), vmem((3, n_chip, rows // 2, cols), F32),
             vmem((2, cols, n), BF), vmem((2, n, cols), BF), vmem((2, 3, cols, dim), BF), vmem((rows // 2, dim), F32),
             vmem((8, rows), F32), vmem((n_chip, 8, rows), F32),
-            vmem((rows, dim), F32), vmem((8, cols), F32), vmem((rows, dim), BF), vmem((rows, dim), BF), vmem((rows, dim), BF), vmem((2, rows // 2, dim), BF), vmem((2, rows // 2, dim), BF),
+            vmem((2, cols), F32), vmem((3, dim), F32), vmem((rows, dim), F32), vmem((8, cols), F32), vmem((rows, dim), BF), vmem((rows, dim), BF), vmem((rows, dim), BF), vmem((2, rows // 2, dim), BF), vmem((2, rows // 2, dim), BF),
             vmem((2, 8, cols // 2), F32), vmem((8, cols // 2), F32), vmem((2,) + tile, F32), vmem(tile, F32), vmem(tile, F32), vmem(tile, F32),
             dma((n_chip,)), dma((n_chip,)), dma((2, 5)), dma((n_chip,)), dma((n_chip,)), dma((10,)), dma((2,)), dma((2, 3)), dma((6, n_chip)), dma((6, n_chip)), dma((3, n_chip)), dma((3, n_chip)),
             dma((n_chip,)), dma((n_chip,)), dma((3,)), dma((2,))],
         compiler_params=pltpu.CompilerParams(collective_id=1, has_side_effects=True, vmem_limit_bytes=67043328),
         cost_estimate=pl.CostEstimate(flops=400 * n * dim * cols, bytes_accessed=40 * n * dim, transcendentals=n * n),
-    )(q, k, v, d_att, att_t, lse, gains_h, gains, inv, hid, qh, kh, cos_a, sin_a, q_raw, k_raw, w_query, w_key, w_value, dwo, w_out, att, x, gy)
+    )(q, k, v, d_att, att_t, lse, *gains, inv, hid, qh, kh, cos_a, sin_a, q_raw, k_raw, w_query, w_key, w_value, dwo, w_out, att, x, gy)
+
+
+def copy_kernel(*refs):
+    n = len(refs) // 2
+    for src, dst in zip(refs[:n], refs[n:]):
+        dst[...] = src[...]
+
+
+def hand_out(arrays, steps=4):
+    specs = []
+    for a in arrays:
+        block = a.shape[:-2] + (a.shape[-2] // steps, a.shape[-1])
+        specs.append(pl.BlockSpec(block, (lambda p: (0, p, 0)) if a.ndim == 3 else (lambda p: (p, 0))))
+    return pl.pallas_call(copy_kernel, grid=(steps,), name='hand_out', in_specs=specs, out_specs=specs, out_shape=[jax.ShapeDtypeStruct(a.shape, a.dtype) for a in arrays])(*arrays)
 
 
 def solution(mesh):
     n_chip = mesh.shape['sp'] // 2
 
     def device_step(x_loc, gy_loc, positions, g_norm, w_query, w_key, w_value, w_out, g_query, g_key):
-        chip = lax.axis_index('sp') // 2
         loc, dim = x_loc.shape[1], x_loc.shape[2]
         rows = 2 * loc
-        cols = dim // n_chip
-        pos = jnp.broadcast_to(positions.astype(F32)[:, None, :], (2, 8, loc))
-        gains = jnp.stack([g_query, g_key, g_norm]).astype(F32)
-        gains_h = lax.dynamic_slice_in_dim(gains, chip * cols, cols, axis=1)
+        gains = (g_query, g_key, g_norm)
         hid_all, q, k, v, qh_hat, kh_hat, att_t, lse, att, d_att, dwo, cos_a, sin_a, inv_all, q_raw, k_raw, x_sw, gy_sw = front(
-            x_loc, gy_loc, w_query, w_key, w_value, w_out, pos, gains_h, gains, rope_rows(), n_chip)
+            x_loc, gy_loc, w_query, w_key, w_value, w_out, positions, gains, rope_rows(), n_chip)
         dwq, dwk, dwv, y, grad_x, dwo, dg, dgn = back(
-            q, k, v, d_att, att_t, lse, gains_h, gains, inv_all, hid_all.reshape(n_chip * rows, dim), qh_hat, kh_hat, cos_a, sin_a,
+            q, k, v, d_att, att_t, lse, gains, inv_all, hid_all.reshape(n_chip * rows, dim), qh_hat, kh_hat, cos_a, sin_a,
             q_raw, k_raw, w_query, w_key, w_value, dwo.reshape(2, loc, dim), w_out, att, x_sw.reshape(rows, dim), gy_sw)
+        y, grad_x, dwq, dwk, dwv, dwo = hand_out((y, grad_x, dwq, dwk, dwv, dwo))
         return y, grad_x, dgn[0], dwq, dwk, dwv, dwo, dg[0], dg[1]
 
     seq_spec = P('dp', 'sp', None)

time: 380 us -> 373 us (0.982)
  local copies, waits for them, and re-layouts: 12.4 us -> 1.28 us
  Pallas kernels: 363 us -> 370 us
    unnamed x18 -> x0, local copies, waits for them, and re-layouts: 7.87 us -> none
    pallas_call x1 -> x2, Pallas kernels: 172 us -> 177 us  [the longest x1 172 us: back(): pl.pallas_call(back_kernel, name='back', in_specs=[VM] * 10 + [any_spec]...]
where the time goes in v6:
time: 373 us; the launch traced here: 372 us
  Pallas kernels  370 us (99%)
    pallas_call x1, Pallas kernels, front(): pl.pallas_call(front_kernel, name='front', out_shape=tuple((jax.ShapeDtyp...  192 us
    pallas_call x1, Pallas kernels, back(): pl.pallas_call(back_kernel, name='back', in_specs=[VM] * 10 + [any_spec]...  172 us

profile of v6, /device:TPU:0, one launch (start us, length us, event | category | flops | bytes accessed | tf_op | source)
XLA Modules:
  0.0 371.5 jit_solution(11207389370366251058)
XLA Ops:
  0.6 192.1 %front.1 = (bf16[8,256,2048]{2,1,0:T(8,128)(2,1)}, bf16[2048,256]{1,0:T(8,128)(2,1)}, bf16[2048,256]{1,0:T(8,128)(2,1)}, bf16[2048,256]{1,0:T(8,128)(2,1)}, f32[...) custom-call(bf16[2,128,2048]{2,1,0:T(8,128)(2,1)} %x_ref.1, ...), custom_call_target="tpu_custom_call" | custom-call | flops 429496729600 | bytes 167772160 | tf_op jit(solution)/shard_map/front/pallas_call | solution.py:743
  192.7 171.7 %back.1 = (f32[128,2048]{1,0:T(8,128)}, f32[128,2048]{1,0:T(8,128)}, f32[128,2048]{1,0:T(8,128)}, bf16[2,128,2048]{2,1,0:T(8,128)(2,1)}, bf16[2,128,2048]{2,1,0:...) custom-call(bf16[2048,256]{1,0:T(8,128)(2,1)} %get-tuple-element.41.q_ref, ...), custom_call_target="tpu_custom_call" | custom-call | flops 429496729600 | bytes 167772160 | tf_op jit(solution)/shard_map/back/pallas_call | solution.py:767
  364.4 5.8 %hand_out.1 = (bf16[2,128,2048]{2,1,0:T(8,128)(2,1)}, bf16[2,128,2048]{2,1,0:T(8,128)(2,1)}, f32[128,2048]{1,0:T(8,128)}, f32[128,2048]{1,0:T(8,128)}, f32[128,2048]{1,0:T(8,128)}, /*index=5*/f32[128,2048]{1,0:T(8,128)}) custom-call(bf16[2,128,2048]{2,1,0:T(8,128)(2,1)} %get-tuple-element.59.refs_0_, bf16[2,128,2048]{2,1,0:T(8,128)(2,1)} %get-tuple-element.60.refs_1_, ...), custom_call_target="tpu_custom_call" | custom-call | tf_op jit(solution)/shard_map/hand_out/pallas_call | solution.py:796
  370.2 1.3 slice_bitcast_fusion
